TPU v7x, 512 devices: a whole 4x4x16 slice. The times are simulated.
512 devices in a mesh: ep: 128 (over x, z, core), dp: 4 (over y).
Axes of the slice: x: 4, y: 4, z: 16, core: 2. Of those that a mesh axis runs over, the one named last changes fastest.
Arguments:
- tokens: bfloat16 [2048, 3584], P('ep'), may hold values from -6 to 6
- expert_ids: int32 [2048, 8], P('ep'), may hold values from 0 to 127, all different within a row; in each aligned block of 16 rows (0 to 15, 16 to 31, ...) at most 4 rows name the same one
- route_logits: float32 [2048, 8], P('ep'), may hold values from -8 to 8
- expert_gate: bfloat16 [128, 3584, 1024], P('ep', None, 'dp'), may hold values from -0.09375 to 0.09375
- expert_up: bfloat16 [128, 3584, 1024], P('ep', None, 'dp'), may hold values from -0.09375 to 0.09375
- expert_down: bfloat16 [128, 1024, 3584], P('ep', 'dp'), may hold values from -0.1875 to 0.1875
Outputs:
- mixed: bfloat16 [2048, 3584], P(('ep', 'dp'))
Inputs may be any that keep to these rules, and one draw needn't show every extreme that they name: `expert_ids`: each row names 8 different experts of 0 to 127 and every expert is named by some row. Within the rows of one index of ep (aligned blocks of 16 rows) no expert is named more than 4 times, and some block names one expert exactly 4 times. Loads are heavy-tailed: a few experts take several times the mean.
All inputs are finite; a program needn't handle non-finite values.
Results may differ from a plain program's by a relative error of at most 0.015.
Values may be sent and summed in bfloat16 or wider, within the bound.
No kernel may reach another device: no remote copies, remote signals or barrier semaphores. Data moves between devices by JAX's collectives and lax.ppermute only.
A program may use at most 64 MiB of HBM per device.

v0:
```python
import jax
import jax.numpy as jnp
from jax import lax
from jax.sharding import PartitionSpec as P

route_scale = 2.5


def on_device(tokens, expert_ids, route_logits, expert_gate, expert_up, expert_down):
    tok_rows, width = tokens.shape
    top = expert_ids.shape[1]
    n_ep = lax.axis_size("ep")
    n_dp = lax.axis_size("dp")
    experts = n_ep
    capacity = min(tok_rows, 4 * max(1, tok_rows * top // experts))
    flat_ids = expert_ids.reshape(-1).astype(jnp.int32)
    onehot = (flat_ids[:, None] == jnp.arange(experts, dtype=jnp.int32)[None, :]).astype(jnp.int32)
    earlier = jnp.cumsum(onehot, axis=0).astype(jnp.int32) - onehot
    within = jnp.sum(earlier * onehot, axis=1).astype(jnp.int32)
    slot_index = flat_ids * capacity + within
    token_of_slot = jnp.arange(tok_rows * top, dtype=jnp.int32) // top
    source_row = (
        jnp.full((experts * capacity,), tok_rows, jnp.int32).at[slot_index].set(token_of_slot)
    )
    extended = jnp.concatenate([tokens, jnp.zeros((1, width), tokens.dtype)], axis=0)
    outgoing = extended[source_row].reshape(n_ep, capacity, width)
    arrived = lax.all_to_all(outgoing, "ep", split_axis=0, concat_axis=0, tiled=True)
    received = arrived.reshape(n_ep * capacity, width)
    gate = jnp.dot(received, expert_gate[0], preferred_element_type=jnp.float32)
    upper = jnp.dot(received, expert_up[0], preferred_element_type=jnp.float32)
    hidden = (jax.nn.silu(gate) * upper).astype(jnp.bfloat16)
    partial_value = jnp.dot(hidden, expert_down[0], preferred_element_type=jnp.float32)
    partial_value = partial_value.reshape(n_ep, capacity, width)
    scores = jax.nn.sigmoid(route_logits)
    weights = route_scale * scores / jnp.sum(scores, axis=1, keepdims=True)
    member = lax.axis_index("dp")
    quarter = capacity // n_dp
    reduced = (
        lax.psum_scatter(partial_value.astype(jnp.bfloat16), "dp", scatter_dimension=1, tiled=True)
        .astype(jnp.float32)
        .astype(jnp.bfloat16)
    )
    back = lax.all_to_all(reduced, "ep", split_axis=0, concat_axis=0, tiled=True)
    offset = within - member * quarter
    held = ((offset >= 0) & (offset < quarter)).astype(jnp.float32)
    picked = flat_ids * quarter + jnp.clip(offset, 0, quarter - 1)
    values = back.reshape(experts * quarter, width)[picked].reshape(tok_rows, top, width)
    masked = weights * held.reshape(tok_rows, top)
    contrib = jnp.sum(masked[:, :, None] * values.astype(jnp.float32), axis=1)
    routed = lax.psum_scatter(
        contrib.astype(jnp.bfloat16), "dp", scatter_dimension=0, tiled=True
    ).astype(jnp.float32)
    return routed.astype(jnp.bfloat16)


def solution(mesh):
    placed = (
        P("ep", None),
        P("ep", None),
        P("ep", None),
        P("ep", None, "dp"),
        P("ep", None, "dp"),
        P("ep", "dp", None),
    )
    return jax.shard_map(
        on_device, mesh=mesh, in_specs=placed, out_specs=P(("ep", "dp"), None), check_vma=False
    )
```

profile of v0, /device:TPU:6, one launch (start us, length us, event | category | flops | bytes accessed | tf_op | source)
XLA Modules:
  0.0 402.3 jit_solution(13666367632085230634)
XLA Ops:
  6.5 0.0 copy-start
  6.5 0.0 reduce-scatter.2.cloned.1.call-start
  6.5 0.9 copy.20
  7.4 0.1 eq.15
  7.5 0.1 reshape.87
  7.6 0.1 fusion.13
  7.7 0.2 reduce_window_sum.11
  7.9 0.2 select_reduce_fusion
  8.1 1.0 scatter_custom_fusion
  9.1 0.9 concatenate.3
  10.0 4.2 %gather_fusion = bf16[512,3584]{1,0:T(8,128)(2,1)} fusion(bf16[17,3584]{1,0:T(8,128)(2,1)S(1)} %concatenate.3, s32[1024]{0:T(1024)S(1)} %pad_clamp_fusion.1), kind=kCustom, calls=%fused_computation | custom fusion | bytes 7342080 | tf_op jit(solution)/shard_map/gather | solution.py:26
  14.2 7.0 %reshape.88 = bf16[128,4,3584]{2,1,0:T(4,128)(2,1)} reshape(bf16[512,3584]{1,0:T(8,128)(2,1)} %gather_fusion) | data formatting | bytes 7340032 | tf_op jit(solution)/shard_map/reshape | solution.py:26
  21.2 184.3 %all_to_all.10 = bf16[128,4,3584]{2,1,0:T(4,128)(2,1)} all-to-all(bf16[128,4,3584]{2,1,0:T(4,128)(2,1)} %reshape.88), channel_id=1, replica_groups=mesh['ep'=128,'dp'=4] {'ep'}, dimensions={0} | all-to-all | bytes 7340032 | tf_op jit(solution)/shard_map/all_to_all | solution.py:27
  205.5 6.7 %reshape.89 = bf16[512,3584]{1,0:T(8,128)(2,1)} reshape(bf16[128,4,3584]{2,1,0:T(4,128)(2,1)} %all_to_all.10) | data formatting | bytes 7340032 | tf_op jit(solution)/shard_map/reshape | solution.py:28
  212.2 0.0 copy-start.1
  212.2 0.0 copy-start.3
  212.2 3.9 fusion.4
  216.1 0.0 copy-done.1
  216.1 0.4 copy-done.3
  216.5 1.1 fusion.9
  217.6 0.1 dot_general.13
  217.7 0.0 copy-done
  217.7 2.9 convolution_convert_fusion
  220.6 0.0 reduce-scatter.2.cloned.1.call-update
  220.6 0.0 copy-start.2
  220.7 47.2 %reduce-scatter.2.cloned.1.call-done = bf16[128,1,3584]{2,0,1:T(8,128)(2,1)} async-done(((bf16[128,4,3584]{2,0,1:T(8,128)(2,1)}), bf16[128,1,3584]{2,0,1:T(8,128)(2,1)}) %reduce-scatter.2.cloned.1.call-update) | async-done | bytes 917520 | tf_op jit(solution)/shard_map/reduce_scatter | solution.py:39
  267.8 0.5 broadcast.120
  268.3 2.5 reduce
  270.8 1.1 reshape.121
  271.9 17.0 %all-to-all-start.1 = ((bf16[128,2,1792]{2,1,0:T(2,128)(2,1)}), bf16[128,2,1792]{2,1,0:T(2,128)(2,1)S(1)}, u32[]{:S(2)}, u32[]{:S(2)}) async-start(bf16[128,2,1792]{2,1,0:T(2,128)(2,1)} %reshape.121), calls=%async_computation.2 | async-start | bytes 1835008 | tf_op jit(solution)/shard_map/all_to_all | solution.py:43
  289.0 0.0 all-reduce.4.cloned.1.call-start
  289.0 0.1 and.14
  289.1 0.0 copy-done.2
  289.1 0.1 copy.21
  289.2 0.1 fusion.14
  289.3 0.1 divide_select_fusion
  289.4 48.0 %all-to-all-done.1 = bf16[128,2,1792]{2,1,0:T(2,128)(2,1)S(1)} async-done(((bf16[128,2,1792]{2,1,0:T(2,128)(2,1)}), bf16[128,2,1792]{2,1,0:T(2,128)(2,1)S(1)}, u32[]{:S(2)}, u32[]{:S(2)}) %all-to-all-start.1) | async-done | bytes 917536 | tf_op jit(solution)/shard_map/all_to_all | solution.py:43
  337.4 2.1 reshape.122
  339.5 1.6 copy.29
  341.1 2.1 gather_fusion.1
  343.2 2.5 fusion
  345.7 0.0 all-reduce.4.cloned.1.call-update
  345.7 1.3 dynamic-slice
  347.7 46.3 %all-reduce.4.cloned.1.call-done = bf16[16,3584]{1,0:T(8,128)(2,1)} async-done(((bf16[16,3584]{1,0:T(8,128)(2,1)}), bf16[16,3584]{1,0:T(8,128)(2,1)}) %all-reduce.4.cloned.1.call-update) | async-done | bytes 114704
  394.0 1.4 constant_dynamic-slice_fusion
  (6 shorter events, 0.0 us)
Async XLA Ops:
  6.5 211.2 %copy-start = (bf16[1,256,3584]{2,1,0:T(8,128)(2,1)S(1)}, bf16[1,256,3584]{2,1,0:T(8,128)(2,1)}, u32[]{:S(2)}) copy-start(bf16[1,256,3584]{2,1,0:T(8,128)(2,1)} %param.11) | copy-start | bytes 5505028
  6.5 261.3 %reduce-scatter.2.cloned.1.call-start = ((), (), s32[]{:S(2)}) async-start(), calls=%async_computation.3 | async-start | bytes 4587520 | tf_op jit(solution)/shard_map/reduce_scatter | solution.py:39
  212.2 3.9 copy-start.1
  212.2 4.3 %copy-start.3 = (bf16[1,3584,256]{2,1,0:T(8,128)(2,1)S(1)}, bf16[1,3584,256]{2,1,0:T(8,128)(2,1)}, u32[]{:S(2)}) copy-start(bf16[1,3584,256]{2,1,0:T(8,128)(2,1)} %param.10) | copy-start | bytes 5505028
  220.6 68.5 %copy-start.2 = (f32[16,8]{0,1:T(8,128)S(1)}, f32[16,8]{0,1:T(8,128)}, u32[]{:S(2)}) copy-start(f32[16,8]{0,1:T(8,128)} %param.8) | copy-start | bytes 1540
  271.9 65.4 %all-to-all-start.1 = ((bf16[128,2,1792]{2,1,0:T(2,128)(2,1)}), bf16[128,2,1792]{2,1,0:T(2,128)(2,1)S(1)}, u32[]{:S(2)}, u32[]{:S(2)}) async-start(bf16[128,2,1792]{2,1,0:T(2,128)(2,1)} %reshape.121), calls=%async_computation.2 | async-start | bytes 1835008 | tf_op jit(solution)/shard_map/all_to_all | solution.py:43
  289.0 105.0 %all-reduce.4.cloned.1.call-start = ((), (), s32[]{:S(2)}) async-start(), calls=%async_computation.4 | async-start | bytes 229376
Sparse Core Ops, SparseCore 0:
  220.8 46.9 reduce-scatter.1
  345.9 48.0 all-reduce.3
where the time goes:
time: 403 us; the launch traced here: 402 us
  blocking collectives  184 us (46%)
  waiting for transfers between devices  141 us (35%)
  local copies, waits for them, and re-layouts  31.7 us (8%)
  starting transfers between devices  17.1 us (4%)
  between operations  14.2 us (4%)
  matrix products  7.89 us (2%)
  other arithmetic  5.68 us (1%)
    all_to_all x1, blocking collectives, on_device(): lax.all_to_all(outgoing, 'ep', split_axis=0, concat_axis=0, tiled=True)  184 us
    all_to_all x1, waiting for transfers between devices, on_device(): lax.all_to_all(reduced, 'ep', split_axis=0, concat_axis=0, tiled=True)  48 us
    reduce_scatter x1, waiting for transfers between devices, on_device(): lax.psum_scatter(partial_value.astype(jnp.bfloat16), 'dp', scatter_dimens...  47.2 us
    unnamed x3, waiting for transfers between devices  46.4 us
    all_to_all x1, starting transfers between devices, on_device(): lax.all_to_all(reduced, 'ep', split_axis=0, concat_axis=0, tiled=True)  17 us
    unnamed x15, local copies, waits for them, and re-layouts  8.91 us
  transfers between devices with their start and end apart: 3, of which 3 were waited for; matrix products, arithmetic and copies ran while one was open for 0% of the time, Pallas kernels for 0%

commit v1 on v0

v1 whole, which is shorter than its diff:
```python
import jax
import jax.numpy as jnp
from jax import lax
from jax.experimental import pallas as pl
from jax.experimental.pallas import tpu as pltpu
from jax.sharding import Mesh, PartitionSpec as P


route_scale = 2.5
SIDE = 128
SLOTS = 4
CHIPS_X, CORES = 4, 2

f32, bf16, i32 = jnp.float32, jnp.bfloat16, jnp.int32
VMEM = pl.BlockSpec(memory_space=pltpu.VMEM)
SMEM = pl.BlockSpec(memory_space=pltpu.SMEM)


def pack_rows(tokens, expert_ids, route_logits, member, n_dp):
    rows, width = tokens.shape
    top = expert_ids.shape[1]
    part = width // n_dp

    def body(member_ref, tokens_ref, ids_ref, logits_ref, out_ref):
        start = pl.multiple_of(member_ref[0] * part, 128)
        out_ref[:, :part] = tokens_ref[:, pl.ds(start, part)]
        scores = 1.0 / (1.0 + jnp.exp(-logits_ref[...]))
        weights = route_scale * scores / jnp.sum(scores, axis=0, keepdims=True)
        high = weights.astype(bf16).astype(f32)
        side = jnp.concatenate(
            [ids_ref[...].astype(f32), high, weights - high, jnp.zeros((SIDE - 3 * top, rows), f32)], axis=0
        )
        out_ref[:, part:] = side.T.astype(bf16)

    return pl.pallas_call(
        body,
        out_shape=jax.ShapeDtypeStruct((rows, part + SIDE), bf16),
        in_specs=[SMEM, VMEM, VMEM, VMEM],
        out_specs=VMEM,
        name="pack_rows",
    )(member, tokens, expert_ids.T, route_logits.T)


def route_rows(gathered, plane, rows, top, n_x, n_z, n_c, n_dp):
    total = gathered.shape[0]
    part = gathered.shape[1] - SIDE
    experts = n_x * n_c
    held = n_z * SLOTS
    pad = max(16, experts)

    def body(plane_ref, gathered_ref, out_ref, high_ref, low_ref, pick_ref):
        side = gathered_ref[:, part:].astype(f32).T
        line = lax.broadcasted_iota(i32, (pad, 1), 0)
        name = ((line // n_c) * n_z + plane_ref[0]) * n_c + line % n_c
        name = jnp.where(line < experts, name, -1).astype(f32)
        named = jnp.zeros((pad, total), f32)
        high = jnp.zeros((pad, total), f32)
        low = jnp.zeros((pad, total), f32)
        for k in range(top):
            same = side[k : k + 1, :] == name
            named = named + jnp.where(same, 1.0, 0.0)
            high = high + jnp.where(same, side[top + k : top + k + 1, :], 0.0)
            low = low + jnp.where(same, side[2 * top + k : 2 * top + k + 1, :], 0.0)
        one = lax.broadcasted_iota(i32, (total, total), 0)
        two = lax.broadcasted_iota(i32, (total, total), 1)
        ahead = jnp.where((one // rows == two // rows) & (one < two), 1.0, 0.0).astype(bf16)
        rank = jnp.dot(named.astype(bf16), ahead, preferred_element_type=f32)
        rank = jnp.where(named > 0.5, rank, -1.0)
        spot = lax.broadcasted_iota(i32, (held, total), 0)
        token = lax.broadcasted_iota(i32, (held, total), 1)
        wanted = jnp.where(token // rows == spot // SLOTS, spot % SLOTS, -2).astype(f32)
        for j in range(experts):
            hit = rank[j : j + 1, :] == wanted
            at = slice(j * held, (j + 1) * held)
            pick_ref[at, :] = jnp.where(hit, 1.0, 0.0).astype(bf16)
            high_ref[at, :] = jnp.where(hit, high[j : j + 1, :], 0.0).astype(bf16)
            low_ref[at, :] = jnp.where(hit, low[j : j + 1, :], 0.0).astype(bf16)
        sent = jnp.dot(pick_ref[...], gathered_ref[:, :part], preferred_element_type=f32).astype(bf16)
        for d in range(n_dp):
            out_ref[d] = sent

    slots = experts * held
    return pl.pallas_call(
        body,
        out_shape=(
            jax.ShapeDtypeStruct((n_dp, slots, part), bf16),
            jax.ShapeDtypeStruct((slots, total), bf16),
            jax.ShapeDtypeStruct((slots, total), bf16),
        ),
        in_specs=[SMEM, VMEM],
        out_specs=(VMEM, VMEM, VMEM),
        scratch_shapes=[pltpu.VMEM((slots, total), bf16)],
        name="route_rows",
    )(plane, gathered)


def hidden_rows(received, w_gate, w_up):
    n_dp, slots, part = received.shape
    units = w_gate.shape[1]

    def body(rows_ref, gate_ref, up_ref, out_ref, sum_gate, sum_up):
        step = pl.program_id(0)

        @pl.when(step == 0)
        def _():
            sum_gate[...] = jnp.zeros_like(sum_gate)
            sum_up[...] = jnp.zeros_like(sum_up)

        rows = rows_ref[0]
        sum_gate[...] += jnp.dot(rows, gate_ref[...], preferred_element_type=f32)
        sum_up[...] += jnp.dot(rows, up_ref[...], preferred_element_type=f32)

        @pl.when(step == n_dp - 1)
        def _():
            v = sum_gate[...]
            made = (v / (1.0 + jnp.exp(-v)) * sum_up[...]).astype(bf16)
            for d in range(n_dp):
                out_ref[d] = made

    return pl.pallas_call(
        body,
        grid=(n_dp,),
        out_shape=jax.ShapeDtypeStruct((n_dp, slots, units), bf16),
        in_specs=[
            pl.BlockSpec((1, slots, part), lambda i: (i, 0, 0)),
            pl.BlockSpec((part, units), lambda i: (i, 0)),
            pl.BlockSpec((part, units), lambda i: (i, 0)),
        ],
        out_specs=pl.BlockSpec((n_dp, slots, units), lambda i: (0, 0, 0)),
        scratch_shapes=[pltpu.VMEM((slots, units), f32), pltpu.VMEM((slots, units), f32)],
        name="hidden_rows",
    )(received, w_gate, w_up)


def output_rows(hidden, downs, member):
    n_dp, slots, _ = hidden.shape
    _, part = downs[0].shape

    def body(member_ref, hidden_ref, *refs):
        out_ref = refs[-1]
        total = jnp.zeros((slots, part), f32)
        for s in range(n_dp):
            source = lax.rem(member_ref[0] + (n_dp - s), n_dp)
            total = total + jnp.dot(hidden_ref[source], refs[s][...], preferred_element_type=f32)
        out_ref[...] = total.astype(bf16)

    return pl.pallas_call(
        body,
        out_shape=jax.ShapeDtypeStruct((slots, part), bf16),
        in_specs=[SMEM, VMEM] + [VMEM] * n_dp,
        out_specs=VMEM,
        name="output_rows",
    )(member, hidden, *downs)


def mix_rows(received, high, low):
    _, part = received.shape
    total = high.shape[1]

    def body(rows_ref, high_ref, low_ref, out_ref):
        rows = rows_ref[...]
        dims = (((0,), (0,)), ((), ()))
        mixed = lax.dot_general(high_ref[...], rows, dims, preferred_element_type=f32)
        mixed = mixed + lax.dot_general(low_ref[...], rows, dims, preferred_element_type=f32)
        out_ref[...] = mixed.astype(bf16)

    return pl.pallas_call(
        body,
        out_shape=jax.ShapeDtypeStruct((total, part), bf16),
        in_specs=[VMEM, VMEM, VMEM],
        out_specs=VMEM,
        name="mix_rows",
    )(received, high, low)


def sum_rows(shares):
    n_z, rows, part = shares.shape

    def body(shares_ref, out_ref):
        total = shares_ref[0].astype(f32)
        for z in range(1, n_z):
            total = total + shares_ref[z].astype(f32)
        out_ref[...] = total.astype(bf16)

    return pl.pallas_call(
        body,
        out_shape=jax.ShapeDtypeStruct((rows, part), bf16),
        in_specs=[VMEM],
        out_specs=VMEM,
        name="sum_rows",
    )(shares)


def on_device(tokens, expert_ids, route_logits, expert_gate, expert_up, expert_down):
    rows, width = tokens.shape
    top = expert_ids.shape[1]
    n_x, n_z, n_c, n_dp = (lax.axis_size(a) for a in ("x", "z", "c", "y"))
    part = width // n_dp
    held = n_z * SLOTS
    slots = n_x * n_c * held
    member = lax.axis_index("y").astype(i32)
    member_ref = member.reshape(1)
    plane_ref = lax.axis_index("z").astype(i32).reshape(1)

    downs = []
    for s in range(n_dp):
        owner = member + s
        owner = jnp.where(owner >= n_dp, owner - n_dp, owner)
        piece = lax.dynamic_slice_in_dim(expert_down[0], owner * part, part, axis=1)
        if s:
            piece = lax.ppermute(piece, "y", [(i, (i + s) % n_dp) for i in range(n_dp)])
        downs.append(piece)

    packed = pack_rows(tokens, expert_ids, route_logits, member_ref, n_dp)
    gathered = lax.all_gather(packed, "z", axis=0, tiled=True)
    outgoing, high, low = route_rows(gathered, plane_ref, rows, top, n_x, n_z, n_c, n_dp)
    outgoing = outgoing.reshape(n_dp * n_x * n_c, held, part)
    arrived = lax.all_to_all(outgoing, ("y", "x", "c"), split_axis=0, concat_axis=0, tiled=True)
    hidden = hidden_rows(arrived.reshape(n_dp, slots, part), expert_gate[0], expert_up[0])
    hidden = lax.all_to_all(hidden, "y", split_axis=0, concat_axis=0, tiled=True)
    results = output_rows(hidden, downs, member_ref)
    results = results.reshape(n_x * n_c, held, part)
    back = lax.all_to_all(results, ("x", "c"), split_axis=0, concat_axis=0, tiled=True)
    mixed = mix_rows(back.reshape(slots, part), high, low)
    mixed = mixed.reshape(n_z, rows, part)
    shares = lax.all_to_all(mixed, "z", split_axis=0, concat_axis=0, tiled=True)
    routed = sum_rows(shares)
    return lax.all_to_all(routed, "y", split_axis=0, concat_axis=1, tiled=True)


def solution(mesh):
    n_ep, n_dp = mesh.devices.shape
    grid = mesh.devices.reshape(CHIPS_X, n_ep // (CHIPS_X * CORES), CORES, n_dp)
    fine = Mesh(grid, ("x", "z", "c", "y"))
    ep = ("x", "z", "c")
    placed = (
        P(ep, None),
        P(ep, None),
        P(ep, None),
        P(ep, None, "y"),
        P(ep, None, "y"),
        P(ep, "y", None),
    )
    return jax.shard_map(
        on_device, mesh=fine, in_specs=placed, out_specs=P(ep + ("y",), None), check_vma=False
    )
```

time: 403 us -> 215 us (0.53)
  waiting for transfers between devices: 141 us -> 23.3 us
  blocking collectives: 184 us -> 151 us
  local copies, waits for them, and re-layouts: 31.7 us -> 3.57 us
  Pallas kernels: 0 us -> 20 us
  between operations: 14.2 us -> 0.11 us
  matrix products: 7.89 us -> 0 us
  other arithmetic: 5.68 us -> 0 us
    all_to_all x1 -> x4, blocking collectives: 184 us -> 110 us  [the longest x1 50.7 us: on_device(): lax.all_to_all(outgoing, ('y', 'x', 'c'), split_axis=0, concat_axis=0, ti...]
    all_to_all x1, waiting for transfers between devices: 48 us -> 0.01 us  [on_device(): lax.all_to_all(hidden, 'y', split_axis=0, concat_axis=0, tiled=True)]
    reduce_scatter x1 -> x0, waiting for transfers between devices: 47.2 us -> none  [on_device(): lax.psum_scatter(partial_value.astype(jnp.bfloat16), 'dp', scatter_dimens...]
    unnamed x3 -> x0, waiting for transfers between devices: 46.4 us -> none
    all_gather x0 -> x1, blocking collectives: none -> 40.8 us  [on_device(): gathered = lax.all_gather(packed, 'z', axis=0, tiled=True)]
    ppermute x0 -> x3, waiting for transfers between devices: none -> 23.3 us  [on_device(): piece = lax.ppermute(piece, 'y', [(i, (i + s) % n_dp) for i in range(n_dp)])]
    pallas_call x0 -> x6, Pallas kernels: none -> 20 us  [the longest x1 6.35 us: hidden_rows(): pl.pallas_call(body, grid=(n_dp,), out_shape=jax.ShapeDtypeStruct((n_dp,...]
    reshape x3 -> x0, local copies, waits for them, and re-layouts: 13.8 us -> none  [the longest x1 7 us: on_device(): outgoing = extended[source_row].reshape(n_ep, capacity, width)]
  transfers between devices with their start and end apart: 3 -> 4, of which waited for: 3 -> 2; matrix products, arithmetic and copies ran while one was open for 0% -> 0% of each run, Pallas kernels for 0% -> 0%
where the time goes in v1:
time: 215 us; the launch traced here: 214 us
  blocking collectives  151 us (70%)
  waiting for transfers between devices  23.3 us (11%)
  Pallas kernels  20 us (9%)
  starting transfers between devices  15.4 us (7%)
  local copies, waits for them, and re-layouts  3.57 us (2%)
    all_to_all x1, blocking collectives, on_device(): lax.all_to_all(outgoing, ('y', 'x', 'c'), split_axis=0, concat_axis=0, ti...  50.7 us
    all_gather x1, blocking collectives, on_device(): gathered = lax.all_gather(packed, 'z', axis=0, tiled=True)  40.8 us
    all_to_all x1, blocking collectives, on_device(): shares = lax.all_to_all(mixed, 'z', split_axis=0, concat_axis=0, tiled=True)  33.5 us
    ppermute x3, waiting for transfers between devices, on_device(): piece = lax.ppermute(piece, 'y', [(i, (i + s) % n_dp) for i in range(n_dp)])  23.3 us
    all_to_all x1, blocking collectives, on_device(): lax.all_to_all(results, ('x', 'c'), split_axis=0, concat_axis=0, tiled=True)  18.4 us
    ppermute x3, starting transfers between devices, on_device(): piece = lax.ppermute(piece, 'y', [(i, (i + s) % n_dp) for i in range(n_dp)])  11.8 us
    all_to_all x1, blocking collectives, on_device(): return lax.all_to_all(routed, 'y', split_axis=0, concat_axis=1, tiled=True)  7.78 us
    pallas_call x1, Pallas kernels, hidden_rows(): pl.pallas_call(body, grid=(n_dp,), out_shape=jax.ShapeDtypeStruct((n_dp,...  6.35 us
  transfers between devices with their start and end apart: 4, of which 2 were waited for; matrix products, arithmetic and copies ran while one was open for 0% of the time, Pallas kernels for 0%

profile of v1, /device:TPU:6, one launch (start us, length us, event | category | flops | bytes accessed | tf_op | source)
XLA Modules:
  0.0 213.6 jit_solution(186357663213501383)
XLA Ops:
  0.0 1.6 pack_rows.1
  1.6 40.8 %all_gather.3.gathered_ref = bf16[256,1024]{1,0:T(8,128)(2,1)} all-gather(bf16[16,1024]{1,0:T(8,128)(2,1)} %pack_rows.1), channel_id=1, replica_groups=mesh['x'=4,'z'=16,'c'=2,'y'=4] {'z'}, dimensions={0}, use_global_device_ids=true | all-gather | bytes 557056 | tf_op jit(solution)/shard_map/all_gather | solution.py:215
  42.4 3.6 %route_rows.1 = (bf16[4,512,896]{2,1,0:T(8,128)(2,1)}, bf16[512,256]{1,0:T(8,128)(2,1)}, bf16[512,256]{1,0:T(8,128)(2,1)}) custom-call(s32[1]{0:T(128)} %bitcast.1.plane_ref, bf16[256,1024]{1,0:T(8,128)(2,1)} %all_gather.3.gathered_ref), custom_call_target="tpu_custom_call" | custom-call | tf_op jit(solution)/shard_map/route_rows/pallas_call | solution.py:83
  46.0 50.7 %all_to_all.39 = bf16[32,64,896]{2,1,0:T(8,128)(2,1)} all-to-all(bf16[32,64,896]{2,1,0:T(8,128)(2,1)} %bitcast.23), channel_id=1, replica_groups=mesh['x'=4,'z'=16,'c'=2,'y'=4] {'y','x','c'}, dimensions={0} | all-to-all | bytes 7340032 | tf_op jit(solution)/shard_map/all_to_all | solution.py:218
  96.7 6.4 %hidden_rows.1 = bf16[4,512,256]{2,1,0:T(8,128)(2,1)} custom-call(bf16[4,512,896]{2,1,0:T(8,128)(2,1)} %bitcast.22, bf16[3584,256]{1,0:T(8,128)(2,1)} %bitcast.27, bf16[3584,256]{1,0:T(8,128)(2,1)} %bitcast.28), custom_call_target="tpu_custom_call" | custom-call | tf_op jit(solution)/shard_map/hidden_rows/pallas_call | solution.py:120
  103.0 0.0 copy-start.1
  103.0 3.6 %all-to-all-start.1 = ((bf16[4,512,256]{2,1,0:T(8,128)(2,1)}), bf16[4,512,256]{2,1,0:T(8,128)(2,1)S(1)}, u32[]{:S(2)}, u32[]{:S(2)}) async-start(bf16[4,512,256]{2,1,0:T(8,128)(2,1)} %hidden_rows.1), calls=%async_computation.1 | async-start | bytes 2097152 | tf_op jit(solution)/shard_map/all_to_all | solution.py:220
  106.7 0.0 copy-done.1
  106.7 0.9 dynamic-slice_bitcast_fusion
  107.7 3.8 %collective-permute-start = (bf16[256,896]{1,0:T(8,128)(2,1)S(1)}, bf16[256,896]{1,0:T(8,128)(2,1)S(1)}, u32[]{:S(2)}, u32[]{:S(2)}) collective-permute-start(bf16[256,896]{1,0:T(8,128)(2,1)S(1)} %get-tuple-element.12), channel_id=1, source_target_pairs={{0,1},{1,2},{2,3},{3,0},{4,5},{5,6},{6,7},{7,4},{8,9},{9,10},{10,1... | collective-permute-start | bytes 1376264 | tf_op jit(solution)/shard_map/ppermute | solution.py:211
  111.5 4.6 %collective-permute-start.1 = (bf16[256,896]{1,0:T(8,128)(2,1)S(1)}, bf16[256,896]{1,0:T(8,128)(2,1)S(1)}, u32[]{:S(2)}, u32[]{:S(2)}) collective-permute-start(bf16[256,896]{1,0:T(8,128)(2,1)S(1)} %get-tuple-element.14), channel_id=1, source_target_pairs={{0,2},{1,3},{2,0},{3,1},{4,6},{5,7},{6,4},{7,5},{8,10},{9,11},{10,... | collective-permute-start | bytes 1376264 | tf_op jit(solution)/shard_map/ppermute | solution.py:211
  116.1 3.4 %collective-permute-start.2 = (bf16[256,896]{1,0:T(8,128)(2,1)S(1)}, bf16[256,896]{1,0:T(8,128)(2,1)S(1)}, u32[]{:S(2)}, u32[]{:S(2)}) collective-permute-start(bf16[256,896]{1,0:T(8,128)(2,1)S(1)} %get-tuple-element.11), channel_id=1, source_target_pairs={{0,3},{1,0},{2,1},{3,2},{4,7},{5,4},{6,5},{7,6},{8,11},{9,8},{10,9... | collective-permute-start | bytes 1376264 | tf_op jit(solution)/shard_map/ppermute | solution.py:211
  119.5 13.2 %collective-permute-done.refs_1_ = bf16[256,896]{1,0:T(8,128)(2,1)S(1)} collective-permute-done((bf16[256,896]{1,0:T(8,128)(2,1)S(1)}, bf16[256,896]{1,0:T(8,128)(2,1)S(1)}, u32[]{:S(2)}, u32[]{:S(2)}) %collective-permute-start) | collective-permute-done | bytes 458784 | tf_op jit(solution)/shard_map/ppermute | solution.py:211
  132.6 0.0 copy-start.2
  132.6 10.2 %collective-permute-done.1.refs_2_ = bf16[256,896]{1,0:T(8,128)(2,1)S(1)} collective-permute-done((bf16[256,896]{1,0:T(8,128)(2,1)S(1)}, bf16[256,896]{1,0:T(8,128)(2,1)S(1)}, u32[]{:S(2)}, u32[]{:S(2)}) %collective-permute-start.1) | collective-permute-done | bytes 458784 | tf_op jit(solution)/shard_map/ppermute | solution.py:211
  142.8 0.0 copy-start.3
  142.8 0.0 collective-permute-done.2.refs_3_
  142.8 0.0 copy-start.4
  142.8 0.0 all-to-all-done.1.hidden_ref
  142.8 0.0 copy-start
  142.8 0.0 copy-done.2
  142.8 0.7 copy-done.3
  143.6 0.2 copy-done.4
  143.7 0.4 copy-done
  144.1 4.0 %output_rows.1 = bf16[512,896]{1,0:T(8,128)(2,1)} custom-call(s32[1]{0:T(128)} %bitcast.member_ref, bf16[4,512,256]{2,1,0:T(8,128)(2,1)} %copy-done, bf16[256,896]{1,0:T(8,128)(2,1)} %get-tuple-element.13.refs_0_, bf16[256,896]{1,0:T(8,128)(2,1)} %copy-done.2, bf16[256,896]{1,0:T(8,128)(2,1)} %copy-done.3, bf16[256,896]{1,0:T(8,128)(2,1)} %copy-done.4), custom_call_target="tpu_custom_call" | custom-call | tf_op jit(solution)/shard_map/output_rows/pallas_call | solution.py:147
  148.1 18.4 %all_to_all.40 = bf16[8,64,896]{2,1,0:T(8,128)(2,1)} all-to-all(bf16[8,64,896]{2,1,0:T(8,128)(2,1)} %bitcast.25), channel_id=1, replica_groups=mesh['x'=4,'z'=16,'c'=2,'y'=4] {'x','c'}, dimensions={0} | all-to-all | bytes 1835008 | tf_op jit(solution)/shard_map/all_to_all | solution.py:223
  166.5 2.8 %mix_rows.1 = bf16[256,896]{1,0:T(8,128)(2,1)} custom-call(bf16[512,896]{1,0:T(8,128)(2,1)} %bitcast.24, bf16[512,256]{1,0:T(8,128)(2,1)} %get-tuple-element.9.high_ref, bf16[512,256]{1,0:T(8,128)(2,1)} %get-tuple-element.10.low_ref), custom_call_target="tpu_custom_call" | custom-call | tf_op jit(solution)/shard_map/mix_rows/pallas_call | solution.py:167
  169.3 33.5 %all_to_all.41.shares_ref = bf16[16,16,896]{2,1,0:T(8,128)(2,1)} all-to-all(bf16[16,16,896]{2,1,0:T(8,128)(2,1)} %bitcast.26), channel_id=1, replica_groups=mesh['x'=4,'z'=16,'c'=2,'y'=4] {'z'}, dimensions={0} | all-to-all | bytes 917504 | tf_op jit(solution)/shard_map/all_to_all | solution.py:226
  202.8 1.7 sum_rows.1
  204.5 0.8 all_to_all.30
  205.2 7.8 %all_to_all.42 = bf16[4,4,896]{2,1,0:T(4,128)(2,1)S(1)} all-to-all(bf16[4,4,896]{2,1,0:T(4,128)(2,1)S(1)} %all_to_all.30), channel_id=1, replica_groups=mesh['x'=4,'z'=16,'c'=2,'y'=4] {'y'}, dimensions={0} | all-to-all | bytes 57344 | tf_op jit(solution)/shard_map/all_to_all | solution.py:228
  213.0 0.6 copy.9
Async XLA Ops:
  103.0 3.7 %copy-start.1 = (bf16[1,256,3584]{2,1,0:T(8,128)(2,1)S(1)}, bf16[1,256,3584]{2,1,0:T(8,128)(2,1)}, u32[]{:S(2)}) copy-start(bf16[1,256,3584]{2,1,0:T(8,128)(2,1)} %param.11) | copy-start | bytes 5505028
  103.0 39.8 %all-to-all-start.1 = ((bf16[4,512,256]{2,1,0:T(8,128)(2,1)}), bf16[4,512,256]{2,1,0:T(8,128)(2,1)S(1)}, u32[]{:S(2)}, u32[]{:S(2)}) async-start(bf16[4,512,256]{2,1,0:T(8,128)(2,1)} %hidden_rows.1), calls=%async_computation.1 | async-start | bytes 2097152 | tf_op jit(solution)/shard_map/all_to_all | solution.py:220
  107.7 25.0 %collective-permute-start = (bf16[256,896]{1,0:T(8,128)(2,1)S(1)}, bf16[256,896]{1,0:T(8,128)(2,1)S(1)}, u32[]{:S(2)}, u32[]{:S(2)}) collective-permute-start(bf16[256,896]{1,0:T(8,128)(2,1)S(1)} %get-tuple-element.12), channel_id=1, source_target_pairs={{0,1},{1,2},{2,3},{3,0},{4,5},{5,6},{6,7},{7,4},{8,9},{9,10},{10,1... | collective-permute-start | bytes 1376264 | tf_op jit(solution)/shard_map/ppermute | solution.py:211
  111.5 31.3 %collective-permute-start.1 = (bf16[256,896]{1,0:T(8,128)(2,1)S(1)}, bf16[256,896]{1,0:T(8,128)(2,1)S(1)}, u32[]{:S(2)}, u32[]{:S(2)}) collective-permute-start(bf16[256,896]{1,0:T(8,128)(2,1)S(1)} %get-tuple-element.14), channel_id=1, source_target_pairs={{0,2},{1,3},{2,0},{3,1},{4,6},{5,7},{6,4},{7,5},{8,10},{9,11},{10,... | collective-permute-start | bytes 1376264 | tf_op jit(solution)/shard_map/ppermute | solution.py:211
  116.1 26.7 %collective-permute-start.2 = (bf16[256,896]{1,0:T(8,128)(2,1)S(1)}, bf16[256,896]{1,0:T(8,128)(2,1)S(1)}, u32[]{:S(2)}, u32[]{:S(2)}) collective-permute-start(bf16[256,896]{1,0:T(8,128)(2,1)S(1)} %get-tuple-element.11), channel_id=1, source_target_pairs={{0,3},{1,0},{2,1},{3,2},{4,7},{5,4},{6,5},{7,6},{8,11},{9,8},{10,9... | collective-permute-start | bytes 1376264 | tf_op jit(solution)/shard_map/ppermute | solution.py:211
  132.6 10.2 %copy-start.2 = (bf16[256,896]{1,0:T(8,128)(2,1)}, bf16[256,896]{1,0:T(8,128)(2,1)S(1)}, u32[]{:S(2)}) copy-start(bf16[256,896]{1,0:T(8,128)(2,1)S(1)} %collective-permute-done.refs_1_) | copy-start | bytes 1376260
  142.8 0.8 copy-start.3
  142.8 0.9 copy-start.4
  142.8 1.3 copy-start

commit v2 on v1

--- a/solution.py
+++ b/solution.py
@@ -12,33 +12,44 @@
 CHIPS_X, CORES = 4, 2
 
 f32, bf16, i32 = jnp.float32, jnp.bfloat16, jnp.int32
+PARAMS = pltpu.CompilerParams(vmem_limit_bytes=20 * 1024 * 1024)
 VMEM = pl.BlockSpec(memory_space=pltpu.VMEM)
 SMEM = pl.BlockSpec(memory_space=pltpu.SMEM)
 
 
-def pack_rows(tokens, expert_ids, route_logits, member, n_dp):
+def call(body, outs, ins, scratch=()):
+    many = isinstance(outs, tuple)
+    return pl.pallas_call(
+        body,
+        out_shape=tuple(jax.ShapeDtypeStruct(*o) for o in outs) if many else jax.ShapeDtypeStruct(*outs[0]),
+        in_specs=ins,
+        out_specs=(VMEM,) * len(outs) if many else VMEM,
+        scratch_shapes=list(scratch),
+        compiler_params=PARAMS,
+    )
+
+
+def pack_rows(tokens, expert_ids, route_logits, member, n_dp, n_z):
     rows, width = tokens.shape
     top = expert_ids.shape[1]
     part = width // n_dp
 
     def body(member_ref, tokens_ref, ids_ref, logits_ref, out_ref):
         start = pl.multiple_of(member_ref[0] * part, 128)
-        out_ref[:, :part] = tokens_ref[:, pl.ds(start, part)]
+        own = tokens_ref[:, pl.ds(start, part)]
         scores = 1.0 / (1.0 + jnp.exp(-logits_ref[...]))
         weights = route_scale * scores / jnp.sum(scores, axis=0, keepdims=True)
         high = weights.astype(bf16).astype(f32)
         side = jnp.concatenate(
             [ids_ref[...].astype(f32), high, weights - high, jnp.zeros((SIDE - 3 * top, rows), f32)], axis=0
         )
-        out_ref[:, part:] = side.T.astype(bf16)
-
-    return pl.pallas_call(
-        body,
-        out_shape=jax.ShapeDtypeStruct((rows, part + SIDE), bf16),
-        in_specs=[SMEM, VMEM, VMEM, VMEM],
-        out_specs=VMEM,
-        name="pack_rows",
-    )(member, tokens, expert_ids.T, route_logits.T)
+        side = side.T.astype(bf16)
+        for z in range(n_z):
+            out_ref[z, :, :part] = own
+            out_ref[z, :, part:] = side
+
+    outs = [((n_z, rows, part + SIDE), bf16)]
+    return call(body, outs, [SMEM, VMEM, VMEM, VMEM])(member, tokens, expert_ids.T, route_logits.T)
 
 
 def route_rows(gathered, plane, rows, top, n_x, n_z, n_c, n_dp):
@@ -80,18 +91,9 @@
             out_ref[d] = sent
 
     slots = experts * held
-    return pl.pallas_call(
-        body,
-        out_shape=(
-            jax.ShapeDtypeStruct((n_dp, slots, part), bf16),
-            jax.ShapeDtypeStruct((slots, total), bf16),
-            jax.ShapeDtypeStruct((slots, total), bf16),
-        ),
-        in_specs=[SMEM, VMEM],
-        out_specs=(VMEM, VMEM, VMEM),
-        scratch_shapes=[pltpu.VMEM((slots, total), bf16)],
-        name="route_rows",
-    )(plane, gathered)
+    outs = (((n_dp, slots, part), bf16),) + (((slots, total), bf16),) * 2
+    scratch = [pltpu.VMEM((slots, total), bf16)]
+    return call(body, outs, [SMEM, VMEM], scratch)(plane, gathered)
 
 
 def hidden_rows(received, w_gate, w_up):
@@ -128,13 +130,14 @@
         ],
         out_specs=pl.BlockSpec((n_dp, slots, units), lambda i: (0, 0, 0)),
         scratch_shapes=[pltpu.VMEM((slots, units), f32), pltpu.VMEM((slots, units), f32)],
+        compiler_params=PARAMS,
         name="hidden_rows",
     )(received, w_gate, w_up)
 
 
 def output_rows(hidden, downs, member):
     n_dp, slots, _ = hidden.shape
-    _, part = downs[0].shape
+    part = downs[0].shape[1]
 
     def body(member_ref, hidden_ref, *refs):
         out_ref = refs[-1]
@@ -144,13 +147,9 @@
             total = total + jnp.dot(hidden_ref[source], refs[s][...], preferred_element_type=f32)
         out_ref[...] = total.astype(bf16)
 
-    return pl.pallas_call(
-        body,
-        out_shape=jax.ShapeDtypeStruct((slots, part), bf16),
-        in_specs=[SMEM, VMEM] + [VMEM] * n_dp,
-        out_specs=VMEM,
-        name="output_rows",
-    )(member, hidden, *downs)
+    return call(body, [((slots, part), bf16)], [SMEM, VMEM] + [VMEM] * n_dp)(
+        member, hidden, *downs
+    )
 
 
 def mix_rows(received, high, low):
@@ -164,13 +163,7 @@
         mixed = mixed + lax.dot_general(low_ref[...], rows, dims, preferred_element_type=f32)
         out_ref[...] = mixed.astype(bf16)
 
-    return pl.pallas_call(
-        body,
-        out_shape=jax.ShapeDtypeStruct((total, part), bf16),
-        in_specs=[VMEM, VMEM, VMEM],
-        out_specs=VMEM,
-        name="mix_rows",
-    )(received, high, low)
+    return call(body, [((total, part), bf16)], [VMEM] * 3)(received, high, low)
 
 
 def sum_rows(shares):
@@ -182,13 +175,11 @@
             total = total + shares_ref[z].astype(f32)
         out_ref[...] = total.astype(bf16)
 
-    return pl.pallas_call(
-        body,
-        out_shape=jax.ShapeDtypeStruct((rows, part), bf16),
-        in_specs=[VMEM],
-        out_specs=VMEM,
-        name="sum_rows",
-    )(shares)
+    return call(body, [((rows, part), bf16)], [VMEM])(shares)
+
+
+def exchange(value, axes):
+    return lax.all_to_all(value, axes, split_axis=0, concat_axis=0, tiled=True)
 
 
 def on_device(tokens, expert_ids, route_logits, expert_gate, expert_up, expert_down):
@@ -198,9 +189,14 @@
     part = width // n_dp
     held = n_z * SLOTS
     slots = n_x * n_c * held
+    total = n_z * rows
     member = lax.axis_index("y").astype(i32)
     member_ref = member.reshape(1)
     plane_ref = lax.axis_index("z").astype(i32).reshape(1)
+    w_gate, w_up = expert_gate[0], expert_up[0]
+
+    packed = pack_rows(tokens, expert_ids, route_logits, member_ref, n_dp, n_z)
+    gathered = exchange(packed, "z")
 
     downs = []
     for s in range(n_dp):
@@ -211,19 +207,16 @@
             piece = lax.ppermute(piece, "y", [(i, (i + s) % n_dp) for i in range(n_dp)])
         downs.append(piece)
 
-    packed = pack_rows(tokens, expert_ids, route_logits, member_ref, n_dp)
-    gathered = lax.all_gather(packed, "z", axis=0, tiled=True)
-    outgoing, high, low = route_rows(gathered, plane_ref, rows, top, n_x, n_z, n_c, n_dp)
-    outgoing = outgoing.reshape(n_dp * n_x * n_c, held, part)
-    arrived = lax.all_to_all(outgoing, ("y", "x", "c"), split_axis=0, concat_axis=0, tiled=True)
-    hidden = hidden_rows(arrived.reshape(n_dp, slots, part), expert_gate[0], expert_up[0])
-    hidden = lax.all_to_all(hidden, "y", split_axis=0, concat_axis=0, tiled=True)
+    outgoing, high, low = route_rows(
+        gathered.reshape(total, -1), plane_ref, rows, top, n_x, n_z, n_c, n_dp
+    )
+    arrived = exchange(outgoing.reshape(n_dp * n_x * n_c, held, part), ("y", "x", "c"))
+    hidden = hidden_rows(arrived.reshape(n_dp, slots, part), w_gate, w_up)
+    hidden = exchange(hidden, "y")
     results = output_rows(hidden, downs, member_ref)
-    results = results.reshape(n_x * n_c, held, part)
-    back = lax.all_to_all(results, ("x", "c"), split_axis=0, concat_axis=0, tiled=True)
+    back = exchange(results.reshape(n_x * n_c, held, part), ("x", "c"))
     mixed = mix_rows(back.reshape(slots, part), high, low)
-    mixed = mixed.reshape(n_z, rows, part)
-    shares = lax.all_to_all(mixed, "z", split_axis=0, concat_axis=0, tiled=True)
+    shares = exchange(mixed.reshape(n_z, rows, part), "z")
     routed = sum_rows(shares)
     return lax.all_to_all(routed, "y", split_axis=0, concat_axis=1, tiled=True)
 

time: 215 us -> 204 us (0.949)
  blocking collectives: 151 us -> 108 us
  waiting for transfers between devices: 23.3 us -> 51.7 us
  starting transfers between devices: 15.4 us -> 30.5 us
  Pallas kernels: 20 us -> 7.71 us
    all_gather x1 -> x0, blocking collectives: 40.8 us -> none  [on_device(): gathered = lax.all_gather(packed, 'z', axis=0, tiled=True)]
    all_to_all x1 -> x2, waiting for transfers between devices: 0.01 us -> 29.1 us  [exchange(): return lax.all_to_all(value, axes, split_axis=0, concat_axis=0, tiled=True)]
    all_to_all x1 -> x2, starting transfers between devices: 3.65 us -> 18.7 us  [exchange(): return lax.all_to_all(value, axes, split_axis=0, concat_axis=0, tiled=True)]
    pallas_call x5, Pallas kernels: 13.7 us -> 3.65 us  [the longest x1 1.25 us: output_rows(): call(body, [((slots, part), bf16)], [SMEM, VMEM] + [VMEM] * n_dp)]
    all_to_all x3, blocking collectives: 103 us -> 100 us  [exchange(): return lax.all_to_all(value, axes, split_axis=0, concat_axis=0, tiled=True)]
    pallas_call x1, Pallas kernels: 6.35 us -> 4.06 us  [hidden_rows(): pl.pallas_call(body, grid=(n_dp,), out_shape=jax.ShapeDtypeStruct((n_dp,...]
  transfers between devices with their start and end apart: 4 -> 5, of which waited for: 2 -> 3; matrix products, arithmetic and copies ran while one was open for 0% -> 1% of each run, Pallas kernels for 0% -> 0%
where the time goes in v2:
time: 204 us; the launch traced here: 202 us
  blocking collectives  108 us (53%)
  waiting for transfers between devices  51.7 us (25%)
  starting transfers between devices  30.5 us (15%)
  Pallas kernels  7.71 us (4%)
  local copies, waits for them, and re-layouts  4.51 us (2%)
    all_to_all x3, blocking collectives, exchange(): return lax.all_to_all(value, axes, split_axis=0, concat_axis=0, tiled=True)  100 us
    all_to_all x2, waiting for transfers between devices, exchange(): return lax.all_to_all(value, axes, split_axis=0, concat_axis=0, tiled=True)  29.1 us
    ppermute x3, waiting for transfers between devices, on_device(): piece = lax.ppermute(piece, 'y', [(i, (i + s) % n_dp) for i in range(n_dp)])  22.7 us
    all_to_all x2, starting transfers between devices, exchange(): return lax.all_to_all(value, axes, split_axis=0, concat_axis=0, tiled=True)  18.7 us
    ppermute x3, starting transfers between devices, on_device(): piece = lax.ppermute(piece, 'y', [(i, (i + s) % n_dp) for i in range(n_dp)])  11.8 us
    all_to_all x1, blocking collectives, on_device(): return lax.all_to_all(routed, 'y', split_axis=0, concat_axis=1, tiled=True)  7.78 us
  transfers between devices with their start and end apart: 5, of which 3 were waited for; matrix products, arithmetic and copies ran while one was open for 1% of the time, Pallas kernels for 0%

profile of v2, /device:TPU:6, one launch (start us, length us, event | category | flops | bytes accessed | tf_op | source)
XLA Modules:
  0.0 202.5 jit_solution(15530062906237522238)
XLA Ops:
  0.0 0.0 copy-start.2
  0.0 0.9 copy-done.2
  0.9 0.0 copy-start.3
  0.9 0.7 copy-done.3
  1.6 0.0 copy-start.4
  1.6 0.7 copy-done.4
  2.3 0.9 shard_map.64
  3.2 15.2 %all-to-all-start = ((bf16[16,16,1024]{2,1,0:T(8,128)(2,1)}), bf16[16,16,1024]{2,1,0:T(8,128)(2,1)S(1)}, u32[]{:S(2)}, u32[]{:S(2)}) async-start(bf16[16,16,1024]{2,1,0:T(8,128)(2,1)} %shard_map.64), calls=%async_computation | async-start | bytes 1048576 | tf_op jit(solution)/shard_map/all_to_all | solution.py:182
  18.4 29.1 %all-to-all-done = bf16[16,16,1024]{2,1,0:T(8,128)(2,1)S(1)} async-done(((bf16[16,16,1024]{2,1,0:T(8,128)(2,1)}), bf16[16,16,1024]{2,1,0:T(8,128)(2,1)S(1)}, u32[]{:S(2)}, u32[]{:S(2)}) %all-to-all-start) | async-done | bytes 524320 | tf_op jit(solution)/shard_map/all_to_all | solution.py:182
  47.5 0.7 shard_map.65
  48.2 0.0 copy-start
  48.2 0.0 copy-start.1
  48.2 50.7 %all_to_all.44 = bf16[32,64,896]{2,1,0:T(8,128)(2,1)S(1)} all-to-all(bf16[32,64,896]{2,1,0:T(8,128)(2,1)S(1)} %bitcast.24), channel_id=1, replica_groups=mesh['x'=4,'z'=16,'c'=2,'y'=4] {'y','x','c'}, dimensions={0} | all-to-all | bytes 7340032 | tf_op jit(solution)/shard_map/all_to_all | solution.py:182
  98.9 0.0 copy-done
  98.9 0.0 copy-done.1
  98.9 4.1 %hidden_rows.1 = bf16[4,512,256]{2,1,0:T(8,128)(2,1)} custom-call(bf16[4,512,896]{2,1,0:T(8,128)(2,1)S(1)} %bitcast.23, bf16[3584,256]{1,0:T(8,128)(2,1)S(1)} %bitcast.29, bf16[3584,256]{1,0:T(8,128)(2,1)S(1)} %bitcast.30), custom_call_target="tpu_custom_call" | custom-call | tf_op jit(solution)/shard_map/hidden_rows/pallas_call | solution.py:122
  102.9 3.5 %all-to-all-start.2 = ((bf16[4,512,256]{2,1,0:T(8,128)(2,1)}), bf16[4,512,256]{2,1,0:T(8,128)(2,1)S(1)}, u32[]{:S(2)}, u32[]{:S(2)}) async-start(bf16[4,512,256]{2,1,0:T(8,128)(2,1)} %hidden_rows.1), calls=%async_computation.2 | async-start | bytes 2097152 | tf_op jit(solution)/shard_map/all_to_all | solution.py:182
  106.5 1.6 dynamic-slice_bitcast_fusion
  108.1 3.8 %collective-permute-start = (bf16[256,896]{1,0:T(8,128)(2,1)S(1)}, bf16[256,896]{1,0:T(8,128)(2,1)S(1)}, u32[]{:S(2)}, u32[]{:S(2)}) collective-permute-start(bf16[256,896]{1,0:T(8,128)(2,1)S(1)} %get-tuple-element.12), channel_id=1, source_target_pairs={{0,1},{1,2},{2,3},{3,0},{4,5},{5,6},{6,7},{7,4},{8,9},{9,10},{10,1... | collective-permute-start | bytes 1376264 | tf_op jit(solution)/shard_map/ppermute | solution.py:207
  111.9 4.6 %collective-permute-start.1 = (bf16[256,896]{1,0:T(8,128)(2,1)S(1)}, bf16[256,896]{1,0:T(8,128)(2,1)S(1)}, u32[]{:S(2)}, u32[]{:S(2)}) collective-permute-start(bf16[256,896]{1,0:T(8,128)(2,1)S(1)} %get-tuple-element.14), channel_id=1, source_target_pairs={{0,2},{1,3},{2,0},{3,1},{4,6},{5,7},{6,4},{7,5},{8,10},{9,11},{10,... | collective-permute-start | bytes 1376264 | tf_op jit(solution)/shard_map/ppermute | solution.py:207
  116.5 3.4 %collective-permute-start.2 = (bf16[256,896]{1,0:T(8,128)(2,1)S(1)}, bf16[256,896]{1,0:T(8,128)(2,1)S(1)}, u32[]{:S(2)}, u32[]{:S(2)}) collective-permute-start(bf16[256,896]{1,0:T(8,128)(2,1)S(1)} %get-tuple-element.11), channel_id=1, source_target_pairs={{0,3},{1,0},{2,1},{3,2},{4,7},{5,4},{6,5},{7,6},{8,11},{9,8},{10,9... | collective-permute-start | bytes 1376264 | tf_op jit(solution)/shard_map/ppermute | solution.py:207
  119.9 12.5 %collective-permute-done.refs_1_ = bf16[256,896]{1,0:T(8,128)(2,1)S(1)} collective-permute-done((bf16[256,896]{1,0:T(8,128)(2,1)S(1)}, bf16[256,896]{1,0:T(8,128)(2,1)S(1)}, u32[]{:S(2)}, u32[]{:S(2)}) %collective-permute-start) | collective-permute-done | bytes 458784 | tf_op jit(solution)/shard_map/ppermute | solution.py:207
  132.4 10.2 %collective-permute-done.1.refs_2_ = bf16[256,896]{1,0:T(8,128)(2,1)S(1)} collective-permute-done((bf16[256,896]{1,0:T(8,128)(2,1)S(1)}, bf16[256,896]{1,0:T(8,128)(2,1)S(1)}, u32[]{:S(2)}, u32[]{:S(2)}) %collective-permute-start.1) | collective-permute-done | bytes 458784 | tf_op jit(solution)/shard_map/ppermute | solution.py:207
  142.6 0.0 collective-permute-done.2.refs_3_
  142.6 0.0 all-to-all-done.2.hidden_ref
  142.6 1.2 shard_map.66
  143.8 16.8 %all_to_all.45 = bf16[8,64,896]{2,1,0:T(8,128)(2,1)S(1)} all-to-all(bf16[8,64,896]{2,1,0:T(8,128)(2,1)S(1)} %bitcast.26), channel_id=1, replica_groups=mesh['x'=4,'z'=16,'c'=2,'y'=4] {'x','c'}, dimensions={0} | all-to-all | bytes 1835008 | tf_op jit(solution)/shard_map/all_to_all | solution.py:182
  160.6 0.7 shard_map.67
  161.4 32.6 %all_to_all.46.shares_ref = bf16[16,16,896]{2,1,0:T(8,128)(2,1)S(1)} all-to-all(bf16[16,16,896]{2,1,0:T(8,128)(2,1)S(1)} %bitcast.28), channel_id=1, replica_groups=mesh['x'=4,'z'=16,'c'=2,'y'=4] {'z'}, dimensions={0} | all-to-all | bytes 917504 | tf_op jit(solution)/shard_map/all_to_all | solution.py:182
  194.0 0.1 shard_map.68
  194.1 7.8 %all_to_all.47 = bf16[4,4,896]{2,1,0:T(4,128)(2,1)S(1)} all-to-all(bf16[4,4,896]{2,1,0:T(4,128)(2,1)S(1)} %all_to_all.34), channel_id=1, replica_groups=mesh['x'=4,'z'=16,'c'=2,'y'=4] {'y'}, dimensions={0} | all-to-all | bytes 57344 | tf_op jit(solution)/shard_map/all_to_all | solution.py:221
  201.9 0.6 copy.9
  (1 shorter events, 0.0 us)
Async XLA Ops:
  0.0 0.9 copy-start.2
  0.9 0.7 copy-start.3
  1.6 0.7 copy-start.4
  3.2 44.3 %all-to-all-start = ((bf16[16,16,1024]{2,1,0:T(8,128)(2,1)}), bf16[16,16,1024]{2,1,0:T(8,128)(2,1)S(1)}, u32[]{:S(2)}, u32[]{:S(2)}) async-start(bf16[16,16,1024]{2,1,0:T(8,128)(2,1)} %shard_map.64), calls=%async_computation | async-start | bytes 1048576 | tf_op jit(solution)/shard_map/all_to_all | solution.py:182
  48.2 50.7 %copy-start = (bf16[1,3584,256]{2,1,0:T(8,128)(2,1)S(1)}, bf16[1,3584,256]{2,1,0:T(8,128)(2,1)}, u32[]{:S(2)}) copy-start(bf16[1,3584,256]{2,1,0:T(8,128)(2,1)} %param.9) | copy-start | bytes 5505028
  48.2 50.7 %copy-start.1 = (bf16[1,3584,256]{2,1,0:T(8,128)(2,1)S(1)}, bf16[1,3584,256]{2,1,0:T(8,128)(2,1)}, u32[]{:S(2)}) copy-start(bf16[1,3584,256]{2,1,0:T(8,128)(2,1)} %param.10) | copy-start | bytes 5505028
  102.9 39.6 %all-to-all-start.2 = ((bf16[4,512,256]{2,1,0:T(8,128)(2,1)}), bf16[4,512,256]{2,1,0:T(8,128)(2,1)S(1)}, u32[]{:S(2)}, u32[]{:S(2)}) async-start(bf16[4,512,256]{2,1,0:T(8,128)(2,1)} %hidden_rows.1), calls=%async_computation.2 | async-start | bytes 2097152 | tf_op jit(solution)/shard_map/all_to_all | solution.py:182
  108.1 24.3 %collective-permute-start = (bf16[256,896]{1,0:T(8,128)(2,1)S(1)}, bf16[256,896]{1,0:T(8,128)(2,1)S(1)}, u32[]{:S(2)}, u32[]{:S(2)}) collective-permute-start(bf16[256,896]{1,0:T(8,128)(2,1)S(1)} %get-tuple-element.12), channel_id=1, source_target_pairs={{0,1},{1,2},{2,3},{3,0},{4,5},{5,6},{6,7},{7,4},{8,9},{9,10},{10,1... | collective-permute-start | bytes 1376264 | tf_op jit(solution)/shard_map/ppermute | solution.py:207
  111.9 30.6 %collective-permute-start.1 = (bf16[256,896]{1,0:T(8,128)(2,1)S(1)}, bf16[256,896]{1,0:T(8,128)(2,1)S(1)}, u32[]{:S(2)}, u32[]{:S(2)}) collective-permute-start(bf16[256,896]{1,0:T(8,128)(2,1)S(1)} %get-tuple-element.14), channel_id=1, source_target_pairs={{0,2},{1,3},{2,0},{3,1},{4,6},{5,7},{6,4},{7,5},{8,10},{9,11},{10,... | collective-permute-start | bytes 1376264 | tf_op jit(solution)/shard_map/ppermute | solution.py:207
  116.5 26.0 %collective-permute-start.2 = (bf16[256,896]{1,0:T(8,128)(2,1)S(1)}, bf16[256,896]{1,0:T(8,128)(2,1)S(1)}, u32[]{:S(2)}, u32[]{:S(2)}) collective-permute-start(bf16[256,896]{1,0:T(8,128)(2,1)S(1)} %get-tuple-element.11), channel_id=1, source_target_pairs={{0,3},{1,0},{2,1},{3,2},{4,7},{5,4},{6,5},{7,6},{8,11},{9,8},{10,9... | collective-permute-start | bytes 1376264 | tf_op jit(solution)/shard_map/ppermute | solution.py:207

commit v3 on v2

--- a/solution.py
+++ b/solution.py
@@ -14,10 +14,11 @@
 f32, bf16, i32 = jnp.float32, jnp.bfloat16, jnp.int32
 PARAMS = pltpu.CompilerParams(vmem_limit_bytes=20 * 1024 * 1024)
 VMEM = pl.BlockSpec(memory_space=pltpu.VMEM)
+HBM = pl.BlockSpec(memory_space=pltpu.HBM)
 SMEM = pl.BlockSpec(memory_space=pltpu.SMEM)
 
 
-def call(body, outs, ins, scratch=()):
+def call(body, outs, ins, scratch=(), params=PARAMS):
     many = isinstance(outs, tuple)
     return pl.pallas_call(
         body,
@@ -25,7 +26,7 @@
         in_specs=ins,
         out_specs=(VMEM,) * len(outs) if many else VMEM,
         scratch_shapes=list(scratch),
-        compiler_params=PARAMS,
+        compiler_params=params,
     )
 
 
@@ -34,9 +35,18 @@
     top = expert_ids.shape[1]
     part = width // n_dp
 
-    def body(member_ref, tokens_ref, ids_ref, logits_ref, out_ref):
+    def body(member_ref, tokens_hbm, ids_hbm, logits_hbm, out_ref, own_ref, ids_ref, logits_ref, sems):
         start = pl.multiple_of(member_ref[0] * part, 128)
-        own = tokens_ref[:, pl.ds(start, part)]
+        copies = [
+            pltpu.make_async_copy(tokens_hbm.at[:, pl.ds(start, part)], own_ref, sems.at[0]),
+            pltpu.make_async_copy(ids_hbm, ids_ref, sems.at[1]),
+            pltpu.make_async_copy(logits_hbm, logits_ref, sems.at[2]),
+        ]
+        for copy in copies:
+            copy.start()
+        for copy in copies:
+            copy.wait()
+        own = own_ref[...]
         scores = 1.0 / (1.0 + jnp.exp(-logits_ref[...]))
         weights = route_scale * scores / jnp.sum(scores, axis=0, keepdims=True)
         high = weights.astype(bf16).astype(f32)
@@ -49,7 +59,13 @@
             out_ref[z, :, part:] = side
 
     outs = [((n_z, rows, part + SIDE), bf16)]
-    return call(body, outs, [SMEM, VMEM, VMEM, VMEM])(member, tokens, expert_ids.T, route_logits.T)
+    scratch = [
+        pltpu.VMEM((rows, part), bf16),
+        pltpu.VMEM((top, rows), i32),
+        pltpu.VMEM((top, rows), f32),
+        pltpu.SemaphoreType.DMA((3,)),
+    ]
+    return call(body, outs, [SMEM, HBM, HBM, HBM], scratch, None)(member, tokens, expert_ids.T, route_logits.T)
 
 
 def route_rows(gathered, plane, rows, top, n_x, n_z, n_c, n_dp):
@@ -100,39 +116,19 @@
     n_dp, slots, part = received.shape
     units = w_gate.shape[1]
 
-    def body(rows_ref, gate_ref, up_ref, out_ref, sum_gate, sum_up):
-        step = pl.program_id(0)
-
-        @pl.when(step == 0)
-        def _():
-            sum_gate[...] = jnp.zeros_like(sum_gate)
-            sum_up[...] = jnp.zeros_like(sum_up)
-
-        rows = rows_ref[0]
-        sum_gate[...] += jnp.dot(rows, gate_ref[...], preferred_element_type=f32)
-        sum_up[...] += jnp.dot(rows, up_ref[...], preferred_element_type=f32)
-
-        @pl.when(step == n_dp - 1)
-        def _():
-            v = sum_gate[...]
-            made = (v / (1.0 + jnp.exp(-v)) * sum_up[...]).astype(bf16)
-            for d in range(n_dp):
-                out_ref[d] = made
-
-    return pl.pallas_call(
-        body,
-        grid=(n_dp,),
-        out_shape=jax.ShapeDtypeStruct((n_dp, slots, units), bf16),
-        in_specs=[
-            pl.BlockSpec((1, slots, part), lambda i: (i, 0, 0)),
-            pl.BlockSpec((part, units), lambda i: (i, 0)),
-            pl.BlockSpec((part, units), lambda i: (i, 0)),
-        ],
-        out_specs=pl.BlockSpec((n_dp, slots, units), lambda i: (0, 0, 0)),
-        scratch_shapes=[pltpu.VMEM((slots, units), f32), pltpu.VMEM((slots, units), f32)],
-        compiler_params=PARAMS,
-        name="hidden_rows",
-    )(received, w_gate, w_up)
+    def body(rows_ref, gate_ref, up_ref, out_ref):
+        v = jnp.zeros((slots, units), f32)
+        u = jnp.zeros((slots, units), f32)
+        for d in range(n_dp):
+            rows = rows_ref[d]
+            at = slice(d * part, (d + 1) * part)
+            v = v + jnp.dot(rows, gate_ref[at, :], preferred_element_type=f32)
+            u = u + jnp.dot(rows, up_ref[at, :], preferred_element_type=f32)
+        made = (v / (1.0 + jnp.exp(-v)) * u).astype(bf16)
+        for d in range(n_dp):
+            out_ref[d] = made
+
+    return call(body, [((n_dp, slots, units), bf16)], [VMEM] * 3)(received, w_gate, w_up)
 
 
 def output_rows(hidden, downs, member):
@@ -152,7 +148,7 @@
     )
 
 
-def mix_rows(received, high, low):
+def mix_rows(received, high, low, share):
     _, part = received.shape
     total = high.shape[1]
 
@@ -161,21 +157,23 @@
         dims = (((0,), (0,)), ((), ()))
         mixed = lax.dot_general(high_ref[...], rows, dims, preferred_element_type=f32)
         mixed = mixed + lax.dot_general(low_ref[...], rows, dims, preferred_element_type=f32)
-        out_ref[...] = mixed.astype(bf16)
-
-    return call(body, [((total, part), bf16)], [VMEM] * 3)(received, high, low)
-
-
-def sum_rows(shares):
-    n_z, rows, part = shares.shape
+        for i in range(total // share):
+            out_ref[i] = mixed[i * share : (i + 1) * share, :].astype(bf16)
+
+    return call(body, [((total // share, share, part), bf16)], [VMEM] * 3)(received, high, low)
+
+
+def sum_rows(shares, n_dp):
+    peers, share, part = shares.shape
 
     def body(shares_ref, out_ref):
-        total = shares_ref[0].astype(f32)
-        for z in range(1, n_z):
-            total = total + shares_ref[z].astype(f32)
-        out_ref[...] = total.astype(bf16)
-
-    return call(body, [((rows, part), bf16)], [VMEM])(shares)
+        for d in range(n_dp):
+            total = shares_ref[d].astype(f32)
+            for z in range(1, peers // n_dp):
+                total = total + shares_ref[z * n_dp + d].astype(f32)
+            out_ref[:, d * part : (d + 1) * part] = total.astype(bf16)
+
+    return call(body, [((share, n_dp * part), bf16)], [VMEM])(shares)
 
 
 def exchange(value, axes):
@@ -212,13 +210,13 @@
     )
     arrived = exchange(outgoing.reshape(n_dp * n_x * n_c, held, part), ("y", "x", "c"))
     hidden = hidden_rows(arrived.reshape(n_dp, slots, part), w_gate, w_up)
+    hidden, downs = lax.optimization_barrier((hidden, downs))
     hidden = exchange(hidden, "y")
     results = output_rows(hidden, downs, member_ref)
     back = exchange(results.reshape(n_x * n_c, held, part), ("x", "c"))
-    mixed = mix_rows(back.reshape(slots, part), high, low)
-    shares = exchange(mixed.reshape(n_z, rows, part), "z")
-    routed = sum_rows(shares)
-    return lax.all_to_all(routed, "y", split_axis=0, concat_axis=1, tiled=True)
+    mixed = mix_rows(back.reshape(slots, part), high, low, rows // n_dp)
+    shares = exchange(mixed, ("z", "y"))
+    return sum_rows(shares, n_dp)
 
 
 def solution(mesh):

time: 204 us -> 198 us (0.971)
  blocking collectives: 108 us -> 72.1 us
  waiting for transfers between devices: 51.7 us -> 72.6 us
  starting transfers between devices: 30.5 us -> 34.2 us
  Pallas kernels: 7.71 us -> 10.5 us
  local copies, waits for them, and re-layouts: 4.51 us -> 6.8 us
    all_to_all x2, waiting for transfers between devices: 29.1 us -> 58.1 us  [exchange(): return lax.all_to_all(value, axes, split_axis=0, concat_axis=0, tiled=True)]
    all_to_all x3, blocking collectives: 100 us -> 72.1 us  [exchange(): return lax.all_to_all(value, axes, split_axis=0, concat_axis=0, tiled=True)]
    ppermute x3, waiting for transfers between devices: 22.7 us -> 14.5 us  [on_device(): piece = lax.ppermute(piece, 'y', [(i, (i + s) % n_dp) for i in range(n_dp)])]
    all_to_all x1 -> x0, blocking collectives: 7.78 us -> none  [on_device(): return lax.all_to_all(routed, 'y', split_axis=0, concat_axis=1, tiled=True)]
    all_to_all x2, starting transfers between devices: 18.7 us -> 22.8 us  [exchange(): return lax.all_to_all(value, axes, split_axis=0, concat_axis=0, tiled=True)]
  transfers between devices with their start and end apart: 5 -> 5, of which waited for: 3 -> 4; matrix products, arithmetic and copies ran while one was open for 1% -> 1% of each run, Pallas kernels for 0% -> 2%
where the time goes in v3:
time: 198 us; the launch traced here: 196 us
  waiting for transfers between devices  72.6 us (37%)
  blocking collectives  72.1 us (36%)
  starting transfers between devices  34.2 us (17%)
  Pallas kernels  10.5 us (5%)
  local copies, waits for them, and re-layouts  6.8 us (3%)
    all_to_all x3, blocking collectives, exchange(): return lax.all_to_all(value, axes, split_axis=0, concat_axis=0, tiled=True)  72.1 us
    all_to_all x2, waiting for transfers between devices, exchange(): return lax.all_to_all(value, axes, split_axis=0, concat_axis=0, tiled=True)  58.1 us
    all_to_all x2, starting transfers between devices, exchange(): return lax.all_to_all(value, axes, split_axis=0, concat_axis=0, tiled=True)  22.8 us
    ppermute x3, waiting for transfers between devices, on_device(): piece = lax.ppermute(piece, 'y', [(i, (i + s) % n_dp) for i in range(n_dp)])  14.5 us
    ppermute x3, starting transfers between devices, on_device(): piece = lax.ppermute(piece, 'y', [(i, (i + s) % n_dp) for i in range(n_dp)])  11.3 us
    pallas_call x1, Pallas kernels, hidden_rows(): call(body, [((n_dp, slots, units), bf16)], [VMEM] * 3)  4.38 us
    unnamed x10, local copies, waits for them, and re-layouts  4.03 us
  transfers between devices with their start and end apart: 5, of which 4 were waited for; matrix products, arithmetic and copies ran while one was open for 1% of the time, Pallas kernels for 2%

profile of v3, /device:TPU:6, one launch (start us, length us, event | category | flops | bytes accessed | tf_op | source)
XLA Modules:
  0.0 196.3 jit_solution(7532360292911408482)
XLA Ops:
  0.0 1.7 shard_map.64
  1.7 15.2 %all-to-all-start = ((bf16[16,16,1024]{2,1,0:T(8,128)(2,1)}), bf16[16,16,1024]{2,1,0:T(8,128)(2,1)S(1)}, u32[]{:S(2)}, u32[]{:S(2)}) async-start(bf16[16,16,1024]{2,1,0:T(8,128)(2,1)} %shard_map.64), calls=%async_computation | async-start | bytes 1048576 | tf_op jit(solution)/shard_map/all_to_all | solution.py:180
  16.9 29.1 %all-to-all-done = bf16[16,16,1024]{2,1,0:T(8,128)(2,1)S(1)} async-done(((bf16[16,16,1024]{2,1,0:T(8,128)(2,1)}), bf16[16,16,1024]{2,1,0:T(8,128)(2,1)S(1)}, u32[]{:S(2)}, u32[]{:S(2)}) %all-to-all-start) | async-done | bytes 524320 | tf_op jit(solution)/shard_map/all_to_all | solution.py:180
  46.0 0.7 shard_map.65
  46.7 0.0 copy-start
  46.7 1.8 copy-done
  48.5 0.0 copy-start.3
  48.5 0.7 copy-done.3
  49.2 7.6 %all-to-all-start.1 = ((bf16[32,64,896]{2,1,0:T(8,128)(2,1)}), bf16[32,64,896]{2,1,0:T(8,128)(2,1)}, u32[]{:S(2)}, u32[]{:S(2)}) async-start(bf16[32,64,896]{2,1,0:T(8,128)(2,1)} %bitcast.19), calls=%async_computation.1 | async-start | bytes 7340032 | tf_op jit(solution)/shard_map/all_to_all | solution.py:180
  56.9 0.0 copy-start.1
  56.9 2.8 %dynamic-slice_bitcast_fusion = (bf16[256,896]{1,0:T(8,128)(2,1)}, bf16[256,896]{1,0:T(8,128)(2,1)}, bf16[256,896]{1,0:T(8,128)(2,1)S(1)}, bf16[256,896]{1,0:T(8,128)(2,1)}) fusion(bf16[1,256,3584]{2,1,0:T(8,128)(2,1)} %param.11, s32[]{:T(128)S(6)} %select_n.32, s32[]{:T(128)S(6)} %select_n.28, s32[]{:T(128)S(6)} %select_n.26, s32[]{:T(128)S(6)} %select_n.30), kind=kLoop, calls=%fused_computation | loop fusion | bytes 3670032 | tf_op jit(solution)/shard_map/dynamic_slice | solution.py:203
  59.6 3.4 %collective-permute-start = (bf16[256,896]{1,0:T(8,128)(2,1)}, bf16[256,896]{1,0:T(8,128)(2,1)S(1)}, u32[]{:S(2)}, u32[]{:S(2)}) collective-permute-start(bf16[256,896]{1,0:T(8,128)(2,1)} %get-tuple-element.22), channel_id=1, source_target_pairs={{0,1},{1,2},{2,3},{3,0},{4,5},{5,6},{6,7},{7,4},{8,9},{9,10},{10,1... | collective-permute-start | bytes 1376264 | tf_op jit(solution)/shard_map/ppermute | solution.py:205
  63.0 4.7 %collective-permute-start.1 = (bf16[256,896]{1,0:T(8,128)(2,1)}, bf16[256,896]{1,0:T(8,128)(2,1)S(1)}, u32[]{:S(2)}, u32[]{:S(2)}) collective-permute-start(bf16[256,896]{1,0:T(8,128)(2,1)} %get-tuple-element.24), channel_id=1, source_target_pairs={{0,2},{1,3},{2,0},{3,1},{4,6},{5,7},{6,4},{7,5},{8,10},{9,11},{10,... | collective-permute-start | bytes 1376264 | tf_op jit(solution)/shard_map/ppermute | solution.py:205
  67.7 3.3 %collective-permute-start.2 = (bf16[256,896]{1,0:T(8,128)(2,1)}, bf16[256,896]{1,0:T(8,128)(2,1)}, u32[]{:S(2)}, u32[]{:S(2)}) collective-permute-start(bf16[256,896]{1,0:T(8,128)(2,1)} %get-tuple-element.21), channel_id=1, source_target_pairs={{0,3},{1,0},{2,1},{3,2},{4,7},{5,4},{6,5},{7,6},{8,11},{9,8},{10,9... | collective-permute-start | bytes 1376264 | tf_op jit(solution)/shard_map/ppermute | solution.py:205
  71.0 29.0 %all-to-all-done.1 = bf16[32,64,896]{2,1,0:T(8,128)(2,1)} async-done(((bf16[32,64,896]{2,1,0:T(8,128)(2,1)}), bf16[32,64,896]{2,1,0:T(8,128)(2,1)}, u32[]{:S(2)}, u32[]{:S(2)}) %all-to-all-start.1) | async-done | bytes 3670048 | tf_op jit(solution)/shard_map/all_to_all | solution.py:180
  100.0 0.0 copy-done.1
  100.0 0.0 copy-start.2
  100.0 1.5 copy-done.2
  101.5 4.4 %shard_map.66 = bf16[4,512,256]{2,1,0:T(8,128)(2,1)S(1)} custom-call(bf16[4,512,896]{2,1,0:T(8,128)(2,1)} %bitcast.6.rows_ref, bf16[3584,256]{1,0:T(8,128)(2,1)S(1)} %bitcast.23, bf16[3584,256]{1,0:T(8,128)(2,1)S(1)} %bitcast.24), custom_call_target="tpu_custom_call" | custom-call | tf_op jit(solution)/shard_map/pallas_call | solution.py:131
  105.9 3.9 %collective-permute-done.refs_1_ = bf16[256,896]{1,0:T(8,128)(2,1)S(1)} collective-permute-done((bf16[256,896]{1,0:T(8,128)(2,1)}, bf16[256,896]{1,0:T(8,128)(2,1)S(1)}, u32[]{:S(2)}, u32[]{:S(2)}) %collective-permute-start) | collective-permute-done | bytes 458784 | tf_op jit(solution)/shard_map/ppermute | solution.py:205
  109.8 10.7 %collective-permute-done.1.refs_2_ = bf16[256,896]{1,0:T(8,128)(2,1)S(1)} collective-permute-done((bf16[256,896]{1,0:T(8,128)(2,1)}, bf16[256,896]{1,0:T(8,128)(2,1)S(1)}, u32[]{:S(2)}, u32[]{:S(2)}) %collective-permute-start.1) | collective-permute-done | bytes 458784 | tf_op jit(solution)/shard_map/ppermute | solution.py:205
  120.4 0.0 collective-permute-done.2.refs_3_
  120.4 17.5 %all_to_all.25.hidden_ref = bf16[4,512,256]{2,1,0:T(8,128)(2,1)S(1)} all-to-all(bf16[4,512,256]{2,1,0:T(8,128)(2,1)S(1)} %shard_map.66), channel_id=1, replica_groups=mesh['x'=4,'z'=16,'c'=2,'y'=4] {'y'}, dimensions={0} | all-to-all | bytes 2097152 | tf_op jit(solution)/shard_map/all_to_all | solution.py:180
  137.9 2.3 %shard_map.67 = bf16[512,896]{1,0:T(8,128)(2,1)S(1)} custom-call(s32[1]{0:T(128)} %bitcast.member_ref, bf16[4,512,256]{2,1,0:T(8,128)(2,1)S(1)} %all_to_all.25.hidden_ref, bf16[256,896]{1,0:T(8,128)(2,1)S(1)} %get-tuple-element.15.refs_0_, bf16[256,896]{1,0:T(8,128)(2,1)S(1)} %collective-permute-done.refs_1_, ...), custom_call_target="tpu_custom_call" | custom-call | tf_op jit(solution)/shard_map/pallas_call | solution.py:146
  140.2 0.0 copy-start.4
  140.2 17.1 %all_to_all.26 = bf16[8,64,896]{2,1,0:T(8,128)(2,1)S(1)} all-to-all(bf16[8,64,896]{2,1,0:T(8,128)(2,1)S(1)} %bitcast.21), channel_id=1, replica_groups=mesh['x'=4,'z'=16,'c'=2,'y'=4] {'x','c'}, dimensions={0} | all-to-all | bytes 1835008 | tf_op jit(solution)/shard_map/all_to_all | solution.py:180
  157.3 0.0 copy-done.4
  157.3 0.7 shard_map.68
  158.1 37.5 %all_to_all.27.shares_ref = bf16[64,4,896]{2,1,0:T(4,128)(2,1)S(1)} all-to-all(bf16[64,4,896]{2,1,0:T(4,128)(2,1)S(1)} %shard_map.68), channel_id=1, replica_groups=mesh['x'=4,'z'=16,'c'=2,'y'=4] {'z','y'}, dimensions={0} | all-to-all | bytes 917504 | tf_op jit(solution)/shard_map/all_to_all | solution.py:180
  195.6 0.7 shard_map.69
Async XLA Ops:
  1.7 44.3 %all-to-all-start = ((bf16[16,16,1024]{2,1,0:T(8,128)(2,1)}), bf16[16,16,1024]{2,1,0:T(8,128)(2,1)S(1)}, u32[]{:S(2)}, u32[]{:S(2)}) async-start(bf16[16,16,1024]{2,1,0:T(8,128)(2,1)} %shard_map.64), calls=%async_computation | async-start | bytes 1048576 | tf_op jit(solution)/shard_map/all_to_all | solution.py:180
  46.7 1.8 copy-start
  48.5 0.7 copy-start.3
  49.2 50.8 %all-to-all-start.1 = ((bf16[32,64,896]{2,1,0:T(8,128)(2,1)}), bf16[32,64,896]{2,1,0:T(8,128)(2,1)}, u32[]{:S(2)}, u32[]{:S(2)}) async-start(bf16[32,64,896]{2,1,0:T(8,128)(2,1)} %bitcast.19), calls=%async_computation.1 | async-start | bytes 7340032 | tf_op jit(solution)/shard_map/all_to_all | solution.py:180
  56.9 43.1 %copy-start.1 = (bf16[1,3584,256]{2,1,0:T(8,128)(2,1)S(1)}, bf16[1,3584,256]{2,1,0:T(8,128)(2,1)}, u32[]{:S(2)}) copy-start(bf16[1,3584,256]{2,1,0:T(8,128)(2,1)} %param.9) | copy-start | bytes 5505028
  59.6 50.1 %collective-permute-start = (bf16[256,896]{1,0:T(8,128)(2,1)}, bf16[256,896]{1,0:T(8,128)(2,1)S(1)}, u32[]{:S(2)}, u32[]{:S(2)}) collective-permute-start(bf16[256,896]{1,0:T(8,128)(2,1)} %get-tuple-element.22), channel_id=1, source_target_pairs={{0,1},{1,2},{2,3},{3,0},{4,5},{5,6},{6,7},{7,4},{8,9},{9,10},{10,1... | collective-permute-start | bytes 1376264 | tf_op jit(solution)/shard_map/ppermute | solution.py:205
  63.0 57.4 %collective-permute-start.1 = (bf16[256,896]{1,0:T(8,128)(2,1)}, bf16[256,896]{1,0:T(8,128)(2,1)S(1)}, u32[]{:S(2)}, u32[]{:S(2)}) collective-permute-start(bf16[256,896]{1,0:T(8,128)(2,1)} %get-tuple-element.24), channel_id=1, source_target_pairs={{0,2},{1,3},{2,0},{3,1},{4,6},{5,7},{6,4},{7,5},{8,10},{9,11},{10,... | collective-permute-start | bytes 1376264 | tf_op jit(solution)/shard_map/ppermute | solution.py:205
  67.7 52.7 %collective-permute-start.2 = (bf16[256,896]{1,0:T(8,128)(2,1)}, bf16[256,896]{1,0:T(8,128)(2,1)}, u32[]{:S(2)}, u32[]{:S(2)}) collective-permute-start(bf16[256,896]{1,0:T(8,128)(2,1)} %get-tuple-element.21), channel_id=1, source_target_pairs={{0,3},{1,0},{2,1},{3,2},{4,7},{5,4},{6,5},{7,6},{8,11},{9,8},{10,9... | collective-permute-start | bytes 1376264 | tf_op jit(solution)/shard_map/ppermute | solution.py:205
  100.0 1.5 copy-start.2
  140.2 17.1 %copy-start.4 = (bf16[512,256]{1,0:T(8,128)(2,1)S(1)}, bf16[512,256]{1,0:T(8,128)(2,1)}, u32[]{:S(2)}) copy-start(bf16[512,256]{1,0:T(8,128)(2,1)} %copy-done.3) | copy-start | bytes 786436

commit v4 on v3

--- a/solution.py
+++ b/solution.py
@@ -30,7 +30,7 @@
     )
 
 
-def pack_rows(tokens, expert_ids, route_logits, member, n_dp, n_z):
+def pack_rows(tokens, expert_ids, route_logits, member, n_dp, peers):
     rows, width = tokens.shape
     top = expert_ids.shape[1]
     part = width // n_dp
@@ -54,11 +54,11 @@
             [ids_ref[...].astype(f32), high, weights - high, jnp.zeros((SIDE - 3 * top, rows), f32)], axis=0
         )
         side = side.T.astype(bf16)
-        for z in range(n_z):
+        for z in range(peers):
             out_ref[z, :, :part] = own
             out_ref[z, :, part:] = side
 
-    outs = [((n_z, rows, part + SIDE), bf16)]
+    outs = [((peers, rows, part + SIDE), bf16)]
     scratch = [
         pltpu.VMEM((rows, part), bf16),
         pltpu.VMEM((top, rows), i32),
@@ -68,15 +68,15 @@
     return call(body, outs, [SMEM, HBM, HBM, HBM], scratch, None)(member, tokens, expert_ids.T, route_logits.T)
 
 
-def route_rows(gathered, plane, rows, top, n_x, n_z, n_c, n_dp):
-    total = gathered.shape[0]
-    part = gathered.shape[1] - SIDE
+def route_rows(near, far, plane, rows, top, n_x, n_z, n_c, n_dp):
+    total = 2 * near.shape[0]
+    part = near.shape[1] - SIDE
     experts = n_x * n_c
     held = n_z * SLOTS
     pad = max(16, experts)
 
-    def body(plane_ref, gathered_ref, out_ref, high_ref, low_ref, pick_ref):
-        side = gathered_ref[:, part:].astype(f32).T
+    def body(plane_ref, near_ref, far_ref, out_ref, high_ref, low_ref, pick_ref):
+        side = jnp.concatenate([near_ref[:, part:], far_ref[:, part:]], axis=0).astype(f32).T
         line = lax.broadcasted_iota(i32, (pad, 1), 0)
         name = ((line // n_c) * n_z + plane_ref[0]) * n_c + line % n_c
         name = jnp.where(line < experts, name, -1).astype(f32)
@@ -102,14 +102,15 @@
             pick_ref[at, :] = jnp.where(hit, 1.0, 0.0).astype(bf16)
             high_ref[at, :] = jnp.where(hit, high[j : j + 1, :], 0.0).astype(bf16)
             low_ref[at, :] = jnp.where(hit, low[j : j + 1, :], 0.0).astype(bf16)
-        sent = jnp.dot(pick_ref[...], gathered_ref[:, :part], preferred_element_type=f32).astype(bf16)
+        own = jnp.concatenate([near_ref[:, :part], far_ref[:, :part]], axis=0)
+        sent = jnp.dot(pick_ref[...], own, preferred_element_type=f32).astype(bf16)
         for d in range(n_dp):
             out_ref[d] = sent
 
     slots = experts * held
     outs = (((n_dp, slots, part), bf16),) + (((slots, total), bf16),) * 2
     scratch = [pltpu.VMEM((slots, total), bf16)]
-    return call(body, outs, [SMEM, VMEM], scratch)(plane, gathered)
+    return call(body, outs, [SMEM, VMEM, VMEM], scratch)(plane, near, far)
 
 
 def hidden_rows(received, w_gate, w_up):
@@ -148,19 +149,30 @@
     )
 
 
-def mix_rows(received, high, low, share):
+def mix_rows(received, high, low):
     _, part = received.shape
-    total = high.shape[1]
-
-    def body(rows_ref, high_ref, low_ref, out_ref):
+    half = high.shape[1] // 2
+
+    def body(rows_ref, high_ref, low_ref, kept_ref, sent_ref):
         rows = rows_ref[...]
         dims = (((0,), (0,)), ((), ()))
         mixed = lax.dot_general(high_ref[...], rows, dims, preferred_element_type=f32)
         mixed = mixed + lax.dot_general(low_ref[...], rows, dims, preferred_element_type=f32)
+        kept_ref[...] = mixed[:half, :]
+        sent_ref[...] = mixed[half:, :].astype(bf16)
+
+    return call(body, (((half, part), f32), ((half, part), bf16)), [VMEM] * 3)(received, high, low)
+
+
+def add_pair(kept, received, share):
+    total, part = kept.shape
+
+    def body(kept_ref, received_ref, out_ref):
+        both = kept_ref[...] + received_ref[...].astype(f32)
         for i in range(total // share):
-            out_ref[i] = mixed[i * share : (i + 1) * share, :].astype(bf16)
-
-    return call(body, [((total // share, share, part), bf16)], [VMEM] * 3)(received, high, low)
+            out_ref[i] = both[i * share : (i + 1) * share, :].astype(bf16)
+
+    return call(body, [((total // share, share, part), bf16)], [VMEM] * 2)(kept, received)
 
 
 def sum_rows(shares, n_dp):
@@ -183,18 +195,19 @@
 def on_device(tokens, expert_ids, route_logits, expert_gate, expert_up, expert_down):
     rows, width = tokens.shape
     top = expert_ids.shape[1]
-    n_x, n_z, n_c, n_dp = (lax.axis_size(a) for a in ("x", "z", "c", "y"))
+    n_x, n_pair, n_c, n_dp = (lax.axis_size(a) for a in ("x", "zh", "c", "y"))
+    n_z = 2 * n_pair
     part = width // n_dp
     held = n_z * SLOTS
     slots = n_x * n_c * held
-    total = n_z * rows
     member = lax.axis_index("y").astype(i32)
     member_ref = member.reshape(1)
-    plane_ref = lax.axis_index("z").astype(i32).reshape(1)
+    plane_ref = (2 * lax.axis_index("zh") + lax.axis_index("zl")).astype(i32).reshape(1)
     w_gate, w_up = expert_gate[0], expert_up[0]
 
-    packed = pack_rows(tokens, expert_ids, route_logits, member_ref, n_dp, n_z)
-    gathered = exchange(packed, "z")
+    packed = pack_rows(tokens, expert_ids, route_logits, member_ref, n_dp, n_pair)
+    near = exchange(packed, "zh").reshape(n_pair * rows, -1)
+    far = lax.ppermute(near, "zl", [(0, 1), (1, 0)])
 
     downs = []
     for s in range(n_dp):
@@ -206,7 +219,7 @@
         downs.append(piece)
 
     outgoing, high, low = route_rows(
-        gathered.reshape(total, -1), plane_ref, rows, top, n_x, n_z, n_c, n_dp
+        near, far, plane_ref, rows, top, n_x, n_z, n_c, n_dp
     )
     arrived = exchange(outgoing.reshape(n_dp * n_x * n_c, held, part), ("y", "x", "c"))
     hidden = hidden_rows(arrived.reshape(n_dp, slots, part), w_gate, w_up)
@@ -214,16 +227,17 @@
     hidden = exchange(hidden, "y")
     results = output_rows(hidden, downs, member_ref)
     back = exchange(results.reshape(n_x * n_c, held, part), ("x", "c"))
-    mixed = mix_rows(back.reshape(slots, part), high, low, rows // n_dp)
-    shares = exchange(mixed, ("z", "y"))
+    kept, sent = mix_rows(back.reshape(slots, part), high, low)
+    sent = lax.ppermute(sent, "zl", [(0, 1), (1, 0)])
+    shares = exchange(add_pair(kept, sent, rows // n_dp), ("zh", "y"))
     return sum_rows(shares, n_dp)
 
 
 def solution(mesh):
     n_ep, n_dp = mesh.devices.shape
-    grid = mesh.devices.reshape(CHIPS_X, n_ep // (CHIPS_X * CORES), CORES, n_dp)
-    fine = Mesh(grid, ("x", "z", "c", "y"))
-    ep = ("x", "z", "c")
+    grid = mesh.devices.reshape(CHIPS_X, n_ep // (CHIPS_X * 2 * CORES), 2, CORES, n_dp)
+    fine = Mesh(grid, ("x", "zh", "zl", "c", "y"))
+    ep = ("x", "zh", "zl", "c")
     placed = (
         P(ep, None),
         P(ep, None),

time: 198 us -> 195 us (0.985)
  blocking collectives: 72.1 us -> 96 us
  waiting for transfers between devices: 72.6 us -> 57 us
  starting transfers between devices: 34.2 us -> 22.8 us
    all_to_all x2 -> x1, waiting for transfers between devices: 58.1 us -> 29 us  [exchange(): return lax.all_to_all(value, axes, split_axis=0, concat_axis=0, tiled=True)]
    all_to_all x3 -> x4, blocking collectives: 72.1 us -> 96 us  [exchange(): return lax.all_to_all(value, axes, split_axis=0, concat_axis=0, tiled=True)]
    all_to_all x2 -> x1, starting transfers between devices: 22.8 us -> 7.62 us  [exchange(): return lax.all_to_all(value, axes, split_axis=0, concat_axis=0, tiled=True)]
    ppermute x0 -> x2, waiting for transfers between devices: none -> 13.5 us  [the longest x1 7.12 us: on_device(): sent = lax.ppermute(sent, 'zl', [(0, 1), (1, 0)])]
    ppermute x0 -> x2, starting transfers between devices: none -> 3.83 us  [the longest x1 1.92 us: on_device(): sent = lax.ppermute(sent, 'zl', [(0, 1), (1, 0)])]
  transfers between devices with their start and end apart: 5 -> 6, of which waited for: 4 -> 5; matrix products, arithmetic and copies ran while one was open for 1% -> 1% of each run, Pallas kernels for 2% -> 2%
where the time goes in v4:
time: 195 us; the launch traced here: 193 us
  blocking collectives  96 us (49%)
  waiting for transfers between devices  57 us (29%)
  starting transfers between devices  22.8 us (12%)
  Pallas kernels  10.4 us (5%)
  local copies, waits for them, and re-layouts  6.77 us (3%)
    all_to_all x4, blocking collectives, exchange(): return lax.all_to_all(value, axes, split_axis=0, concat_axis=0, tiled=True)  96 us
    all_to_all x1, waiting for transfers between devices, exchange(): return lax.all_to_all(value, axes, split_axis=0, concat_axis=0, tiled=True)  29 us
    ppermute x3, waiting for transfers between devices, on_device(): piece = lax.ppermute(piece, 'y', [(i, (i + s) % n_dp) for i in range(n_dp)])  14.5 us
    ppermute x3, starting transfers between devices, on_device(): piece = lax.ppermute(piece, 'y', [(i, (i + s) % n_dp) for i in range(n_dp)])  11.3 us
    all_to_all x1, starting transfers between devices, exchange(): return lax.all_to_all(value, axes, split_axis=0, concat_axis=0, tiled=True)  7.62 us
    ppermute x1, waiting for transfers between devices, on_device(): sent = lax.ppermute(sent, 'zl', [(0, 1), (1, 0)])  7.12 us
    ppermute x1, waiting for transfers between devices, on_device(): far = lax.ppermute(near, 'zl', [(0, 1), (1, 0)])  6.33 us
    pallas_call x1, Pallas kernels, hidden_rows(): call(body, [((n_dp, slots, units), bf16)], [VMEM] * 3)  4.38 us
  transfers between devices with their start and end apart: 6, of which 5 were waited for; matrix products, arithmetic and copies ran while one was open for 1% of the time, Pallas kernels for 2%

profile of v4, /device:TPU:6, one launch (start us, length us, event | category | flops | bytes accessed | tf_op | source)
XLA Modules:
  0.0 193.1 jit_solution(16582425537878893450)
XLA Ops:
  0.0 1.6 shard_map.64
  1.6 36.5 %all_to_all.25 = bf16[8,16,1024]{2,1,0:T(8,128)(2,1)S(1)} all-to-all(bf16[8,16,1024]{2,1,0:T(8,128)(2,1)} %shard_map.64), channel_id=1, replica_groups=mesh['x'=4,'zh'=8,'zl'=2,'c'=2,'y'=4] {'zh'}, dimensions={0} | all-to-all | bytes 524288 | tf_op jit(solution)/shard_map/all_to_all | solution.py:192
  38.1 1.9 collective-permute-start
  40.0 6.3 %collective-permute-done.far_ref = bf16[128,1024]{1,0:T(8,128)(2,1)S(1)} collective-permute-done((bf16[128,1024]{1,0:T(8,128)(2,1)S(1)}, bf16[128,1024]{1,0:T(8,128)(2,1)S(1)}, u32[]{:S(2)}, u32[]{:S(2)}) %collective-permute-start) | collective-permute-done | bytes 262176 | tf_op jit(solution)/shard_map/ppermute | solution.py:210
  46.3 0.7 shard_map.65
  47.0 0.0 copy-start
  47.0 1.8 copy-done
  48.8 0.0 copy-start.3
  48.8 0.7 copy-done.3
  49.5 7.6 %all-to-all-start.1 = ((bf16[32,64,896]{2,1,0:T(8,128)(2,1)}), bf16[32,64,896]{2,1,0:T(8,128)(2,1)}, u32[]{:S(2)}, u32[]{:S(2)}) async-start(bf16[32,64,896]{2,1,0:T(8,128)(2,1)} %bitcast.19), calls=%async_computation.1 | async-start | bytes 7340032 | tf_op jit(solution)/shard_map/all_to_all | solution.py:192
  57.2 0.0 copy-start.1
  57.2 2.8 %dynamic-slice_bitcast_fusion = (bf16[256,896]{1,0:T(8,128)(2,1)}, bf16[256,896]{1,0:T(8,128)(2,1)}, bf16[256,896]{1,0:T(8,128)(2,1)S(1)}, bf16[256,896]{1,0:T(8,128)(2,1)}) fusion(bf16[1,256,3584]{2,1,0:T(8,128)(2,1)} %param.11, s32[]{:T(128)S(6)} %select_n.32, s32[]{:T(128)S(6)} %select_n.28, s32[]{:T(128)S(6)} %select_n.26, s32[]{:T(128)S(6)} %select_n.30), kind=kLoop, calls=%fused_computation | loop fusion | bytes 3670032 | tf_op jit(solution)/shard_map/dynamic_slice | solution.py:216
  60.0 3.4 %collective-permute-start.1 = (bf16[256,896]{1,0:T(8,128)(2,1)}, bf16[256,896]{1,0:T(8,128)(2,1)S(1)}, u32[]{:S(2)}, u32[]{:S(2)}) collective-permute-start(bf16[256,896]{1,0:T(8,128)(2,1)} %get-tuple-element.26), channel_id=1, source_target_pairs={{0,1},{1,2},{2,3},{3,0},{4,5},{5,6},{6,7},{7,4},{8,9},{9,10},{10,1... | collective-permute-start | bytes 1376264 | tf_op jit(solution)/shard_map/ppermute | solution.py:218
  63.3 4.7 %collective-permute-start.2 = (bf16[256,896]{1,0:T(8,128)(2,1)}, bf16[256,896]{1,0:T(8,128)(2,1)S(1)}, u32[]{:S(2)}, u32[]{:S(2)}) collective-permute-start(bf16[256,896]{1,0:T(8,128)(2,1)} %get-tuple-element.28), channel_id=1, source_target_pairs={{0,2},{1,3},{2,0},{3,1},{4,6},{5,7},{6,4},{7,5},{8,10},{9,11},{10,... | collective-permute-start | bytes 1376264 | tf_op jit(solution)/shard_map/ppermute | solution.py:218
  68.0 3.3 %collective-permute-start.3 = (bf16[256,896]{1,0:T(8,128)(2,1)}, bf16[256,896]{1,0:T(8,128)(2,1)}, u32[]{:S(2)}, u32[]{:S(2)}) collective-permute-start(bf16[256,896]{1,0:T(8,128)(2,1)} %get-tuple-element.25), channel_id=1, source_target_pairs={{0,3},{1,0},{2,1},{3,2},{4,7},{5,4},{6,5},{7,6},{8,11},{9,8},{10,9... | collective-permute-start | bytes 1376264 | tf_op jit(solution)/shard_map/ppermute | solution.py:218
  71.3 29.0 %all-to-all-done.1 = bf16[32,64,896]{2,1,0:T(8,128)(2,1)} async-done(((bf16[32,64,896]{2,1,0:T(8,128)(2,1)}), bf16[32,64,896]{2,1,0:T(8,128)(2,1)}, u32[]{:S(2)}, u32[]{:S(2)}) %all-to-all-start.1) | async-done | bytes 3670048 | tf_op jit(solution)/shard_map/all_to_all | solution.py:192
  100.3 0.0 copy-done.1
  100.4 0.0 copy-start.2
  100.4 1.5 copy-done.2
  101.9 4.4 %shard_map.66 = bf16[4,512,256]{2,1,0:T(8,128)(2,1)S(1)} custom-call(bf16[4,512,896]{2,1,0:T(8,128)(2,1)} %bitcast.6.rows_ref, bf16[3584,256]{1,0:T(8,128)(2,1)S(1)} %bitcast.22, bf16[3584,256]{1,0:T(8,128)(2,1)S(1)} %bitcast.23), custom_call_target="tpu_custom_call" | custom-call | tf_op jit(solution)/shard_map/pallas_call | solution.py:132
  106.2 3.9 %collective-permute-done.1.refs_1_ = bf16[256,896]{1,0:T(8,128)(2,1)S(1)} collective-permute-done((bf16[256,896]{1,0:T(8,128)(2,1)}, bf16[256,896]{1,0:T(8,128)(2,1)S(1)}, u32[]{:S(2)}, u32[]{:S(2)}) %collective-permute-start.1) | collective-permute-done | bytes 458784 | tf_op jit(solution)/shard_map/ppermute | solution.py:218
  110.1 10.7 %collective-permute-done.2.refs_2_ = bf16[256,896]{1,0:T(8,128)(2,1)S(1)} collective-permute-done((bf16[256,896]{1,0:T(8,128)(2,1)}, bf16[256,896]{1,0:T(8,128)(2,1)S(1)}, u32[]{:S(2)}, u32[]{:S(2)}) %collective-permute-start.2) | collective-permute-done | bytes 458784 | tf_op jit(solution)/shard_map/ppermute | solution.py:218
  120.8 0.0 collective-permute-done.3.refs_3_
  120.8 17.5 %all_to_all.26.hidden_ref = bf16[4,512,256]{2,1,0:T(8,128)(2,1)S(1)} all-to-all(bf16[4,512,256]{2,1,0:T(8,128)(2,1)S(1)} %shard_map.66), channel_id=1, replica_groups=mesh['x'=4,'zh'=8,'zl'=2,'c'=2,'y'=4] {'y'}, dimensions={0} | all-to-all | bytes 2097152 | tf_op jit(solution)/shard_map/all_to_all | solution.py:192
  138.3 2.3 %shard_map.67 = bf16[512,896]{1,0:T(8,128)(2,1)S(1)} custom-call(s32[1]{0:T(128)} %bitcast.member_ref, bf16[4,512,256]{2,1,0:T(8,128)(2,1)S(1)} %all_to_all.26.hidden_ref, bf16[256,896]{1,0:T(8,128)(2,1)S(1)} %get-tuple-element.17.refs_0_, bf16[256,896]{1,0:T(8,128)(2,1)S(1)} %collective-permute-done.1.refs_1_, ...), custom_call_target="tpu_custom_call" | custom-call | tf_op jit(solution)/shard_map/pallas_call | solution.py:147
  140.5 0.0 copy-start.4
  140.6 17.1 %all_to_all.27 = bf16[8,64,896]{2,1,0:T(8,128)(2,1)S(1)} all-to-all(bf16[8,64,896]{2,1,0:T(8,128)(2,1)S(1)} %bitcast.21), channel_id=1, replica_groups=mesh['x'=4,'zh'=8,'zl'=2,'c'=2,'y'=4] {'x','c'}, dimensions={0} | all-to-all | bytes 1835008 | tf_op jit(solution)/shard_map/all_to_all | solution.py:192
  157.7 0.0 copy-done.4
  157.7 0.7 shard_map.68
  158.4 1.9 collective-permute-start.4
  160.3 7.1 %collective-permute-done.4.received_ref = bf16[128,896]{1,0:T(8,128)(2,1)S(1)} collective-permute-done((bf16[128,896]{1,0:T(8,128)(2,1)S(1)}, bf16[128,896]{1,0:T(8,128)(2,1)S(1)}, u32[]{:S(2)}, u32[]{:S(2)}) %collective-permute-start.4) | collective-permute-done | bytes 229408 | tf_op jit(solution)/shard_map/ppermute | solution.py:231
  167.4 0.1 shard_map.69
  167.5 24.9 %all_to_all.28.shares_ref = bf16[32,4,896]{2,1,0:T(4,128)(2,1)S(1)} all-to-all(bf16[32,4,896]{2,1,0:T(4,128)(2,1)S(1)} %shard_map.69), channel_id=1, replica_groups=mesh['x'=4,'zh'=8,'zl'=2,'c'=2,'y'=4] {'zh','y'}, dimensions={0} | all-to-all | bytes 458752 | tf_op jit(solution)/shard_map/all_to_all | solution.py:192
  192.4 0.7 shard_map.70
Async XLA Ops:
  38.1 8.3 %collective-permute-start = (bf16[128,1024]{1,0:T(8,128)(2,1)S(1)}, bf16[128,1024]{1,0:T(8,128)(2,1)S(1)}, u32[]{:S(2)}, u32[]{:S(2)}) collective-permute-start(bf16[128,1024]{1,0:T(8,128)(2,1)S(1)} %bitcast.24), channel_id=1, source_target_pairs={{0,8},{8,0},{1,9},{9,1},{2,10},{10,2},{3,11},{11,3},{4,12},{12,4},... | collective-permute-start | bytes 786440 | tf_op jit(solution)/shard_map/ppermute | solution.py:210
  47.0 1.8 copy-start
  48.8 0.7 copy-start.3
  49.5 50.8 %all-to-all-start.1 = ((bf16[32,64,896]{2,1,0:T(8,128)(2,1)}), bf16[32,64,896]{2,1,0:T(8,128)(2,1)}, u32[]{:S(2)}, u32[]{:S(2)}) async-start(bf16[32,64,896]{2,1,0:T(8,128)(2,1)} %bitcast.19), calls=%async_computation.1 | async-start | bytes 7340032 | tf_op jit(solution)/shard_map/all_to_all | solution.py:192
  57.2 43.1 %copy-start.1 = (bf16[1,3584,256]{2,1,0:T(8,128)(2,1)S(1)}, bf16[1,3584,256]{2,1,0:T(8,128)(2,1)}, u32[]{:S(2)}) copy-start(bf16[1,3584,256]{2,1,0:T(8,128)(2,1)} %param.9) | copy-start | bytes 5505028
  60.0 50.1 %collective-permute-start.1 = (bf16[256,896]{1,0:T(8,128)(2,1)}, bf16[256,896]{1,0:T(8,128)(2,1)S(1)}, u32[]{:S(2)}, u32[]{:S(2)}) collective-permute-start(bf16[256,896]{1,0:T(8,128)(2,1)} %get-tuple-element.26), channel_id=1, source_target_pairs={{0,1},{1,2},{2,3},{3,0},{4,5},{5,6},{6,7},{7,4},{8,9},{9,10},{10,1... | collective-permute-start | bytes 1376264 | tf_op jit(solution)/shard_map/ppermute | solution.py:218
  63.3 57.4 %collective-permute-start.2 = (bf16[256,896]{1,0:T(8,128)(2,1)}, bf16[256,896]{1,0:T(8,128)(2,1)S(1)}, u32[]{:S(2)}, u32[]{:S(2)}) collective-permute-start(bf16[256,896]{1,0:T(8,128)(2,1)} %get-tuple-element.28), channel_id=1, source_target_pairs={{0,2},{1,3},{2,0},{3,1},{4,6},{5,7},{6,4},{7,5},{8,10},{9,11},{10,... | collective-permute-start | bytes 1376264 | tf_op jit(solution)/shard_map/ppermute | solution.py:218
  68.0 52.8 %collective-permute-start.3 = (bf16[256,896]{1,0:T(8,128)(2,1)}, bf16[256,896]{1,0:T(8,128)(2,1)}, u32[]{:S(2)}, u32[]{:S(2)}) collective-permute-start(bf16[256,896]{1,0:T(8,128)(2,1)} %get-tuple-element.25), channel_id=1, source_target_pairs={{0,3},{1,0},{2,1},{3,2},{4,7},{5,4},{6,5},{7,6},{8,11},{9,8},{10,9... | collective-permute-start | bytes 1376264 | tf_op jit(solution)/shard_map/ppermute | solution.py:218
  100.4 1.5 copy-start.2
  140.5 17.1 %copy-start.4 = (bf16[512,256]{1,0:T(8,128)(2,1)S(1)}, bf16[512,256]{1,0:T(8,128)(2,1)}, u32[]{:S(2)}) copy-start(bf16[512,256]{1,0:T(8,128)(2,1)} %copy-done.3) | copy-start | bytes 786436
  158.4 9.0 %collective-permute-start.4 = (bf16[128,896]{1,0:T(8,128)(2,1)S(1)}, bf16[128,896]{1,0:T(8,128)(2,1)S(1)}, u32[]{:S(2)}, u32[]{:S(2)}) collective-permute-start(bf16[128,896]{1,0:T(8,128)(2,1)S(1)} %get-tuple-element.24), channel_id=1, source_target_pairs={{0,8},{8,0},{1,9},{9,1},{2,10},{10,2},{3,11},{11,3},{4,12},{12,4},... | collective-permute-start | bytes 688136 | tf_op jit(solution)/shard_map/ppermute | solution.py:231

commit v5 on v4

--- a/solution.py
+++ b/solution.py
@@ -149,6 +149,33 @@
     )
 
 
+def cut_columns(down, member, n_dp, shifts):
+    units, width = down.shape
+    part = width // n_dp
+
+    def body(member_ref, down_hbm, *refs):
+        sems = refs[-1]
+        copies = []
+        for i, s in enumerate(shifts):
+            owner = lax.rem(member_ref[0] + s, n_dp)
+            start = pl.multiple_of(owner * part, 128)
+            copies.append(pltpu.make_async_copy(down_hbm.at[:, pl.ds(start, part)], refs[i], sems.at[i]))
+        for copy in copies:
+            copy.start()
+        for copy in copies:
+            copy.wait()
+
+    count = len(shifts)
+    return pl.pallas_call(
+        body,
+        out_shape=(jax.ShapeDtypeStruct((units, part), bf16),) * count,
+        in_specs=[SMEM, HBM],
+        out_specs=(HBM,) * count,
+        scratch_shapes=[pltpu.SemaphoreType.DMA((count,))],
+        name="cut_columns",
+    )(member, down)
+
+
 def mix_rows(received, high, low):
     _, part = received.shape
     half = high.shape[1] // 2
@@ -209,14 +236,11 @@
     near = exchange(packed, "zh").reshape(n_pair * rows, -1)
     far = lax.ppermute(near, "zl", [(0, 1), (1, 0)])
 
-    downs = []
-    for s in range(n_dp):
-        owner = member + s
-        owner = jnp.where(owner >= n_dp, owner - n_dp, owner)
-        piece = lax.dynamic_slice_in_dim(expert_down[0], owner * part, part, axis=1)
-        if s:
-            piece = lax.ppermute(piece, "y", [(i, (i + s) % n_dp) for i in range(n_dp)])
-        downs.append(piece)
+    early = cut_columns(expert_down[0], member_ref, n_dp, range(1, n_dp - 1))
+    late = cut_columns(expert_down[0], member_ref, n_dp, (0, n_dp - 1))
+    downs = [late[0], *early, late[1]]
+    for s in range(1, n_dp):
+        downs[s] = lax.ppermute(downs[s], "y", [(i, (i + s) % n_dp) for i in range(n_dp)])
 
     outgoing, high, low = route_rows(
         near, far, plane_ref, rows, top, n_x, n_z, n_c, n_dp

time: 195 us -> 210 us (1.077)
  Pallas kernels: 10.4 us -> 67.2 us
  waiting for transfers between devices: 57 us -> 18.3 us
  local copies, waits for them, and re-layouts: 6.77 us -> 4.01 us
    pallas_call x0 -> x2, Pallas kernels: none -> 57.8 us  [cut_columns(): pl.pallas_call(body, out_shape=(jax.ShapeDtypeStruct((units, part), bf16)...]
    all_to_all x1, waiting for transfers between devices: 29 us -> 0.01 us  [exchange(): return lax.all_to_all(value, axes, split_axis=0, concat_axis=0, tiled=True)]
    ppermute x3, waiting for transfers between devices: 14.5 us -> 4.83 us  [on_device(): lax.ppermute(downs[s], 'y', [(i, (i + s) % n_dp) for i in range(n_dp)])]
    dynamic_slice x1 -> x0, local copies, waits for them, and re-layouts: 2.76 us -> none  [on_device(): piece = lax.dynamic_slice_in_dim(expert_down[0], owner * part, part, axis=1)]
  transfers between devices with their start and end apart: 6 -> 6, of which waited for: 5 -> 3; matrix products, arithmetic and copies ran while one was open for 1% -> 0% of each run, Pallas kernels for 2% -> 30%
where the time goes in v5:
time: 210 us; the launch traced here: 209 us
  blocking collectives  96.2 us (46%)
  Pallas kernels  67.2 us (32%)
  starting transfers between devices  22.8 us (11%)
  waiting for transfers between devices  18.3 us (9%)
  local copies, waits for them, and re-layouts  4.01 us (2%)
    all_to_all x4, blocking collectives, exchange(): return lax.all_to_all(value, axes, split_axis=0, concat_axis=0, tiled=True)  96.2 us
    pallas_call x2, Pallas kernels, cut_columns(): pl.pallas_call(body, out_shape=(jax.ShapeDtypeStruct((units, part), bf16)...  57.8 us
    ppermute x3, starting transfers between devices, on_device(): lax.ppermute(downs[s], 'y', [(i, (i + s) % n_dp) for i in range(n_dp)])  11.4 us
    all_to_all x1, starting transfers between devices, exchange(): return lax.all_to_all(value, axes, split_axis=0, concat_axis=0, tiled=True)  7.62 us
    ppermute x1, waiting for transfers between devices, on_device(): sent = lax.ppermute(sent, 'zl', [(0, 1), (1, 0)])  7.11 us
    ppermute x1, waiting for transfers between devices, on_device(): far = lax.ppermute(near, 'zl', [(0, 1), (1, 0)])  6.33 us
    ppermute x3, waiting for transfers between devices, on_device(): lax.ppermute(downs[s], 'y', [(i, (i + s) % n_dp) for i in range(n_dp)])  4.83 us
    pallas_call x1, Pallas kernels, hidden_rows(): call(body, [((n_dp, slots, units), bf16)], [VMEM] * 3)  4.38 us
  transfers between devices with their start and end apart: 6, of which 3 were waited for; matrix products, arithmetic and copies ran while one was open for 0% of the time, Pallas kernels for 30%

profile of v5, /device:TPU:6, one launch (start us, length us, event | category | flops | bytes accessed | tf_op | source)
XLA Modules:
  0.0 208.7 jit_solution(17628726812683241008)
XLA Ops:
  0.0 1.6 shard_map.64
  1.6 36.5 %all_to_all.25 = bf16[8,16,1024]{2,1,0:T(8,128)(2,1)S(1)} all-to-all(bf16[8,16,1024]{2,1,0:T(8,128)(2,1)} %shard_map.64), channel_id=1, replica_groups=mesh['x'=4,'zh'=8,'zl'=2,'c'=2,'y'=4] {'zh'}, dimensions={0} | all-to-all | bytes 524288 | tf_op jit(solution)/shard_map/all_to_all | solution.py:219
  38.0 1.9 collective-permute-start
  40.0 6.3 %collective-permute-done.far_ref = bf16[128,1024]{1,0:T(8,128)(2,1)S(1)} collective-permute-done((bf16[128,1024]{1,0:T(8,128)(2,1)S(1)}, bf16[128,1024]{1,0:T(8,128)(2,1)S(1)}, u32[]{:S(2)}, u32[]{:S(2)}) %collective-permute-start) | collective-permute-done | bytes 262176 | tf_op jit(solution)/shard_map/ppermute | solution.py:237
  46.3 0.7 shard_map.65
  47.0 0.0 copy-start
  47.0 1.8 copy-done
  48.8 0.0 copy-start.4
  48.8 0.7 copy-done.4
  49.5 7.6 %all-to-all-start.1 = ((bf16[32,64,896]{2,1,0:T(8,128)(2,1)}), bf16[32,64,896]{2,1,0:T(8,128)(2,1)}, u32[]{:S(2)}, u32[]{:S(2)}) async-start(bf16[32,64,896]{2,1,0:T(8,128)(2,1)} %bitcast.12), calls=%async_computation.1 | async-start | bytes 7340032 | tf_op jit(solution)/shard_map/all_to_all | solution.py:219
  57.1 0.0 copy-start.1
  57.2 28.9 %cut_columns.3 = (bf16[256,896]{1,0:T(8,128)(2,1)}, bf16[256,896]{1,0:T(8,128)(2,1)}) custom-call(s32[1]{0:T(128)} %bitcast.member_ref, bf16[256,3584]{1,0:T(8,128)(2,1)} %bitcast.19), custom_call_target="tpu_custom_call" | custom-call | tf_op jit(solution)/shard_map/cut_columns/pallas_call | solution.py:169
  86.1 3.4 %collective-permute-start.1 = (bf16[256,896]{1,0:T(8,128)(2,1)}, bf16[256,896]{1,0:T(8,128)(2,1)S(1)}, u32[]{:S(2)}, u32[]{:S(2)}) collective-permute-start(bf16[256,896]{1,0:T(8,128)(2,1)} %get-tuple-element.21), channel_id=1, source_target_pairs={{0,1},{1,2},{2,3},{3,0},{4,5},{5,6},{6,7},{7,4},{8,9},{9,10},{10,1... | collective-permute-start | bytes 1376264 | tf_op jit(solution)/shard_map/ppermute | solution.py:243
  89.5 4.7 %collective-permute-start.2 = (bf16[256,896]{1,0:T(8,128)(2,1)}, bf16[256,896]{1,0:T(8,128)(2,1)S(1)}, u32[]{:S(2)}, u32[]{:S(2)}) collective-permute-start(bf16[256,896]{1,0:T(8,128)(2,1)} %get-tuple-element.22), channel_id=1, source_target_pairs={{0,2},{1,3},{2,0},{3,1},{4,6},{5,7},{6,4},{7,5},{8,10},{9,11},{10,... | collective-permute-start | bytes 1376264 | tf_op jit(solution)/shard_map/ppermute | solution.py:243
  94.1 28.9 %cut_columns.2 = (bf16[256,896]{1,0:T(8,128)(2,1)}, bf16[256,896]{1,0:T(8,128)(2,1)}) custom-call(s32[1]{0:T(128)} %bitcast.member_ref, bf16[256,3584]{1,0:T(8,128)(2,1)} %bitcast.20), custom_call_target="tpu_custom_call" | custom-call | tf_op jit(solution)/shard_map/cut_columns/pallas_call | solution.py:169
  123.1 3.3 %collective-permute-start.3 = (bf16[256,896]{1,0:T(8,128)(2,1)}, bf16[256,896]{1,0:T(8,128)(2,1)S(1)}, u32[]{:S(2)}, u32[]{:S(2)}) collective-permute-start(bf16[256,896]{1,0:T(8,128)(2,1)} %get-tuple-element.23), channel_id=1, source_target_pairs={{0,3},{1,0},{2,1},{3,2},{4,7},{5,4},{6,5},{7,6},{8,11},{9,8},{10,9... | collective-permute-start | bytes 1376264 | tf_op jit(solution)/shard_map/ppermute | solution.py:243
  126.4 0.0 all-to-all-done.1
  126.4 0.0 copy-done.1
  126.4 0.0 copy-start.2
  126.4 1.5 copy-done.2
  127.9 4.4 %shard_map.66 = bf16[4,512,256]{2,1,0:T(8,128)(2,1)S(1)} custom-call(bf16[4,512,896]{2,1,0:T(8,128)(2,1)} %bitcast.6.rows_ref, bf16[3584,256]{1,0:T(8,128)(2,1)S(1)} %bitcast.15, bf16[3584,256]{1,0:T(8,128)(2,1)S(1)} %bitcast.16), custom_call_target="tpu_custom_call" | custom-call | tf_op jit(solution)/shard_map/pallas_call | solution.py:132
  132.3 0.0 copy-start.3
  132.3 0.0 collective-permute-done.1.refs_1_
  132.3 0.0 collective-permute-done.2.refs_2_
  132.3 4.8 %collective-permute-done.3.refs_3_ = bf16[256,896]{1,0:T(8,128)(2,1)S(1)} collective-permute-done((bf16[256,896]{1,0:T(8,128)(2,1)}, bf16[256,896]{1,0:T(8,128)(2,1)S(1)}, u32[]{:S(2)}, u32[]{:S(2)}) %collective-permute-start.3) | collective-permute-done | bytes 458784 | tf_op jit(solution)/shard_map/ppermute | solution.py:243
  137.2 17.6 %all_to_all.26.hidden_ref = bf16[4,512,256]{2,1,0:T(8,128)(2,1)S(1)} all-to-all(bf16[4,512,256]{2,1,0:T(8,128)(2,1)S(1)} %shard_map.66), channel_id=1, replica_groups=mesh['x'=4,'zh'=8,'zl'=2,'c'=2,'y'=4] {'y'}, dimensions={0} | all-to-all | bytes 2097152 | tf_op jit(solution)/shard_map/all_to_all | solution.py:219
  154.8 0.0 copy-done.3
  154.8 1.2 shard_map.67
  156.1 0.0 copy-start.5
  156.1 17.2 %all_to_all.27 = bf16[8,64,896]{2,1,0:T(8,128)(2,1)S(1)} all-to-all(bf16[8,64,896]{2,1,0:T(8,128)(2,1)S(1)} %bitcast.14), channel_id=1, replica_groups=mesh['x'=4,'zh'=8,'zl'=2,'c'=2,'y'=4] {'x','c'}, dimensions={0} | all-to-all | bytes 1835008 | tf_op jit(solution)/shard_map/all_to_all | solution.py:219
  173.3 0.0 copy-done.5
  173.3 0.7 shard_map.68
  174.0 1.9 collective-permute-start.4
  176.0 7.1 %collective-permute-done.4.received_ref = bf16[128,896]{1,0:T(8,128)(2,1)S(1)} collective-permute-done((bf16[128,896]{1,0:T(8,128)(2,1)S(1)}, bf16[128,896]{1,0:T(8,128)(2,1)S(1)}, u32[]{:S(2)}, u32[]{:S(2)}) %collective-permute-start.4) | collective-permute-done | bytes 229408 | tf_op jit(solution)/shard_map/ppermute | solution.py:255
  183.1 0.1 shard_map.69
  183.1 24.9 %all_to_all.28.shares_ref = bf16[32,4,896]{2,1,0:T(4,128)(2,1)S(1)} all-to-all(bf16[32,4,896]{2,1,0:T(4,128)(2,1)S(1)} %shard_map.69), channel_id=1, replica_groups=mesh['x'=4,'zh'=8,'zl'=2,'c'=2,'y'=4] {'zh','y'}, dimensions={0} | all-to-all | bytes 458752 | tf_op jit(solution)/shard_map/all_to_all | solution.py:219
  208.1 0.7 shard_map.70
Async XLA Ops:
  38.0 8.3 %collective-permute-start = (bf16[128,1024]{1,0:T(8,128)(2,1)S(1)}, bf16[128,1024]{1,0:T(8,128)(2,1)S(1)}, u32[]{:S(2)}, u32[]{:S(2)}) collective-permute-start(bf16[128,1024]{1,0:T(8,128)(2,1)S(1)} %bitcast.17), channel_id=1, source_target_pairs={{0,8},{8,0},{1,9},{9,1},{2,10},{10,2},{3,11},{11,3},{4,12},{12,4},... | collective-permute-start | bytes 786440 | tf_op jit(solution)/shard_map/ppermute | solution.py:237
  47.0 1.8 copy-start
  48.8 0.7 copy-start.4
  49.5 76.9 %all-to-all-start.1 = ((bf16[32,64,896]{2,1,0:T(8,128)(2,1)}), bf16[32,64,896]{2,1,0:T(8,128)(2,1)}, u32[]{:S(2)}, u32[]{:S(2)}) async-start(bf16[32,64,896]{2,1,0:T(8,128)(2,1)} %bitcast.12), calls=%async_computation.1 | async-start | bytes 7340032 | tf_op jit(solution)/shard_map/all_to_all | solution.py:219
  57.1 69.3 %copy-start.1 = (bf16[1,3584,256]{2,1,0:T(8,128)(2,1)S(1)}, bf16[1,3584,256]{2,1,0:T(8,128)(2,1)}, u32[]{:S(2)}) copy-start(bf16[1,3584,256]{2,1,0:T(8,128)(2,1)} %param.9) | copy-start | bytes 5505028
  86.1 46.2 %collective-permute-start.1 = (bf16[256,896]{1,0:T(8,128)(2,1)}, bf16[256,896]{1,0:T(8,128)(2,1)S(1)}, u32[]{:S(2)}, u32[]{:S(2)}) collective-permute-start(bf16[256,896]{1,0:T(8,128)(2,1)} %get-tuple-element.21), channel_id=1, source_target_pairs={{0,1},{1,2},{2,3},{3,0},{4,5},{5,6},{6,7},{7,4},{8,9},{9,10},{10,1... | collective-permute-start | bytes 1376264 | tf_op jit(solution)/shard_map/ppermute | solution.py:243
  89.5 42.9 %collective-permute-start.2 = (bf16[256,896]{1,0:T(8,128)(2,1)}, bf16[256,896]{1,0:T(8,128)(2,1)S(1)}, u32[]{:S(2)}, u32[]{:S(2)}) collective-permute-start(bf16[256,896]{1,0:T(8,128)(2,1)} %get-tuple-element.22), channel_id=1, source_target_pairs={{0,2},{1,3},{2,0},{3,1},{4,6},{5,7},{6,4},{7,5},{8,10},{9,11},{10,... | collective-permute-start | bytes 1376264 | tf_op jit(solution)/shard_map/ppermute | solution.py:243
  123.1 14.1 %collective-permute-start.3 = (bf16[256,896]{1,0:T(8,128)(2,1)}, bf16[256,896]{1,0:T(8,128)(2,1)S(1)}, u32[]{:S(2)}, u32[]{:S(2)}) collective-permute-start(bf16[256,896]{1,0:T(8,128)(2,1)} %get-tuple-element.23), channel_id=1, source_target_pairs={{0,3},{1,0},{2,1},{3,2},{4,7},{5,4},{6,5},{7,6},{8,11},{9,8},{10,9... | collective-permute-start | bytes 1376264 | tf_op jit(solution)/shard_map/ppermute | solution.py:243
  126.4 1.5 copy-start.2
  132.3 22.5 %copy-start.3 = (bf16[256,896]{1,0:T(8,128)(2,1)S(1)}, bf16[256,896]{1,0:T(8,128)(2,1)}, u32[]{:S(2)}) copy-start(bf16[256,896]{1,0:T(8,128)(2,1)} %get-tuple-element.25.refs_0_) | copy-start | bytes 1376260
  156.1 17.2 %copy-start.5 = (bf16[512,256]{1,0:T(8,128)(2,1)S(1)}, bf16[512,256]{1,0:T(8,128)(2,1)}, u32[]{:S(2)}) copy-start(bf16[512,256]{1,0:T(8,128)(2,1)} %copy-done.4) | copy-start | bytes 786436
  174.0 9.0 %collective-permute-start.4 = (bf16[128,896]{1,0:T(8,128)(2,1)S(1)}, bf16[128,896]{1,0:T(8,128)(2,1)S(1)}, u32[]{:S(2)}, u32[]{:S(2)}) collective-permute-start(bf16[128,896]{1,0:T(8,128)(2,1)S(1)} %get-tuple-element.32), channel_id=1, source_target_pairs={{0,8},{8,0},{1,9},{9,1},{2,10},{10,2},{3,11},{11,3},{4,12},{12,4},... | collective-permute-start | bytes 688136 | tf_op jit(solution)/shard_map/ppermute | solution.py:255

commit v6 on v5

--- a/solution.py
+++ b/solution.py
@@ -166,14 +166,8 @@
             copy.wait()
 
     count = len(shifts)
-    return pl.pallas_call(
-        body,
-        out_shape=(jax.ShapeDtypeStruct((units, part), bf16),) * count,
-        in_specs=[SMEM, HBM],
-        out_specs=(HBM,) * count,
-        scratch_shapes=[pltpu.SemaphoreType.DMA((count,))],
-        name="cut_columns",
-    )(member, down)
+    outs = (((units, part), bf16),) * count
+    return call(body, outs, [SMEM, HBM], [pltpu.SemaphoreType.DMA((count,))], None)(member, down)
 
 
 def mix_rows(received, high, low):

time: 210 us -> 194 us (0.924)
  Pallas kernels: 67.2 us -> 13.8 us
  waiting for transfers between devices: 18.3 us -> 55.3 us
    pallas_call x2, Pallas kernels: 57.8 us -> 4.48 us  [cut_columns(): call(body, outs, [SMEM, HBM], [pltpu.SemaphoreType.DMA((count,))], None)]
    all_to_all x1, waiting for transfers between devices: 0.01 us -> 27.3 us  [exchange(): return lax.all_to_all(value, axes, split_axis=0, concat_axis=0, tiled=True)]
    ppermute x3, waiting for transfers between devices: 4.83 us -> 14.5 us  [on_device(): lax.ppermute(downs[s], 'y', [(i, (i + s) % n_dp) for i in range(n_dp)])]
  transfers between devices with their start and end apart: 6 -> 6, of which waited for: 3 -> 5; matrix products, arithmetic and copies ran while one was open for 0% -> 0% of each run, Pallas kernels for 30% -> 5%
where the time goes in v6:
time: 194 us; the launch traced here: 192 us
  blocking collectives  96 us (49%)
  waiting for transfers between devices  55.3 us (29%)
  starting transfers between devices  22.8 us (12%)
  Pallas kernels  13.8 us (7%)
  local copies, waits for them, and re-layouts  4.01 us (2%)
    all_to_all x4, blocking collectives, exchange(): return lax.all_to_all(value, axes, split_axis=0, concat_axis=0, tiled=True)  96 us
    all_to_all x1, waiting for transfers between devices, exchange(): return lax.all_to_all(value, axes, split_axis=0, concat_axis=0, tiled=True)  27.3 us
    ppermute x3, waiting for transfers between devices, on_device(): lax.ppermute(downs[s], 'y', [(i, (i + s) % n_dp) for i in range(n_dp)])  14.5 us
    ppermute x3, starting transfers between devices, on_device(): lax.ppermute(downs[s], 'y', [(i, (i + s) % n_dp) for i in range(n_dp)])  11.4 us
    all_to_all x1, starting transfers between devices, exchange(): return lax.all_to_all(value, axes, split_axis=0, concat_axis=0, tiled=True)  7.62 us
    ppermute x1, waiting for transfers between devices, on_device(): sent = lax.ppermute(sent, 'zl', [(0, 1), (1, 0)])  7.11 us
    ppermute x1, waiting for transfers between devices, on_device(): far = lax.ppermute(near, 'zl', [(0, 1), (1, 0)])  6.33 us
    pallas_call x2, Pallas kernels, cut_columns(): call(body, outs, [SMEM, HBM], [pltpu.SemaphoreType.DMA((count,))], None)  4.48 us
  transfers between devices with their start and end apart: 6, of which 5 were waited for; matrix products, arithmetic and copies ran while one was open for 0% of the time, Pallas kernels for 5%

profile of v6, /device:TPU:6, one launch (start us, length us, event | category | flops | bytes accessed | tf_op | source)
XLA Modules:
  0.0 192.0 jit_solution(4834227293011925883)
XLA Ops:
  0.0 1.6 shard_map.64
  1.6 36.5 %all_to_all.25 = bf16[8,16,1024]{2,1,0:T(8,128)(2,1)S(1)} all-to-all(bf16[8,16,1024]{2,1,0:T(8,128)(2,1)} %shard_map.64), channel_id=1, replica_groups=mesh['x'=4,'zh'=8,'zl'=2,'c'=2,'y'=4] {'zh'}, dimensions={0} | all-to-all | bytes 524288 | tf_op jit(solution)/shard_map/all_to_all | solution.py:213
  38.0 1.9 collective-permute-start
  40.0 6.3 %collective-permute-done.far_ref = bf16[128,1024]{1,0:T(8,128)(2,1)S(1)} collective-permute-done((bf16[128,1024]{1,0:T(8,128)(2,1)S(1)}, bf16[128,1024]{1,0:T(8,128)(2,1)S(1)}, u32[]{:S(2)}, u32[]{:S(2)}) %collective-permute-start) | collective-permute-done | bytes 262176 | tf_op jit(solution)/shard_map/ppermute | solution.py:231
  46.3 0.7 shard_map.65
  47.0 0.0 copy-start
  47.0 1.8 copy-done
  48.8 0.0 copy-start.4
  48.8 0.7 copy-done.4
  49.5 7.6 %all-to-all-start.1 = ((bf16[32,64,896]{2,1,0:T(8,128)(2,1)}), bf16[32,64,896]{2,1,0:T(8,128)(2,1)}, u32[]{:S(2)}, u32[]{:S(2)}) async-start(bf16[32,64,896]{2,1,0:T(8,128)(2,1)} %bitcast.12), calls=%async_computation.1 | async-start | bytes 7340032 | tf_op jit(solution)/shard_map/all_to_all | solution.py:213
  57.1 0.0 copy-start.1
  57.2 2.3 %shard_map.68 = (bf16[256,896]{1,0:T(8,128)(2,1)}, bf16[256,896]{1,0:T(8,128)(2,1)}) custom-call(s32[1]{0:T(128)} %bitcast.member_ref, bf16[256,3584]{1,0:T(8,128)(2,1)} %bitcast.19), custom_call_target="tpu_custom_call" | custom-call | tf_op jit(solution)/shard_map/pallas_call | solution.py:170
  59.5 3.4 %collective-permute-start.1 = (bf16[256,896]{1,0:T(8,128)(2,1)}, bf16[256,896]{1,0:T(8,128)(2,1)S(1)}, u32[]{:S(2)}, u32[]{:S(2)}) collective-permute-start(bf16[256,896]{1,0:T(8,128)(2,1)} %get-tuple-element.21), channel_id=1, source_target_pairs={{0,1},{1,2},{2,3},{3,0},{4,5},{5,6},{6,7},{7,4},{8,9},{9,10},{10,1... | collective-permute-start | bytes 1376264 | tf_op jit(solution)/shard_map/ppermute | solution.py:237
  62.9 4.7 %collective-permute-start.2 = (bf16[256,896]{1,0:T(8,128)(2,1)}, bf16[256,896]{1,0:T(8,128)(2,1)S(1)}, u32[]{:S(2)}, u32[]{:S(2)}) collective-permute-start(bf16[256,896]{1,0:T(8,128)(2,1)} %get-tuple-element.22), channel_id=1, source_target_pairs={{0,2},{1,3},{2,0},{3,1},{4,6},{5,7},{6,4},{7,5},{8,10},{9,11},{10,... | collective-permute-start | bytes 1376264 | tf_op jit(solution)/shard_map/ppermute | solution.py:237
  67.5 2.2 %shard_map.67 = (bf16[256,896]{1,0:T(8,128)(2,1)}, bf16[256,896]{1,0:T(8,128)(2,1)}) custom-call(s32[1]{0:T(128)} %bitcast.member_ref, bf16[256,3584]{1,0:T(8,128)(2,1)} %bitcast.20), custom_call_target="tpu_custom_call" | custom-call | tf_op jit(solution)/shard_map/pallas_call | solution.py:170
  69.7 3.3 %collective-permute-start.3 = (bf16[256,896]{1,0:T(8,128)(2,1)}, bf16[256,896]{1,0:T(8,128)(2,1)S(1)}, u32[]{:S(2)}, u32[]{:S(2)}) collective-permute-start(bf16[256,896]{1,0:T(8,128)(2,1)} %get-tuple-element.23), channel_id=1, source_target_pairs={{0,3},{1,0},{2,1},{3,2},{4,7},{5,4},{6,5},{7,6},{8,11},{9,8},{10,9... | collective-permute-start | bytes 1376264 | tf_op jit(solution)/shard_map/ppermute | solution.py:237
  73.0 27.3 %all-to-all-done.1 = bf16[32,64,896]{2,1,0:T(8,128)(2,1)} async-done(((bf16[32,64,896]{2,1,0:T(8,128)(2,1)}), bf16[32,64,896]{2,1,0:T(8,128)(2,1)}, u32[]{:S(2)}, u32[]{:S(2)}) %all-to-all-start.1) | async-done | bytes 3670048 | tf_op jit(solution)/shard_map/all_to_all | solution.py:213
  100.3 0.0 copy-done.1
  100.3 0.0 copy-start.2
  100.3 1.5 copy-done.2
  101.8 4.4 %shard_map.66 = bf16[4,512,256]{2,1,0:T(8,128)(2,1)S(1)} custom-call(bf16[4,512,896]{2,1,0:T(8,128)(2,1)} %bitcast.6.rows_ref, bf16[3584,256]{1,0:T(8,128)(2,1)S(1)} %bitcast.15, bf16[3584,256]{1,0:T(8,128)(2,1)S(1)} %bitcast.16), custom_call_target="tpu_custom_call" | custom-call | tf_op jit(solution)/shard_map/pallas_call | solution.py:132
  106.2 0.0 copy-start.3
  106.2 3.9 %collective-permute-done.1.refs_1_ = bf16[256,896]{1,0:T(8,128)(2,1)S(1)} collective-permute-done((bf16[256,896]{1,0:T(8,128)(2,1)}, bf16[256,896]{1,0:T(8,128)(2,1)S(1)}, u32[]{:S(2)}, u32[]{:S(2)}) %collective-permute-start.1) | collective-permute-done | bytes 458784 | tf_op jit(solution)/shard_map/ppermute | solution.py:237
  110.1 10.7 %collective-permute-done.2.refs_2_ = bf16[256,896]{1,0:T(8,128)(2,1)S(1)} collective-permute-done((bf16[256,896]{1,0:T(8,128)(2,1)}, bf16[256,896]{1,0:T(8,128)(2,1)S(1)}, u32[]{:S(2)}, u32[]{:S(2)}) %collective-permute-start.2) | collective-permute-done | bytes 458784 | tf_op jit(solution)/shard_map/ppermute | solution.py:237
  120.7 0.0 collective-permute-done.3.refs_3_
  120.8 17.5 %all_to_all.26.hidden_ref = bf16[4,512,256]{2,1,0:T(8,128)(2,1)S(1)} all-to-all(bf16[4,512,256]{2,1,0:T(8,128)(2,1)S(1)} %shard_map.66), channel_id=1, replica_groups=mesh['x'=4,'zh'=8,'zl'=2,'c'=2,'y'=4] {'y'}, dimensions={0} | all-to-all | bytes 2097152 | tf_op jit(solution)/shard_map/all_to_all | solution.py:213
  138.3 0.0 copy-done.3
  138.3 1.2 shard_map.69
  139.5 0.0 copy-start.5
  139.5 17.1 %all_to_all.27 = bf16[8,64,896]{2,1,0:T(8,128)(2,1)S(1)} all-to-all(bf16[8,64,896]{2,1,0:T(8,128)(2,1)S(1)} %bitcast.14), channel_id=1, replica_groups=mesh['x'=4,'zh'=8,'zl'=2,'c'=2,'y'=4] {'x','c'}, dimensions={0} | all-to-all | bytes 1835008 | tf_op jit(solution)/shard_map/all_to_all | solution.py:213
  156.6 0.0 copy-done.5
  156.6 0.7 shard_map.70
  157.4 1.9 %collective-permute-start.4 = (bf16[128,896]{1,0:T(8,128)(2,1)S(1)}, bf16[128,896]{1,0:T(8,128)(2,1)S(1)}, u32[]{:S(2)}, u32[]{:S(2)}) collective-permute-start(bf16[128,896]{1,0:T(8,128)(2,1)S(1)} %get-tuple-element.32), channel_id=1, source_target_pairs={{0,8},{8,0},{1,9},{9,1},{2,10},{10,2},{3,11},{11,3},{4,12},{12,4},... | collective-permute-start | bytes 688136 | tf_op jit(solution)/shard_map/ppermute | solution.py:249
  159.3 7.1 %collective-permute-done.4.received_ref = bf16[128,896]{1,0:T(8,128)(2,1)S(1)} collective-permute-done((bf16[128,896]{1,0:T(8,128)(2,1)S(1)}, bf16[128,896]{1,0:T(8,128)(2,1)S(1)}, u32[]{:S(2)}, u32[]{:S(2)}) %collective-permute-start.4) | collective-permute-done | bytes 229408 | tf_op jit(solution)/shard_map/ppermute | solution.py:249
  166.4 0.1 shard_map.71
  166.5 24.9 %all_to_all.28.shares_ref = bf16[32,4,896]{2,1,0:T(4,128)(2,1)S(1)} all-to-all(bf16[32,4,896]{2,1,0:T(4,128)(2,1)S(1)} %shard_map.71), channel_id=1, replica_groups=mesh['x'=4,'zh'=8,'zl'=2,'c'=2,'y'=4] {'zh','y'}, dimensions={0} | all-to-all | bytes 458752 | tf_op jit(solution)/shard_map/all_to_all | solution.py:213
  191.4 0.7 shard_map.72
Async XLA Ops:
  38.0 8.3 %collective-permute-start = (bf16[128,1024]{1,0:T(8,128)(2,1)S(1)}, bf16[128,1024]{1,0:T(8,128)(2,1)S(1)}, u32[]{:S(2)}, u32[]{:S(2)}) collective-permute-start(bf16[128,1024]{1,0:T(8,128)(2,1)S(1)} %bitcast.17), channel_id=1, source_target_pairs={{0,8},{8,0},{1,9},{9,1},{2,10},{10,2},{3,11},{11,3},{4,12},{12,4},... | collective-permute-start | bytes 786440 | tf_op jit(solution)/shard_map/ppermute | solution.py:231
  47.0 1.8 copy-start
  48.8 0.7 copy-start.4
  49.5 50.8 %all-to-all-start.1 = ((bf16[32,64,896]{2,1,0:T(8,128)(2,1)}), bf16[32,64,896]{2,1,0:T(8,128)(2,1)}, u32[]{:S(2)}, u32[]{:S(2)}) async-start(bf16[32,64,896]{2,1,0:T(8,128)(2,1)} %bitcast.12), calls=%async_computation.1 | async-start | bytes 7340032 | tf_op jit(solution)/shard_map/all_to_all | solution.py:213
  57.1 43.2 %copy-start.1 = (bf16[1,3584,256]{2,1,0:T(8,128)(2,1)S(1)}, bf16[1,3584,256]{2,1,0:T(8,128)(2,1)}, u32[]{:S(2)}) copy-start(bf16[1,3584,256]{2,1,0:T(8,128)(2,1)} %param.9) | copy-start | bytes 5505028
  59.5 50.6 %collective-permute-start.1 = (bf16[256,896]{1,0:T(8,128)(2,1)}, bf16[256,896]{1,0:T(8,128)(2,1)S(1)}, u32[]{:S(2)}, u32[]{:S(2)}) collective-permute-start(bf16[256,896]{1,0:T(8,128)(2,1)} %get-tuple-element.21), channel_id=1, source_target_pairs={{0,1},{1,2},{2,3},{3,0},{4,5},{5,6},{6,7},{7,4},{8,9},{9,10},{10,1... | collective-permute-start | bytes 1376264 | tf_op jit(solution)/shard_map/ppermute | solution.py:237
  62.9 57.9 %collective-permute-start.2 = (bf16[256,896]{1,0:T(8,128)(2,1)}, bf16[256,896]{1,0:T(8,128)(2,1)S(1)}, u32[]{:S(2)}, u32[]{:S(2)}) collective-permute-start(bf16[256,896]{1,0:T(8,128)(2,1)} %get-tuple-element.22), channel_id=1, source_target_pairs={{0,2},{1,3},{2,0},{3,1},{4,6},{5,7},{6,4},{7,5},{8,10},{9,11},{10,... | collective-permute-start | bytes 1376264 | tf_op jit(solution)/shard_map/ppermute | solution.py:237
  69.7 51.0 %collective-permute-start.3 = (bf16[256,896]{1,0:T(8,128)(2,1)}, bf16[256,896]{1,0:T(8,128)(2,1)S(1)}, u32[]{:S(2)}, u32[]{:S(2)}) collective-permute-start(bf16[256,896]{1,0:T(8,128)(2,1)} %get-tuple-element.23), channel_id=1, source_target_pairs={{0,3},{1,0},{2,1},{3,2},{4,7},{5,4},{6,5},{7,6},{8,11},{9,8},{10,9... | collective-permute-start | bytes 1376264 | tf_op jit(solution)/shard_map/ppermute | solution.py:237
  100.3 1.5 copy-start.2
  106.2 32.0 %copy-start.3 = (bf16[256,896]{1,0:T(8,128)(2,1)S(1)}, bf16[256,896]{1,0:T(8,128)(2,1)}, u32[]{:S(2)}) copy-start(bf16[256,896]{1,0:T(8,128)(2,1)} %get-tuple-element.25.refs_0_) | copy-start | bytes 1376260
  139.5 17.1 %copy-start.5 = (bf16[512,256]{1,0:T(8,128)(2,1)S(1)}, bf16[512,256]{1,0:T(8,128)(2,1)}, u32[]{:S(2)}) copy-start(bf16[512,256]{1,0:T(8,128)(2,1)} %copy-done.4) | copy-start | bytes 786436
  157.4 9.0 %collective-permute-start.4 = (bf16[128,896]{1,0:T(8,128)(2,1)S(1)}, bf16[128,896]{1,0:T(8,128)(2,1)S(1)}, u32[]{:S(2)}, u32[]{:S(2)}) collective-permute-start(bf16[128,896]{1,0:T(8,128)(2,1)S(1)} %get-tuple-element.32), channel_id=1, source_target_pairs={{0,8},{8,0},{1,9},{9,1},{2,10},{10,2},{3,11},{11,3},{4,12},{12,4},... | collective-permute-start | bytes 688136 | tf_op jit(solution)/shard_map/ppermute | solution.py:249

commit v7 on v6

--- a/solution.py
+++ b/solution.py
@@ -68,17 +68,17 @@
     return call(body, outs, [SMEM, HBM, HBM, HBM], scratch, None)(member, tokens, expert_ids.T, route_logits.T)
 
 
-def route_rows(near, far, plane, rows, top, n_x, n_z, n_c, n_dp):
-    total = 2 * near.shape[0]
-    part = near.shape[1] - SIDE
-    experts = n_x * n_c
-    held = n_z * SLOTS
+def route_rows(gathered, pair, rows, top, n_x, n_pair, n_c, n_dp):
+    total = gathered.shape[0]
+    part = gathered.shape[1] - SIDE
+    experts = n_x * 2 * n_c
+    held = n_pair * SLOTS
     pad = max(16, experts)
 
-    def body(plane_ref, near_ref, far_ref, out_ref, high_ref, low_ref, pick_ref):
-        side = jnp.concatenate([near_ref[:, part:], far_ref[:, part:]], axis=0).astype(f32).T
+    def body(pair_ref, gathered_ref, out_ref, high_ref, low_ref, pick_ref):
+        side = gathered_ref[:, part:].astype(f32).T
         line = lax.broadcasted_iota(i32, (pad, 1), 0)
-        name = ((line // n_c) * n_z + plane_ref[0]) * n_c + line % n_c
+        name = ((line // (2 * n_c)) * n_pair + pair_ref[0]) * (2 * n_c) + line % (2 * n_c)
         name = jnp.where(line < experts, name, -1).astype(f32)
         named = jnp.zeros((pad, total), f32)
         high = jnp.zeros((pad, total), f32)
@@ -102,15 +102,14 @@
             pick_ref[at, :] = jnp.where(hit, 1.0, 0.0).astype(bf16)
             high_ref[at, :] = jnp.where(hit, high[j : j + 1, :], 0.0).astype(bf16)
             low_ref[at, :] = jnp.where(hit, low[j : j + 1, :], 0.0).astype(bf16)
-        own = jnp.concatenate([near_ref[:, :part], far_ref[:, :part]], axis=0)
-        sent = jnp.dot(pick_ref[...], own, preferred_element_type=f32).astype(bf16)
+        sent = jnp.dot(pick_ref[...], gathered_ref[:, :part], preferred_element_type=f32).astype(bf16)
         for d in range(n_dp):
             out_ref[d] = sent
 
     slots = experts * held
     outs = (((n_dp, slots, part), bf16),) + (((slots, total), bf16),) * 2
     scratch = [pltpu.VMEM((slots, total), bf16)]
-    return call(body, outs, [SMEM, VMEM, VMEM], scratch)(plane, near, far)
+    return call(body, outs, [SMEM, VMEM], scratch)(pair, gathered)
 
 
 def hidden_rows(received, w_gate, w_up):
@@ -170,30 +169,19 @@
     return call(body, outs, [SMEM, HBM], [pltpu.SemaphoreType.DMA((count,))], None)(member, down)
 
 
-def mix_rows(received, high, low):
+def mix_rows(received, high, low, share):
     _, part = received.shape
-    half = high.shape[1] // 2
-
-    def body(rows_ref, high_ref, low_ref, kept_ref, sent_ref):
+    total = high.shape[1]
+
+    def body(rows_ref, high_ref, low_ref, out_ref):
         rows = rows_ref[...]
         dims = (((0,), (0,)), ((), ()))
         mixed = lax.dot_general(high_ref[...], rows, dims, preferred_element_type=f32)
         mixed = mixed + lax.dot_general(low_ref[...], rows, dims, preferred_element_type=f32)
-        kept_ref[...] = mixed[:half, :]
-        sent_ref[...] = mixed[half:, :].astype(bf16)
-
-    return call(body, (((half, part), f32), ((half, part), bf16)), [VMEM] * 3)(received, high, low)
-
-
-def add_pair(kept, received, share):
-    total, part = kept.shape
-
-    def body(kept_ref, received_ref, out_ref):
-        both = kept_ref[...] + received_ref[...].astype(f32)
         for i in range(total // share):
-            out_ref[i] = both[i * share : (i + 1) * share, :].astype(bf16)
-
-    return call(body, [((total // share, share, part), bf16)], [VMEM] * 2)(kept, received)
+            out_ref[i] = mixed[i * share : (i + 1) * share, :].astype(bf16)
+
+    return call(body, [((total // share, share, part), bf16)], [VMEM] * 3)(received, high, low)
 
 
 def sum_rows(shares, n_dp):
@@ -217,18 +205,17 @@
     rows, width = tokens.shape
     top = expert_ids.shape[1]
     n_x, n_pair, n_c, n_dp = (lax.axis_size(a) for a in ("x", "zh", "c", "y"))
-    n_z = 2 * n_pair
     part = width // n_dp
-    held = n_z * SLOTS
-    slots = n_x * n_c * held
+    experts = n_x * 2 * n_c
+    held = n_pair * SLOTS
+    slots = experts * held
     member = lax.axis_index("y").astype(i32)
     member_ref = member.reshape(1)
-    plane_ref = (2 * lax.axis_index("zh") + lax.axis_index("zl")).astype(i32).reshape(1)
+    pair_ref = lax.axis_index("zh").astype(i32).reshape(1)
     w_gate, w_up = expert_gate[0], expert_up[0]
 
     packed = pack_rows(tokens, expert_ids, route_logits, member_ref, n_dp, n_pair)
-    near = exchange(packed, "zh").reshape(n_pair * rows, -1)
-    far = lax.ppermute(near, "zl", [(0, 1), (1, 0)])
+    gathered = exchange(packed, "zh").reshape(n_pair * rows, -1)
 
     early = cut_columns(expert_down[0], member_ref, n_dp, range(1, n_dp - 1))
     late = cut_columns(expert_down[0], member_ref, n_dp, (0, n_dp - 1))
@@ -236,18 +223,15 @@
     for s in range(1, n_dp):
         downs[s] = lax.ppermute(downs[s], "y", [(i, (i + s) % n_dp) for i in range(n_dp)])
 
-    outgoing, high, low = route_rows(
-        near, far, plane_ref, rows, top, n_x, n_z, n_c, n_dp
-    )
-    arrived = exchange(outgoing.reshape(n_dp * n_x * n_c, held, part), ("y", "x", "c"))
+    outgoing, high, low = route_rows(gathered, pair_ref, rows, top, n_x, n_pair, n_c, n_dp)
+    arrived = exchange(outgoing.reshape(n_dp * experts, held, part), ("y", "x", "zl", "c"))
     hidden = hidden_rows(arrived.reshape(n_dp, slots, part), w_gate, w_up)
     hidden, downs = lax.optimization_barrier((hidden, downs))
     hidden = exchange(hidden, "y")
     results = output_rows(hidden, downs, member_ref)
-    back = exchange(results.reshape(n_x * n_c, held, part), ("x", "c"))
-    kept, sent = mix_rows(back.reshape(slots, part), high, low)
-    sent = lax.ppermute(sent, "zl", [(0, 1), (1, 0)])
-    shares = exchange(add_pair(kept, sent, rows // n_dp), ("zh", "y"))
+    back = exchange(results.reshape(experts, held, part), ("x", "zl", "c"))
+    mixed = mix_rows(back.reshape(slots, part), high, low, rows // n_dp)
+    shares = exchange(mixed, ("zh", "y"))
     return sum_rows(shares, n_dp)
 
 

time: 194 us -> 179 us (0.923)
  blocking collectives: 96 us -> 61.3 us
  starting transfers between devices: 22.8 us -> 34.7 us
  waiting for transfers between devices: 55.3 us -> 63 us
    all_to_all x4 -> x3, blocking collectives: 96 us -> 61.3 us  [exchange(): return lax.all_to_all(value, axes, split_axis=0, concat_axis=0, tiled=True)]
    all_to_all x1 -> x2, waiting for transfers between devices: 27.3 us -> 49.4 us  [exchange(): return lax.all_to_all(value, axes, split_axis=0, concat_axis=0, tiled=True)]
    all_to_all x1 -> x2, starting transfers between devices: 7.62 us -> 23.2 us  [exchange(): return lax.all_to_all(value, axes, split_axis=0, concat_axis=0, tiled=True)]
    ppermute x2 -> x0, waiting for transfers between devices: 13.4 us -> none  [the longest x1 7.11 us: on_device(): sent = lax.ppermute(sent, 'zl', [(0, 1), (1, 0)])]
    ppermute x2 -> x0, starting transfers between devices: 3.84 us -> none  [the longest x1 1.93 us: on_device(): sent = lax.ppermute(sent, 'zl', [(0, 1), (1, 0)])]
    unnamed x12 -> x8, local copies, waits for them, and re-layouts: 4.01 us -> 3.34 us
  transfers between devices with their start and end apart: 6 -> 5, of which waited for: 5 -> 4; matrix products, arithmetic and copies ran while one was open for 0% -> 0% of each run, Pallas kernels for 5% -> 5%
where the time goes in v7:
time: 179 us; the launch traced here: 176 us
  waiting for transfers between devices  63 us (35%)
  blocking collectives  61.3 us (34%)
  starting transfers between devices  34.7 us (19%)
  Pallas kernels  13.5 us (8%)
  local copies, waits for them, and re-layouts  3.34 us (2%)
    all_to_all x3, blocking collectives, exchange(): return lax.all_to_all(value, axes, split_axis=0, concat_axis=0, tiled=True)  61.3 us
    all_to_all x2, waiting for transfers between devices, exchange(): return lax.all_to_all(value, axes, split_axis=0, concat_axis=0, tiled=True)  49.4 us
    all_to_all x2, starting transfers between devices, exchange(): return lax.all_to_all(value, axes, split_axis=0, concat_axis=0, tiled=True)  23.2 us
    ppermute x3, waiting for transfers between devices, on_device(): lax.ppermute(downs[s], 'y', [(i, (i + s) % n_dp) for i in range(n_dp)])  13.6 us
    ppermute x3, starting transfers between devices, on_device(): lax.ppermute(downs[s], 'y', [(i, (i + s) % n_dp) for i in range(n_dp)])  11.5 us
    pallas_call x2, Pallas kernels, cut_columns(): call(body, outs, [SMEM, HBM], [pltpu.SemaphoreType.DMA((count,))], None)  4.47 us
    pallas_call x1, Pallas kernels, hidden_rows(): call(body, [((n_dp, slots, units), bf16)], [VMEM] * 3)  4.38 us
  transfers between devices with their start and end apart: 5, of which 4 were waited for; matrix products, arithmetic and copies ran while one was open for 0% of the time, Pallas kernels for 5%

profile of v7, /device:TPU:6, one launch (start us, length us, event | category | flops | bytes accessed | tf_op | source)
XLA Modules:
  0.0 176.0 jit_solution(4870983163167133061)
XLA Ops:
  0.0 1.6 shard_map.64
  1.6 15.1 %all-to-all-start = ((bf16[8,16,1024]{2,1,0:T(8,128)(2,1)}), bf16[8,16,1024]{2,1,0:T(8,128)(2,1)S(1)}, u32[]{:S(2)}, u32[]{:S(2)}) async-start(bf16[8,16,1024]{2,1,0:T(8,128)(2,1)} %shard_map.64), calls=%async_computation | async-start | bytes 524288 | tf_op jit(solution)/shard_map/all_to_all | solution.py:201
  16.7 21.4 %all-to-all-done = bf16[8,16,1024]{2,1,0:T(8,128)(2,1)S(1)} async-done(((bf16[8,16,1024]{2,1,0:T(8,128)(2,1)}), bf16[8,16,1024]{2,1,0:T(8,128)(2,1)S(1)}, u32[]{:S(2)}, u32[]{:S(2)}) %all-to-all-start) | async-done | bytes 262176 | tf_op jit(solution)/shard_map/all_to_all | solution.py:201
  38.1 0.7 shard_map.65
  38.8 0.0 copy-start
  38.8 1.8 %copy-done = bf16[4,512,896]{2,1,0:T(8,128)(2,1)} copy-done((bf16[4,512,896]{2,1,0:T(8,128)(2,1)}, bf16[4,512,896]{2,1,0:T(8,128)(2,1)S(1)}, u32[]{:S(2)}) %copy-start) | copy-done | bytes 3670040
  40.6 8.1 %all-to-all-start.1 = ((bf16[64,32,896]{2,1,0:T(8,128)(2,1)}), bf16[64,32,896]{2,1,0:T(8,128)(2,1)}, u32[]{:S(2)}, u32[]{:S(2)}) async-start(bf16[64,32,896]{2,1,0:T(8,128)(2,1)} %bitcast.12), calls=%async_computation.1 | async-start | bytes 7340032 | tf_op jit(solution)/shard_map/all_to_all | solution.py:201
  48.7 0.0 copy-start.1
  48.7 2.3 %shard_map.68 = (bf16[256,896]{1,0:T(8,128)(2,1)}, bf16[256,896]{1,0:T(8,128)(2,1)}) custom-call(s32[1]{0:T(128)} %bitcast.member_ref, bf16[256,3584]{1,0:T(8,128)(2,1)} %bitcast.18), custom_call_target="tpu_custom_call" | custom-call | tf_op jit(solution)/shard_map/pallas_call | solution.py:169
  51.1 3.4 %collective-permute-start = (bf16[256,896]{1,0:T(8,128)(2,1)}, bf16[256,896]{1,0:T(8,128)(2,1)S(1)}, u32[]{:S(2)}, u32[]{:S(2)}) collective-permute-start(bf16[256,896]{1,0:T(8,128)(2,1)} %get-tuple-element.19), channel_id=1, source_target_pairs={{0,1},{1,2},{2,3},{3,0},{4,5},{5,6},{6,7},{7,4},{8,9},{9,10},{10,1... | collective-permute-start | bytes 1376264 | tf_op jit(solution)/shard_map/ppermute | solution.py:224
  54.5 4.8 %collective-permute-start.1 = (bf16[256,896]{1,0:T(8,128)(2,1)}, bf16[256,896]{1,0:T(8,128)(2,1)S(1)}, u32[]{:S(2)}, u32[]{:S(2)}) collective-permute-start(bf16[256,896]{1,0:T(8,128)(2,1)} %get-tuple-element.20), channel_id=1, source_target_pairs={{0,2},{1,3},{2,0},{3,1},{4,6},{5,7},{6,4},{7,5},{8,10},{9,11},{10,... | collective-permute-start | bytes 1376264 | tf_op jit(solution)/shard_map/ppermute | solution.py:224
  59.3 2.2 %shard_map.67 = (bf16[256,896]{1,0:T(8,128)(2,1)}, bf16[256,896]{1,0:T(8,128)(2,1)}) custom-call(s32[1]{0:T(128)} %bitcast.member_ref, bf16[256,3584]{1,0:T(8,128)(2,1)} %bitcast.19), custom_call_target="tpu_custom_call" | custom-call | tf_op jit(solution)/shard_map/pallas_call | solution.py:169
  61.5 3.3 %collective-permute-start.2 = (bf16[256,896]{1,0:T(8,128)(2,1)}, bf16[256,896]{1,0:T(8,128)(2,1)S(1)}, u32[]{:S(2)}, u32[]{:S(2)}) collective-permute-start(bf16[256,896]{1,0:T(8,128)(2,1)} %get-tuple-element.21), channel_id=1, source_target_pairs={{0,3},{1,0},{2,1},{3,2},{4,7},{5,4},{6,5},{7,6},{8,11},{9,8},{10,9... | collective-permute-start | bytes 1376264 | tf_op jit(solution)/shard_map/ppermute | solution.py:224
  64.8 28.0 %all-to-all-done.1 = bf16[64,32,896]{2,1,0:T(8,128)(2,1)} async-done(((bf16[64,32,896]{2,1,0:T(8,128)(2,1)}), bf16[64,32,896]{2,1,0:T(8,128)(2,1)}, u32[]{:S(2)}, u32[]{:S(2)}) %all-to-all-start.1) | async-done | bytes 3670048 | tf_op jit(solution)/shard_map/all_to_all | solution.py:201
  92.8 0.0 copy-done.1
  92.8 0.0 copy-start.2
  92.8 1.5 copy-done.2
  94.3 4.4 %shard_map.66 = bf16[4,512,256]{2,1,0:T(8,128)(2,1)S(1)} custom-call(bf16[4,512,896]{2,1,0:T(8,128)(2,1)} %bitcast.6.rows_ref, bf16[3584,256]{1,0:T(8,128)(2,1)S(1)} %bitcast.15, bf16[3584,256]{1,0:T(8,128)(2,1)S(1)} %bitcast.16), custom_call_target="tpu_custom_call" | custom-call | tf_op jit(solution)/shard_map/pallas_call | solution.py:131
  98.7 0.0 copy-start.3
  98.7 3.1 %collective-permute-done.refs_1_ = bf16[256,896]{1,0:T(8,128)(2,1)S(1)} collective-permute-done((bf16[256,896]{1,0:T(8,128)(2,1)}, bf16[256,896]{1,0:T(8,128)(2,1)S(1)}, u32[]{:S(2)}, u32[]{:S(2)}) %collective-permute-start) | collective-permute-done | bytes 458784 | tf_op jit(solution)/shard_map/ppermute | solution.py:224
  101.8 10.5 %collective-permute-done.1.refs_2_ = bf16[256,896]{1,0:T(8,128)(2,1)S(1)} collective-permute-done((bf16[256,896]{1,0:T(8,128)(2,1)}, bf16[256,896]{1,0:T(8,128)(2,1)S(1)}, u32[]{:S(2)}, u32[]{:S(2)}) %collective-permute-start.1) | collective-permute-done | bytes 458784 | tf_op jit(solution)/shard_map/ppermute | solution.py:224
  112.3 0.0 collective-permute-done.2.refs_3_
  112.3 17.8 %all_to_all.25.hidden_ref = bf16[4,512,256]{2,1,0:T(8,128)(2,1)S(1)} all-to-all(bf16[4,512,256]{2,1,0:T(8,128)(2,1)S(1)} %shard_map.66), channel_id=1, replica_groups=mesh['x'=4,'zh'=8,'zl'=2,'c'=2,'y'=4] {'y'}, dimensions={0} | all-to-all | bytes 2097152 | tf_op jit(solution)/shard_map/all_to_all | solution.py:201
  130.1 0.0 copy-done.3
  130.1 1.2 shard_map.69
  131.4 19.4 %all_to_all.26 = bf16[16,32,896]{2,1,0:T(8,128)(2,1)S(1)} all-to-all(bf16[16,32,896]{2,1,0:T(8,128)(2,1)S(1)} %bitcast.14), channel_id=1, replica_groups=mesh['x'=4,'zh'=8,'zl'=2,'c'=2,'y'=4] {'x','zl','c'}, dimensions={0} | all-to-all | bytes 1835008 | tf_op jit(solution)/shard_map/all_to_all | solution.py:201
  150.8 0.5 shard_map.70
  151.3 24.1 %all_to_all.27.shares_ref = bf16[32,4,896]{2,1,0:T(4,128)(2,1)S(1)} all-to-all(bf16[32,4,896]{2,1,0:T(4,128)(2,1)S(1)} %shard_map.70), channel_id=1, replica_groups=mesh['x'=4,'zh'=8,'zl'=2,'c'=2,'y'=4] {'zh','y'}, dimensions={0} | all-to-all | bytes 458752 | tf_op jit(solution)/shard_map/all_to_all | solution.py:201
  175.4 0.7 shard_map.71
Async XLA Ops:
  1.6 36.5 %all-to-all-start = ((bf16[8,16,1024]{2,1,0:T(8,128)(2,1)}), bf16[8,16,1024]{2,1,0:T(8,128)(2,1)S(1)}, u32[]{:S(2)}, u32[]{:S(2)}) async-start(bf16[8,16,1024]{2,1,0:T(8,128)(2,1)} %shard_map.64), calls=%async_computation | async-start | bytes 524288 | tf_op jit(solution)/shard_map/all_to_all | solution.py:201
  38.8 1.8 %copy-start = (bf16[4,512,896]{2,1,0:T(8,128)(2,1)}, bf16[4,512,896]{2,1,0:T(8,128)(2,1)S(1)}, u32[]{:S(2)}) copy-start(bf16[4,512,896]{2,1,0:T(8,128)(2,1)S(1)} %get-tuple-element.17) | copy-start | bytes 11010052
  40.6 52.2 %all-to-all-start.1 = ((bf16[64,32,896]{2,1,0:T(8,128)(2,1)}), bf16[64,32,896]{2,1,0:T(8,128)(2,1)}, u32[]{:S(2)}, u32[]{:S(2)}) async-start(bf16[64,32,896]{2,1,0:T(8,128)(2,1)} %bitcast.12), calls=%async_computation.1 | async-start | bytes 7340032 | tf_op jit(solution)/shard_map/all_to_all | solution.py:201
  48.7 44.1 %copy-start.1 = (bf16[1,3584,256]{2,1,0:T(8,128)(2,1)S(1)}, bf16[1,3584,256]{2,1,0:T(8,128)(2,1)}, u32[]{:S(2)}) copy-start(bf16[1,3584,256]{2,1,0:T(8,128)(2,1)} %param.9) | copy-start | bytes 5505028
  51.1 50.7 %collective-permute-start = (bf16[256,896]{1,0:T(8,128)(2,1)}, bf16[256,896]{1,0:T(8,128)(2,1)S(1)}, u32[]{:S(2)}, u32[]{:S(2)}) collective-permute-start(bf16[256,896]{1,0:T(8,128)(2,1)} %get-tuple-element.19), channel_id=1, source_target_pairs={{0,1},{1,2},{2,3},{3,0},{4,5},{5,6},{6,7},{7,4},{8,9},{9,10},{10,1... | collective-permute-start | bytes 1376264 | tf_op jit(solution)/shard_map/ppermute | solution.py:224
  54.5 57.8 %collective-permute-start.1 = (bf16[256,896]{1,0:T(8,128)(2,1)}, bf16[256,896]{1,0:T(8,128)(2,1)S(1)}, u32[]{:S(2)}, u32[]{:S(2)}) collective-permute-start(bf16[256,896]{1,0:T(8,128)(2,1)} %get-tuple-element.20), channel_id=1, source_target_pairs={{0,2},{1,3},{2,0},{3,1},{4,6},{5,7},{6,4},{7,5},{8,10},{9,11},{10,... | collective-permute-start | bytes 1376264 | tf_op jit(solution)/shard_map/ppermute | solution.py:224
  61.5 50.8 %collective-permute-start.2 = (bf16[256,896]{1,0:T(8,128)(2,1)}, bf16[256,896]{1,0:T(8,128)(2,1)S(1)}, u32[]{:S(2)}, u32[]{:S(2)}) collective-permute-start(bf16[256,896]{1,0:T(8,128)(2,1)} %get-tuple-element.21), channel_id=1, source_target_pairs={{0,3},{1,0},{2,1},{3,2},{4,7},{5,4},{6,5},{7,6},{8,11},{9,8},{10,9... | collective-permute-start | bytes 1376264 | tf_op jit(solution)/shard_map/ppermute | solution.py:224
  92.8 1.5 copy-start.2
  98.7 31.4 %copy-start.3 = (bf16[256,896]{1,0:T(8,128)(2,1)S(1)}, bf16[256,896]{1,0:T(8,128)(2,1)}, u32[]{:S(2)}) copy-start(bf16[256,896]{1,0:T(8,128)(2,1)} %get-tuple-element.23.refs_0_) | copy-start | bytes 1376260

commit v8 on v7

--- a/solution.py
+++ b/solution.py
@@ -68,17 +68,31 @@
     return call(body, outs, [SMEM, HBM, HBM, HBM], scratch, None)(member, tokens, expert_ids.T, route_logits.T)
 
 
-def route_rows(gathered, pair, rows, top, n_x, n_pair, n_c, n_dp):
+def route_masks(pair, total, rows, held):
+    def body(pair_ref, ahead_ref, wanted_ref):
+        one = lax.broadcasted_iota(i32, (total, total), 0)
+        two = lax.broadcasted_iota(i32, (total, total), 1)
+        ahead_ref[...] = jnp.where((one // rows == two // rows) & (one < two), 1.0, 0.0).astype(bf16)
+        spot = lax.broadcasted_iota(i32, (held, total), 0)
+        token = lax.broadcasted_iota(i32, (held, total), 1)
+        wanted_ref[...] = jnp.where(token // rows == spot // SLOTS, spot % SLOTS, -2).astype(f32)
+
+    outs = (((total, total), bf16), ((held, total), f32))
+    return call(body, outs, [SMEM])(pair)
+
+
+def route_rows(gathered, pair, ahead, wanted, top, n_x, n_pair, n_c, n_dp):
     total = gathered.shape[0]
     part = gathered.shape[1] - SIDE
     experts = n_x * 2 * n_c
     held = n_pair * SLOTS
     pad = max(16, experts)
 
-    def body(pair_ref, gathered_ref, out_ref, high_ref, low_ref, pick_ref):
+    def body(pair_ref, gathered_ref, ahead_ref, wanted_ref, out_ref, high_ref, low_ref, pick_ref):
         side = gathered_ref[:, part:].astype(f32).T
         line = lax.broadcasted_iota(i32, (pad, 1), 0)
-        name = ((line // (2 * n_c)) * n_pair + pair_ref[0]) * (2 * n_c) + line % (2 * n_c)
+        core, chip, side_plane = line // (2 * n_x), line // 2 % n_x, line % 2
+        name = ((chip * n_pair + pair_ref[0]) * 2 + side_plane) * n_c + core
         name = jnp.where(line < experts, name, -1).astype(f32)
         named = jnp.zeros((pad, total), f32)
         high = jnp.zeros((pad, total), f32)
@@ -88,14 +102,9 @@
             named = named + jnp.where(same, 1.0, 0.0)
             high = high + jnp.where(same, side[top + k : top + k + 1, :], 0.0)
             low = low + jnp.where(same, side[2 * top + k : 2 * top + k + 1, :], 0.0)
-        one = lax.broadcasted_iota(i32, (total, total), 0)
-        two = lax.broadcasted_iota(i32, (total, total), 1)
-        ahead = jnp.where((one // rows == two // rows) & (one < two), 1.0, 0.0).astype(bf16)
-        rank = jnp.dot(named.astype(bf16), ahead, preferred_element_type=f32)
+        rank = jnp.dot(named.astype(bf16), ahead_ref[...], preferred_element_type=f32)
         rank = jnp.where(named > 0.5, rank, -1.0)
-        spot = lax.broadcasted_iota(i32, (held, total), 0)
-        token = lax.broadcasted_iota(i32, (held, total), 1)
-        wanted = jnp.where(token // rows == spot // SLOTS, spot % SLOTS, -2).astype(f32)
+        wanted = wanted_ref[...]
         for j in range(experts):
             hit = rank[j : j + 1, :] == wanted
             at = slice(j * held, (j + 1) * held)
@@ -109,7 +118,7 @@
     slots = experts * held
     outs = (((n_dp, slots, part), bf16),) + (((slots, total), bf16),) * 2
     scratch = [pltpu.VMEM((slots, total), bf16)]
-    return call(body, outs, [SMEM, VMEM], scratch)(pair, gathered)
+    return call(body, outs, [SMEM] + [VMEM] * 3, scratch)(pair, gathered, ahead, wanted)
 
 
 def hidden_rows(received, w_gate, w_up):
@@ -146,27 +155,6 @@
     return call(body, [((slots, part), bf16)], [SMEM, VMEM] + [VMEM] * n_dp)(
         member, hidden, *downs
     )
-
-
-def cut_columns(down, member, n_dp, shifts):
-    units, width = down.shape
-    part = width // n_dp
-
-    def body(member_ref, down_hbm, *refs):
-        sems = refs[-1]
-        copies = []
-        for i, s in enumerate(shifts):
-            owner = lax.rem(member_ref[0] + s, n_dp)
-            start = pl.multiple_of(owner * part, 128)
-            copies.append(pltpu.make_async_copy(down_hbm.at[:, pl.ds(start, part)], refs[i], sems.at[i]))
-        for copy in copies:
-            copy.start()
-        for copy in copies:
-            copy.wait()
-
-    count = len(shifts)
-    outs = (((units, part), bf16),) * count
-    return call(body, outs, [SMEM, HBM], [pltpu.SemaphoreType.DMA((count,))], None)(member, down)
 
 
 def mix_rows(received, high, low, share):
@@ -217,19 +205,23 @@
     packed = pack_rows(tokens, expert_ids, route_logits, member_ref, n_dp, n_pair)
     gathered = exchange(packed, "zh").reshape(n_pair * rows, -1)
 
-    early = cut_columns(expert_down[0], member_ref, n_dp, range(1, n_dp - 1))
-    late = cut_columns(expert_down[0], member_ref, n_dp, (0, n_dp - 1))
-    downs = [late[0], *early, late[1]]
-    for s in range(1, n_dp):
-        downs[s] = lax.ppermute(downs[s], "y", [(i, (i + s) % n_dp) for i in range(n_dp)])
-
-    outgoing, high, low = route_rows(gathered, pair_ref, rows, top, n_x, n_pair, n_c, n_dp)
-    arrived = exchange(outgoing.reshape(n_dp * experts, held, part), ("y", "x", "zl", "c"))
+    downs = []
+    for s in range(n_dp):
+        owner = member + s
+        owner = jnp.where(owner >= n_dp, owner - n_dp, owner)
+        piece = lax.dynamic_slice_in_dim(expert_down[0], owner * part, part, axis=1)
+        if s:
+            piece = lax.ppermute(piece, "y", [(i, (i + s) % n_dp) for i in range(n_dp)])
+        downs.append(piece)
+
+    ahead, wanted = route_masks(pair_ref, n_pair * rows, rows, held)
+    outgoing, high, low = route_rows(gathered, pair_ref, ahead, wanted, top, n_x, n_pair, n_c, n_dp)
+    arrived = exchange(outgoing.reshape(n_dp * experts, held, part), ("y", "c", "x", "zl"))
     hidden = hidden_rows(arrived.reshape(n_dp, slots, part), w_gate, w_up)
     hidden, downs = lax.optimization_barrier((hidden, downs))
     hidden = exchange(hidden, "y")
     results = output_rows(hidden, downs, member_ref)
-    back = exchange(results.reshape(experts, held, part), ("x", "zl", "c"))
+    back = exchange(results.reshape(experts, held, part), ("c", "x", "zl"))
     mixed = mix_rows(back.reshape(slots, part), high, low, rows // n_dp)
     shares = exchange(mixed, ("zh", "y"))
     return sum_rows(shares, n_dp)

time: 179 us -> 177 us (0.989)
  Pallas kernels: 13.5 us -> 10.1 us
  local copies, waits for them, and re-layouts: 3.34 us -> 6.09 us
    pallas_call x3 -> x2, Pallas kernels: 5.16 us -> 0.71 us  [the longest x1 0.69 us: route_rows(): call(body, outs, [SMEM] + [VMEM] * 3, scratch)]
    dynamic_slice x0 -> x1, local copies, waits for them, and re-layouts: none -> 2.75 us  [on_device(): piece = lax.dynamic_slice_in_dim(expert_down[0], owner * part, part, axis=1)]
    all_to_all x2, waiting for transfers between devices: 49.4 us -> 51.3 us  [exchange(): return lax.all_to_all(value, axes, split_axis=0, concat_axis=0, tiled=True)]
  transfers between devices with their start and end apart: 5 -> 5, of which waited for: 4 -> 4; matrix products, arithmetic and copies ran while one was open for 0% -> 2% of each run, Pallas kernels for 5% -> 3%
where the time goes in v8:
time: 177 us; the launch traced here: 176 us
  waiting for transfers between devices  64 us (36%)
  blocking collectives  60.9 us (34%)
  starting transfers between devices  34.7 us (20%)
  Pallas kernels  10.1 us (6%)
  local copies, waits for them, and re-layouts  6.09 us (3%)
    all_to_all x3, blocking collectives, exchange(): return lax.all_to_all(value, axes, split_axis=0, concat_axis=0, tiled=True)  60.9 us
    all_to_all x2, waiting for transfers between devices, exchange(): return lax.all_to_all(value, axes, split_axis=0, concat_axis=0, tiled=True)  51.3 us
    all_to_all x2, starting transfers between devices, exchange(): return lax.all_to_all(value, axes, split_axis=0, concat_axis=0, tiled=True)  23.2 us
    ppermute x3, waiting for transfers between devices, on_device(): piece = lax.ppermute(piece, 'y', [(i, (i + s) % n_dp) for i in range(n_dp)])  12.7 us
    ppermute x3, starting transfers between devices, on_device(): piece = lax.ppermute(piece, 'y', [(i, (i + s) % n_dp) for i in range(n_dp)])  11.4 us
    pallas_call x1, Pallas kernels, hidden_rows(): call(body, [((n_dp, slots, units), bf16)], [VMEM] * 3)  4.38 us
  transfers between devices with their start and end apart: 5, of which 4 were waited for; matrix products, arithmetic and copies ran while one was open for 2% of the time, Pallas kernels for 3%

profile of v8, /device:TPU:6, one launch (start us, length us, event | category | flops | bytes accessed | tf_op | source)
XLA Modules:
  0.0 175.8 jit_solution(8080570193763979773)
XLA Ops:
  0.0 1.6 shard_map.64
  1.6 15.1 %all-to-all-start = ((bf16[8,16,1024]{2,1,0:T(8,128)(2,1)}), bf16[8,16,1024]{2,1,0:T(8,128)(2,1)S(1)}, u32[]{:S(2)}, u32[]{:S(2)}) async-start(bf16[8,16,1024]{2,1,0:T(8,128)(2,1)} %shard_map.64), calls=%async_computation | async-start | bytes 524288 | tf_op jit(solution)/shard_map/all_to_all | solution.py:189
  16.7 21.3 %all-to-all-done = bf16[8,16,1024]{2,1,0:T(8,128)(2,1)S(1)} async-done(((bf16[8,16,1024]{2,1,0:T(8,128)(2,1)}), bf16[8,16,1024]{2,1,0:T(8,128)(2,1)S(1)}, u32[]{:S(2)}, u32[]{:S(2)}) %all-to-all-start) | async-done | bytes 262176 | tf_op jit(solution)/shard_map/all_to_all | solution.py:189
  38.1 0.7 shard_map.66
  38.8 0.0 copy-start
  38.8 1.8 %copy-done = bf16[4,512,896]{2,1,0:T(8,128)(2,1)} copy-done((bf16[4,512,896]{2,1,0:T(8,128)(2,1)}, bf16[4,512,896]{2,1,0:T(8,128)(2,1)S(1)}, u32[]{:S(2)}) %copy-start) | copy-done | bytes 3670040
  40.6 8.1 %all-to-all-start.1 = ((bf16[64,32,896]{2,1,0:T(8,128)(2,1)}), bf16[64,32,896]{2,1,0:T(8,128)(2,1)}, u32[]{:S(2)}, u32[]{:S(2)}) async-start(bf16[64,32,896]{2,1,0:T(8,128)(2,1)} %bitcast.19), calls=%async_computation.1 | async-start | bytes 7340032 | tf_op jit(solution)/shard_map/all_to_all | solution.py:189
  48.8 0.0 copy-start.1
  48.8 2.8 %dynamic-slice_bitcast_fusion = (bf16[256,896]{1,0:T(8,128)(2,1)}, bf16[256,896]{1,0:T(8,128)(2,1)}, bf16[256,896]{1,0:T(8,128)(2,1)S(1)}, bf16[256,896]{1,0:T(8,128)(2,1)}) fusion(bf16[1,256,3584]{2,1,0:T(8,128)(2,1)} %param.11, s32[]{:T(128)S(6)} %select_n.32, s32[]{:T(128)S(6)} %select_n.28, s32[]{:T(128)S(6)} %select_n.26, s32[]{:T(128)S(6)} %select_n.30), kind=kLoop, calls=%fused_computation | loop fusion | bytes 3670032 | tf_op jit(solution)/shard_map/dynamic_slice | solution.py:212
  51.5 3.4 %collective-permute-start = (bf16[256,896]{1,0:T(8,128)(2,1)}, bf16[256,896]{1,0:T(8,128)(2,1)S(1)}, u32[]{:S(2)}, u32[]{:S(2)}) collective-permute-start(bf16[256,896]{1,0:T(8,128)(2,1)} %get-tuple-element.26), channel_id=1, source_target_pairs={{0,1},{1,2},{2,3},{3,0},{4,5},{5,6},{6,7},{7,4},{8,9},{9,10},{10,1... | collective-permute-start | bytes 1376264 | tf_op jit(solution)/shard_map/ppermute | solution.py:214
  54.9 4.8 %collective-permute-start.1 = (bf16[256,896]{1,0:T(8,128)(2,1)}, bf16[256,896]{1,0:T(8,128)(2,1)S(1)}, u32[]{:S(2)}, u32[]{:S(2)}) collective-permute-start(bf16[256,896]{1,0:T(8,128)(2,1)} %get-tuple-element.28), channel_id=1, source_target_pairs={{0,2},{1,3},{2,0},{3,1},{4,6},{5,7},{6,4},{7,5},{8,10},{9,11},{10,... | collective-permute-start | bytes 1376264 | tf_op jit(solution)/shard_map/ppermute | solution.py:214
  59.7 3.3 %collective-permute-start.2 = (bf16[256,896]{1,0:T(8,128)(2,1)}, bf16[256,896]{1,0:T(8,128)(2,1)}, u32[]{:S(2)}, u32[]{:S(2)}) collective-permute-start(bf16[256,896]{1,0:T(8,128)(2,1)} %get-tuple-element.25), channel_id=1, source_target_pairs={{0,3},{1,0},{2,1},{3,2},{4,7},{5,4},{6,5},{7,6},{8,11},{9,8},{10,9... | collective-permute-start | bytes 1376264 | tf_op jit(solution)/shard_map/ppermute | solution.py:214
  63.0 29.9 %all-to-all-done.1 = bf16[64,32,896]{2,1,0:T(8,128)(2,1)} async-done(((bf16[64,32,896]{2,1,0:T(8,128)(2,1)}), bf16[64,32,896]{2,1,0:T(8,128)(2,1)}, u32[]{:S(2)}, u32[]{:S(2)}) %all-to-all-start.1) | async-done | bytes 3670048 | tf_op jit(solution)/shard_map/all_to_all | solution.py:189
  92.9 0.0 copy-done.1
  93.0 0.0 copy-start.2
  93.0 1.5 copy-done.2
  94.5 4.4 %shard_map.67 = bf16[4,512,256]{2,1,0:T(8,128)(2,1)S(1)} custom-call(bf16[4,512,896]{2,1,0:T(8,128)(2,1)} %bitcast.6.rows_ref, bf16[3584,256]{1,0:T(8,128)(2,1)S(1)} %bitcast.22, bf16[3584,256]{1,0:T(8,128)(2,1)S(1)} %bitcast.23), custom_call_target="tpu_custom_call" | custom-call | tf_op jit(solution)/shard_map/pallas_call | solution.py:140
  98.8 3.0 %collective-permute-done.refs_1_ = bf16[256,896]{1,0:T(8,128)(2,1)S(1)} collective-permute-done((bf16[256,896]{1,0:T(8,128)(2,1)}, bf16[256,896]{1,0:T(8,128)(2,1)S(1)}, u32[]{:S(2)}, u32[]{:S(2)}) %collective-permute-start) | collective-permute-done | bytes 458784 | tf_op jit(solution)/shard_map/ppermute | solution.py:214
  101.9 9.7 %collective-permute-done.1.refs_2_ = bf16[256,896]{1,0:T(8,128)(2,1)S(1)} collective-permute-done((bf16[256,896]{1,0:T(8,128)(2,1)}, bf16[256,896]{1,0:T(8,128)(2,1)S(1)}, u32[]{:S(2)}, u32[]{:S(2)}) %collective-permute-start.1) | collective-permute-done | bytes 458784 | tf_op jit(solution)/shard_map/ppermute | solution.py:214
  111.5 0.0 collective-permute-done.2.refs_3_
  111.5 18.1 %all_to_all.25.hidden_ref = bf16[4,512,256]{2,1,0:T(8,128)(2,1)S(1)} all-to-all(bf16[4,512,256]{2,1,0:T(8,128)(2,1)S(1)} %shard_map.67), channel_id=1, replica_groups=mesh['x'=4,'zh'=8,'zl'=2,'c'=2,'y'=4] {'y'}, dimensions={0} | all-to-all | bytes 2097152 | tf_op jit(solution)/shard_map/all_to_all | solution.py:189
  129.7 2.3 %shard_map.68 = bf16[512,896]{1,0:T(8,128)(2,1)S(1)} custom-call(s32[1]{0:T(128)} %bitcast.member_ref, bf16[4,512,256]{2,1,0:T(8,128)(2,1)S(1)} %all_to_all.25.hidden_ref, bf16[256,896]{1,0:T(8,128)(2,1)S(1)} %get-tuple-element.19.refs_0_, bf16[256,896]{1,0:T(8,128)(2,1)S(1)} %collective-permute-done.refs_1_, ...), custom_call_target="tpu_custom_call" | custom-call | tf_op jit(solution)/shard_map/pallas_call | solution.py:155
  132.0 18.2 %all_to_all.26 = bf16[16,32,896]{2,1,0:T(8,128)(2,1)S(1)} all-to-all(bf16[16,32,896]{2,1,0:T(8,128)(2,1)S(1)} %bitcast.21), channel_id=1, replica_groups=mesh['x'=4,'zh'=8,'zl'=2,'c'=2,'y'=4] {'c','x','zl'}, dimensions={0} | all-to-all | bytes 1835008 | tf_op jit(solution)/shard_map/all_to_all | solution.py:189
  150.2 0.5 shard_map.69
  150.7 24.5 %all_to_all.27.shares_ref = bf16[32,4,896]{2,1,0:T(4,128)(2,1)S(1)} all-to-all(bf16[32,4,896]{2,1,0:T(4,128)(2,1)S(1)} %shard_map.69), channel_id=1, replica_groups=mesh['x'=4,'zh'=8,'zl'=2,'c'=2,'y'=4] {'zh','y'}, dimensions={0} | all-to-all | bytes 458752 | tf_op jit(solution)/shard_map/all_to_all | solution.py:189
  175.1 0.7 shard_map.70
  (1 shorter events, 0.0 us)
Async XLA Ops:
  1.6 36.5 %all-to-all-start = ((bf16[8,16,1024]{2,1,0:T(8,128)(2,1)}), bf16[8,16,1024]{2,1,0:T(8,128)(2,1)S(1)}, u32[]{:S(2)}, u32[]{:S(2)}) async-start(bf16[8,16,1024]{2,1,0:T(8,128)(2,1)} %shard_map.64), calls=%async_computation | async-start | bytes 524288 | tf_op jit(solution)/shard_map/all_to_all | solution.py:189
  38.8 1.8 %copy-start = (bf16[4,512,896]{2,1,0:T(8,128)(2,1)}, bf16[4,512,896]{2,1,0:T(8,128)(2,1)S(1)}, u32[]{:S(2)}) copy-start(bf16[4,512,896]{2,1,0:T(8,128)(2,1)S(1)} %get-tuple-element.17) | copy-start | bytes 11010052
  40.6 52.3 %all-to-all-start.1 = ((bf16[64,32,896]{2,1,0:T(8,128)(2,1)}), bf16[64,32,896]{2,1,0:T(8,128)(2,1)}, u32[]{:S(2)}, u32[]{:S(2)}) async-start(bf16[64,32,896]{2,1,0:T(8,128)(2,1)} %bitcast.19), calls=%async_computation.1 | async-start | bytes 7340032 | tf_op jit(solution)/shard_map/all_to_all | solution.py:189
  48.8 44.2 %copy-start.1 = (bf16[1,3584,256]{2,1,0:T(8,128)(2,1)S(1)}, bf16[1,3584,256]{2,1,0:T(8,128)(2,1)}, u32[]{:S(2)}) copy-start(bf16[1,3584,256]{2,1,0:T(8,128)(2,1)} %param.9) | copy-start | bytes 5505028
  51.5 50.3 %collective-permute-start = (bf16[256,896]{1,0:T(8,128)(2,1)}, bf16[256,896]{1,0:T(8,128)(2,1)S(1)}, u32[]{:S(2)}, u32[]{:S(2)}) collective-permute-start(bf16[256,896]{1,0:T(8,128)(2,1)} %get-tuple-element.26), channel_id=1, source_target_pairs={{0,1},{1,2},{2,3},{3,0},{4,5},{5,6},{6,7},{7,4},{8,9},{9,10},{10,1... | collective-permute-start | bytes 1376264 | tf_op jit(solution)/shard_map/ppermute | solution.py:214
  54.9 56.6 %collective-permute-start.1 = (bf16[256,896]{1,0:T(8,128)(2,1)}, bf16[256,896]{1,0:T(8,128)(2,1)S(1)}, u32[]{:S(2)}, u32[]{:S(2)}) collective-permute-start(bf16[256,896]{1,0:T(8,128)(2,1)} %get-tuple-element.28), channel_id=1, source_target_pairs={{0,2},{1,3},{2,0},{3,1},{4,6},{5,7},{6,4},{7,5},{8,10},{9,11},{10,... | collective-permute-start | bytes 1376264 | tf_op jit(solution)/shard_map/ppermute | solution.py:214
  59.7 51.8 %collective-permute-start.2 = (bf16[256,896]{1,0:T(8,128)(2,1)}, bf16[256,896]{1,0:T(8,128)(2,1)}, u32[]{:S(2)}, u32[]{:S(2)}) collective-permute-start(bf16[256,896]{1,0:T(8,128)(2,1)} %get-tuple-element.25), channel_id=1, source_target_pairs={{0,3},{1,0},{2,1},{3,2},{4,7},{5,4},{6,5},{7,6},{8,11},{9,8},{10,9... | collective-permute-start | bytes 1376264 | tf_op jit(solution)/shard_map/ppermute | solution.py:214
  93.0 1.5 copy-start.2

commit v9 on v8

--- a/solution.py
+++ b/solution.py
@@ -133,28 +133,23 @@
             at = slice(d * part, (d + 1) * part)
             v = v + jnp.dot(rows, gate_ref[at, :], preferred_element_type=f32)
             u = u + jnp.dot(rows, up_ref[at, :], preferred_element_type=f32)
-        made = (v / (1.0 + jnp.exp(-v)) * u).astype(bf16)
-        for d in range(n_dp):
-            out_ref[d] = made
-
-    return call(body, [((n_dp, slots, units), bf16)], [VMEM] * 3)(received, w_gate, w_up)
-
-
-def output_rows(hidden, downs, member):
-    n_dp, slots, _ = hidden.shape
+        out_ref[...] = (v / (1.0 + jnp.exp(-v)) * u).astype(bf16)
+
+    return call(body, [((slots, units), bf16)], [VMEM] * 3)(received, w_gate, w_up)
+
+
+def output_rows(hiddens, downs):
+    count = len(downs)
+    slots = hiddens[0].shape[0]
     part = downs[0].shape[1]
 
-    def body(member_ref, hidden_ref, *refs):
-        out_ref = refs[-1]
+    def body(*refs):
         total = jnp.zeros((slots, part), f32)
-        for s in range(n_dp):
-            source = lax.rem(member_ref[0] + (n_dp - s), n_dp)
-            total = total + jnp.dot(hidden_ref[source], refs[s][...], preferred_element_type=f32)
-        out_ref[...] = total.astype(bf16)
-
-    return call(body, [((slots, part), bf16)], [SMEM, VMEM] + [VMEM] * n_dp)(
-        member, hidden, *downs
-    )
+        for s in range(count):
+            total = total + jnp.dot(refs[s][...], refs[count + s][...], preferred_element_type=f32)
+        refs[-1][...] = total.astype(bf16)
+
+    return call(body, [((slots, part), bf16)], [VMEM] * (2 * count))(*hiddens, *downs)
 
 
 def mix_rows(received, high, low, share):
@@ -219,8 +214,10 @@
     arrived = exchange(outgoing.reshape(n_dp * experts, held, part), ("y", "c", "x", "zl"))
     hidden = hidden_rows(arrived.reshape(n_dp, slots, part), w_gate, w_up)
     hidden, downs = lax.optimization_barrier((hidden, downs))
-    hidden = exchange(hidden, "y")
-    results = output_rows(hidden, downs, member_ref)
+    hiddens = [hidden]
+    for s in range(1, n_dp):
+        hiddens.append(lax.ppermute(hidden, "y", [(i, (i + s) % n_dp) for i in range(n_dp)]))
+    results = output_rows(hiddens, downs)
     back = exchange(results.reshape(experts, held, part), ("c", "x", "zl"))
     mixed = mix_rows(back.reshape(slots, part), high, low, rows // n_dp)
     shares = exchange(mixed, ("zh", "y"))

time: 177 us -> 180 us (1.017)
  blocking collectives: 60.9 us -> 44.8 us
  starting transfers between devices: 34.7 us -> 44.8 us
  waiting for transfers between devices: 64 us -> 72.8 us
    all_to_all x3 -> x2, blocking collectives: 60.9 us -> 44.8 us  [exchange(): return lax.all_to_all(value, axes, split_axis=0, concat_axis=0, tiled=True)]
    ppermute x0 -> x3, starting transfers between devices: none -> 10.1 us  [on_device(): lax.ppermute(hidden, 'y', [(i, (i + s) % n_dp) for i in range(n_dp)])]
    ppermute x0 -> x3, waiting for transfers between devices: none -> 8.86 us  [on_device(): lax.ppermute(hidden, 'y', [(i, (i + s) % n_dp) for i in range(n_dp)])]
  transfers between devices with their start and end apart: 5 -> 8, of which waited for: 4 -> 6; matrix products, arithmetic and copies ran while one was open for 2% -> 2% of each run, Pallas kernels for 3% -> 2%
where the time goes in v9:
time: 180 us; the launch traced here: 179 us
  waiting for transfers between devices  72.8 us (40%)
  starting transfers between devices  44.8 us (25%)
  blocking collectives  44.8 us (25%)
  Pallas kernels  10.1 us (6%)
  local copies, waits for them, and re-layouts  6.11 us (3%)
    all_to_all x2, waiting for transfers between devices, exchange(): return lax.all_to_all(value, axes, split_axis=0, concat_axis=0, tiled=True)  51.3 us
    all_to_all x2, blocking collectives, exchange(): return lax.all_to_all(value, axes, split_axis=0, concat_axis=0, tiled=True)  44.8 us
    all_to_all x2, starting transfers between devices, exchange(): return lax.all_to_all(value, axes, split_axis=0, concat_axis=0, tiled=True)  23.2 us
    ppermute x3, waiting for transfers between devices, on_device(): piece = lax.ppermute(piece, 'y', [(i, (i + s) % n_dp) for i in range(n_dp)])  12.7 us
    ppermute x3, starting transfers between devices, on_device(): piece = lax.ppermute(piece, 'y', [(i, (i + s) % n_dp) for i in range(n_dp)])  11.4 us
    ppermute x3, starting transfers between devices, on_device(): lax.ppermute(hidden, 'y', [(i, (i + s) % n_dp) for i in range(n_dp)])  10.1 us
    ppermute x3, waiting for transfers between devices, on_device(): lax.ppermute(hidden, 'y', [(i, (i + s) % n_dp) for i in range(n_dp)])  8.86 us
    pallas_call x1, Pallas kernels, hidden_rows(): call(body, [((slots, units), bf16)], [VMEM] * 3)(received, w_gate, w_up)  4.38 us
  transfers between devices with their start and end apart: 8, of which 6 were waited for; matrix products, arithmetic and copies ran while one was open for 2% of the time, Pallas kernels for 2%

profile of v9, /device:TPU:6, one launch (start us, length us, event | category | flops | bytes accessed | tf_op | source)
XLA Modules:
  0.0 178.8 jit_solution(18219695560741283866)
XLA Ops:
  0.0 1.6 shard_map.64
  1.6 15.1 %all-to-all-start = ((bf16[8,16,1024]{2,1,0:T(8,128)(2,1)}), bf16[8,16,1024]{2,1,0:T(8,128)(2,1)S(1)}, u32[]{:S(2)}, u32[]{:S(2)}) async-start(bf16[8,16,1024]{2,1,0:T(8,128)(2,1)} %shard_map.64), calls=%async_computation | async-start | bytes 524288 | tf_op jit(solution)/shard_map/all_to_all | solution.py:184
  16.7 21.3 %all-to-all-done = bf16[8,16,1024]{2,1,0:T(8,128)(2,1)S(1)} async-done(((bf16[8,16,1024]{2,1,0:T(8,128)(2,1)}), bf16[8,16,1024]{2,1,0:T(8,128)(2,1)S(1)}, u32[]{:S(2)}, u32[]{:S(2)}) %all-to-all-start) | async-done | bytes 262176 | tf_op jit(solution)/shard_map/all_to_all | solution.py:184
  38.1 0.7 shard_map.66
  38.8 0.0 copy-start
  38.8 1.8 %copy-done = bf16[4,512,896]{2,1,0:T(8,128)(2,1)} copy-done((bf16[4,512,896]{2,1,0:T(8,128)(2,1)}, bf16[4,512,896]{2,1,0:T(8,128)(2,1)S(1)}, u32[]{:S(2)}) %copy-start) | copy-done | bytes 3670040
  40.6 8.1 %all-to-all-start.1 = ((bf16[64,32,896]{2,1,0:T(8,128)(2,1)}), bf16[64,32,896]{2,1,0:T(8,128)(2,1)}, u32[]{:S(2)}, u32[]{:S(2)}) async-start(bf16[64,32,896]{2,1,0:T(8,128)(2,1)} %bitcast.19), calls=%async_computation.1 | async-start | bytes 7340032 | tf_op jit(solution)/shard_map/all_to_all | solution.py:184
  48.8 0.0 copy-start.1
  48.8 2.8 %dynamic-slice_bitcast_fusion = (bf16[256,896]{1,0:T(8,128)(2,1)}, bf16[256,896]{1,0:T(8,128)(2,1)}, bf16[256,896]{1,0:T(8,128)(2,1)S(1)}, bf16[256,896]{1,0:T(8,128)(2,1)}) fusion(bf16[1,256,3584]{2,1,0:T(8,128)(2,1)} %param.11, s32[]{:T(128)S(6)} %select_n.32, s32[]{:T(128)S(6)} %select_n.28, s32[]{:T(128)S(6)} %select_n.26, s32[]{:T(128)S(6)} %select_n.30), kind=kLoop, calls=%fused_computation | loop fusion | bytes 3670032 | tf_op jit(solution)/shard_map/dynamic_slice | solution.py:207
  51.6 3.4 %collective-permute-start = (bf16[256,896]{1,0:T(8,128)(2,1)}, bf16[256,896]{1,0:T(8,128)(2,1)S(1)}, u32[]{:S(2)}, u32[]{:S(2)}) collective-permute-start(bf16[256,896]{1,0:T(8,128)(2,1)} %get-tuple-element.26), channel_id=1, source_target_pairs={{0,1},{1,2},{2,3},{3,0},{4,5},{5,6},{6,7},{7,4},{8,9},{9,10},{10,1... | collective-permute-start | bytes 1376264 | tf_op jit(solution)/shard_map/ppermute | solution.py:209
  54.9 4.8 %collective-permute-start.1 = (bf16[256,896]{1,0:T(8,128)(2,1)}, bf16[256,896]{1,0:T(8,128)(2,1)S(1)}, u32[]{:S(2)}, u32[]{:S(2)}) collective-permute-start(bf16[256,896]{1,0:T(8,128)(2,1)} %get-tuple-element.28), channel_id=1, source_target_pairs={{0,2},{1,3},{2,0},{3,1},{4,6},{5,7},{6,4},{7,5},{8,10},{9,11},{10,... | collective-permute-start | bytes 1376264 | tf_op jit(solution)/shard_map/ppermute | solution.py:209
  59.8 3.3 %collective-permute-start.2 = (bf16[256,896]{1,0:T(8,128)(2,1)}, bf16[256,896]{1,0:T(8,128)(2,1)}, u32[]{:S(2)}, u32[]{:S(2)}) collective-permute-start(bf16[256,896]{1,0:T(8,128)(2,1)} %get-tuple-element.25), channel_id=1, source_target_pairs={{0,3},{1,0},{2,1},{3,2},{4,7},{5,4},{6,5},{7,6},{8,11},{9,8},{10,9... | collective-permute-start | bytes 1376264 | tf_op jit(solution)/shard_map/ppermute | solution.py:209
  63.0 29.9 %all-to-all-done.1 = bf16[64,32,896]{2,1,0:T(8,128)(2,1)} async-done(((bf16[64,32,896]{2,1,0:T(8,128)(2,1)}), bf16[64,32,896]{2,1,0:T(8,128)(2,1)}, u32[]{:S(2)}, u32[]{:S(2)}) %all-to-all-start.1) | async-done | bytes 3670048 | tf_op jit(solution)/shard_map/all_to_all | solution.py:184
  92.9 0.0 copy-done.1
  92.9 0.0 copy-start.2
  93.0 1.5 copy-done.2
  94.5 4.4 %shard_map.67.refs_0_ = bf16[512,256]{1,0:T(8,128)(2,1)S(1)} custom-call(bf16[4,512,896]{2,1,0:T(8,128)(2,1)} %bitcast.6.rows_ref, bf16[3584,256]{1,0:T(8,128)(2,1)S(1)} %bitcast.22, bf16[3584,256]{1,0:T(8,128)(2,1)S(1)} %bitcast.23), custom_call_target="tpu_custom_call" | custom-call | tf_op jit(solution)/shard_map/pallas_call | solution.py:138
  98.8 3.0 %collective-permute-done.refs_5_ = bf16[256,896]{1,0:T(8,128)(2,1)S(1)} collective-permute-done((bf16[256,896]{1,0:T(8,128)(2,1)}, bf16[256,896]{1,0:T(8,128)(2,1)S(1)}, u32[]{:S(2)}, u32[]{:S(2)}) %collective-permute-start) | collective-permute-done | bytes 458784 | tf_op jit(solution)/shard_map/ppermute | solution.py:209
  101.9 9.7 %collective-permute-done.1.refs_6_ = bf16[256,896]{1,0:T(8,128)(2,1)S(1)} collective-permute-done((bf16[256,896]{1,0:T(8,128)(2,1)}, bf16[256,896]{1,0:T(8,128)(2,1)S(1)}, u32[]{:S(2)}, u32[]{:S(2)}) %collective-permute-start.1) | collective-permute-done | bytes 458784 | tf_op jit(solution)/shard_map/ppermute | solution.py:209
  111.5 0.0 collective-permute-done.2.refs_7_
  111.5 1.9 %collective-permute-start.3 = (bf16[512,256]{1,0:T(8,128)(2,1)S(1)}, bf16[512,256]{1,0:T(8,128)(2,1)S(1)}, u32[]{:S(2)}, u32[]{:S(2)}) collective-permute-start(bf16[512,256]{1,0:T(8,128)(2,1)S(1)} %shard_map.67.refs_0_), channel_id=1, source_target_pairs={{0,1},{1,2},{2,3},{3,0},{4,5},{5,6},{6,7},{7,4},{8,9},{9,10},{10,1... | collective-permute-start | bytes 786440 | tf_op jit(solution)/shard_map/ppermute | solution.py:219
  113.5 3.7 %collective-permute-start.4 = (bf16[512,256]{1,0:T(8,128)(2,1)S(1)}, bf16[512,256]{1,0:T(8,128)(2,1)S(1)}, u32[]{:S(2)}, u32[]{:S(2)}) collective-permute-start(bf16[512,256]{1,0:T(8,128)(2,1)S(1)} %shard_map.67.refs_0_), channel_id=1, source_target_pairs={{0,2},{1,3},{2,0},{3,1},{4,6},{5,7},{6,4},{7,5},{8,10},{9,11},{10,... | collective-permute-start | bytes 786440 | tf_op jit(solution)/shard_map/ppermute | solution.py:219
  117.1 4.5 %collective-permute-start.5 = (bf16[512,256]{1,0:T(8,128)(2,1)S(1)}, bf16[512,256]{1,0:T(8,128)(2,1)S(1)}, u32[]{:S(2)}, u32[]{:S(2)}) collective-permute-start(bf16[512,256]{1,0:T(8,128)(2,1)S(1)} %shard_map.67.refs_0_), channel_id=1, source_target_pairs={{0,3},{1,0},{2,1},{3,2},{4,7},{5,4},{6,5},{7,6},{8,11},{9,8},{10,9... | collective-permute-start | bytes 786440 | tf_op jit(solution)/shard_map/ppermute | solution.py:219
  121.7 6.4 %collective-permute-done.3.refs_1_ = bf16[512,256]{1,0:T(8,128)(2,1)S(1)} collective-permute-done((bf16[512,256]{1,0:T(8,128)(2,1)S(1)}, bf16[512,256]{1,0:T(8,128)(2,1)S(1)}, u32[]{:S(2)}, u32[]{:S(2)}) %collective-permute-start.3) | collective-permute-done | bytes 262176 | tf_op jit(solution)/shard_map/ppermute | solution.py:219
  128.0 0.0 collective-permute-done.4.refs_2_
  128.0 2.5 %collective-permute-done.5.refs_3_ = bf16[512,256]{1,0:T(8,128)(2,1)S(1)} collective-permute-done((bf16[512,256]{1,0:T(8,128)(2,1)S(1)}, bf16[512,256]{1,0:T(8,128)(2,1)S(1)}, u32[]{:S(2)}, u32[]{:S(2)}) %collective-permute-start.5) | collective-permute-done | bytes 262176 | tf_op jit(solution)/shard_map/ppermute | solution.py:219
  130.5 2.3 %shard_map.68 = bf16[512,896]{1,0:T(8,128)(2,1)S(1)} custom-call(bf16[512,256]{1,0:T(8,128)(2,1)S(1)} %shard_map.67.refs_0_, bf16[512,256]{1,0:T(8,128)(2,1)S(1)} %collective-permute-done.3.refs_1_, bf16[512,256]{1,0:T(8,128)(2,1)S(1)} %collective-permute-done.4.refs_2_, bf16[512,256]{1,0:T(8,128)(2,1)S(1)} %collective-permute-done.5.refs_3_, ...), custom_call_target="tpu_custom_call" | custom-call | tf_op jit(solution)/shard_map/pallas_call | solution.py:152
  132.8 18.9 %all_to_all.20 = bf16[16,32,896]{2,1,0:T(8,128)(2,1)S(1)} all-to-all(bf16[16,32,896]{2,1,0:T(8,128)(2,1)S(1)} %bitcast.21), channel_id=1, replica_groups=mesh['x'=4,'zh'=8,'zl'=2,'c'=2,'y'=4] {'c','x','zl'}, dimensions={0} | all-to-all | bytes 1835008 | tf_op jit(solution)/shard_map/all_to_all | solution.py:184
  151.7 0.5 shard_map.69
  152.2 25.9 %all_to_all.21.shares_ref = bf16[32,4,896]{2,1,0:T(4,128)(2,1)S(1)} all-to-all(bf16[32,4,896]{2,1,0:T(4,128)(2,1)S(1)} %shard_map.69), channel_id=1, replica_groups=mesh['x'=4,'zh'=8,'zl'=2,'c'=2,'y'=4] {'zh','y'}, dimensions={0} | all-to-all | bytes 458752 | tf_op jit(solution)/shard_map/all_to_all | solution.py:184
  178.1 0.7 shard_map.70
  (1 shorter events, 0.0 us)
Async XLA Ops:
  1.6 36.5 %all-to-all-start = ((bf16[8,16,1024]{2,1,0:T(8,128)(2,1)}), bf16[8,16,1024]{2,1,0:T(8,128)(2,1)S(1)}, u32[]{:S(2)}, u32[]{:S(2)}) async-start(bf16[8,16,1024]{2,1,0:T(8,128)(2,1)} %shard_map.64), calls=%async_computation | async-start | bytes 524288 | tf_op jit(solution)/shard_map/all_to_all | solution.py:184
  38.8 1.8 %copy-start = (bf16[4,512,896]{2,1,0:T(8,128)(2,1)}, bf16[4,512,896]{2,1,0:T(8,128)(2,1)S(1)}, u32[]{:S(2)}) copy-start(bf16[4,512,896]{2,1,0:T(8,128)(2,1)S(1)} %get-tuple-element.17) | copy-start | bytes 11010052
  40.6 52.3 %all-to-all-start.1 = ((bf16[64,32,896]{2,1,0:T(8,128)(2,1)}), bf16[64,32,896]{2,1,0:T(8,128)(2,1)}, u32[]{:S(2)}, u32[]{:S(2)}) async-start(bf16[64,32,896]{2,1,0:T(8,128)(2,1)} %bitcast.19), calls=%async_computation.1 | async-start | bytes 7340032 | tf_op jit(solution)/shard_map/all_to_all | solution.py:184
  48.8 44.2 %copy-start.1 = (bf16[1,3584,256]{2,1,0:T(8,128)(2,1)S(1)}, bf16[1,3584,256]{2,1,0:T(8,128)(2,1)}, u32[]{:S(2)}) copy-start(bf16[1,3584,256]{2,1,0:T(8,128)(2,1)} %param.9) | copy-start | bytes 5505028
  51.6 50.3 %collective-permute-start = (bf16[256,896]{1,0:T(8,128)(2,1)}, bf16[256,896]{1,0:T(8,128)(2,1)S(1)}, u32[]{:S(2)}, u32[]{:S(2)}) collective-permute-start(bf16[256,896]{1,0:T(8,128)(2,1)} %get-tuple-element.26), channel_id=1, source_target_pairs={{0,1},{1,2},{2,3},{3,0},{4,5},{5,6},{6,7},{7,4},{8,9},{9,10},{10,1... | collective-permute-start | bytes 1376264 | tf_op jit(solution)/shard_map/ppermute | solution.py:209
  54.9 56.6 %collective-permute-start.1 = (bf16[256,896]{1,0:T(8,128)(2,1)}, bf16[256,896]{1,0:T(8,128)(2,1)S(1)}, u32[]{:S(2)}, u32[]{:S(2)}) collective-permute-start(bf16[256,896]{1,0:T(8,128)(2,1)} %get-tuple-element.28), channel_id=1, source_target_pairs={{0,2},{1,3},{2,0},{3,1},{4,6},{5,7},{6,4},{7,5},{8,10},{9,11},{10,... | collective-permute-start | bytes 1376264 | tf_op jit(solution)/shard_map/ppermute | solution.py:209
  59.8 51.8 %collective-permute-start.2 = (bf16[256,896]{1,0:T(8,128)(2,1)}, bf16[256,896]{1,0:T(8,128)(2,1)}, u32[]{:S(2)}, u32[]{:S(2)}) collective-permute-start(bf16[256,896]{1,0:T(8,128)(2,1)} %get-tuple-element.25), channel_id=1, source_target_pairs={{0,3},{1,0},{2,1},{3,2},{4,7},{5,4},{6,5},{7,6},{8,11},{9,8},{10,9... | collective-permute-start | bytes 1376264 | tf_op jit(solution)/shard_map/ppermute | solution.py:209
  92.9 1.5 copy-start.2
  111.5 16.5 %collective-permute-start.3 = (bf16[512,256]{1,0:T(8,128)(2,1)S(1)}, bf16[512,256]{1,0:T(8,128)(2,1)S(1)}, u32[]{:S(2)}, u32[]{:S(2)}) collective-permute-start(bf16[512,256]{1,0:T(8,128)(2,1)S(1)} %shard_map.67.refs_0_), channel_id=1, source_target_pairs={{0,1},{1,2},{2,3},{3,0},{4,5},{5,6},{6,7},{7,4},{8,9},{9,10},{10,1... | collective-permute-start | bytes 786440 | tf_op jit(solution)/shard_map/ppermute | solution.py:219
  113.5 14.6 %collective-permute-start.4 = (bf16[512,256]{1,0:T(8,128)(2,1)S(1)}, bf16[512,256]{1,0:T(8,128)(2,1)S(1)}, u32[]{:S(2)}, u32[]{:S(2)}) collective-permute-start(bf16[512,256]{1,0:T(8,128)(2,1)S(1)} %shard_map.67.refs_0_), channel_id=1, source_target_pairs={{0,2},{1,3},{2,0},{3,1},{4,6},{5,7},{6,4},{7,5},{8,10},{9,11},{10,... | collective-permute-start | bytes 786440 | tf_op jit(solution)/shard_map/ppermute | solution.py:219
  117.1 13.4 %collective-permute-start.5 = (bf16[512,256]{1,0:T(8,128)(2,1)S(1)}, bf16[512,256]{1,0:T(8,128)(2,1)S(1)}, u32[]{:S(2)}, u32[]{:S(2)}) collective-permute-start(bf16[512,256]{1,0:T(8,128)(2,1)S(1)} %shard_map.67.refs_0_), channel_id=1, source_target_pairs={{0,3},{1,0},{2,1},{3,2},{4,7},{5,4},{6,5},{7,6},{8,11},{9,8},{10,9... | collective-permute-start | bytes 786440 | tf_op jit(solution)/shard_map/ppermute | solution.py:219

commit v10 on v8

--- a/solution.py
+++ b/solution.py
@@ -7,7 +7,7 @@
 
 
 route_scale = 2.5
-SIDE = 128
+LANES, SIDE = 128, 8
 SLOTS = 4
 CHIPS_X, CORES = 4, 2
 
@@ -34,6 +34,7 @@
     rows, width = tokens.shape
     top = expert_ids.shape[1]
     part = width // n_dp
+    pieces = part // LANES
 
     def body(member_ref, tokens_hbm, ids_hbm, logits_hbm, out_ref, own_ref, ids_ref, logits_ref, sems):
         start = pl.multiple_of(member_ref[0] * part, 128)
@@ -51,14 +52,17 @@
         weights = route_scale * scores / jnp.sum(scores, axis=0, keepdims=True)
         high = weights.astype(bf16).astype(f32)
         side = jnp.concatenate(
-            [ids_ref[...].astype(f32), high, weights - high, jnp.zeros((SIDE - 3 * top, rows), f32)], axis=0
+            [ids_ref[...].astype(f32), high, weights - high, jnp.zeros((top, LANES - 3 * rows), f32)], axis=1
         )
-        side = side.T.astype(bf16)
+        if top < SIDE:
+            side = jnp.concatenate([side, jnp.zeros((SIDE - top, LANES), f32)], axis=0)
+        side = side.astype(bf16)
         for z in range(peers):
-            out_ref[z, :, :part] = own
-            out_ref[z, :, part:] = side
-
-    outs = [((peers, rows, part + SIDE), bf16)]
+            for i in range(pieces):
+                out_ref[z, i * rows : (i + 1) * rows, :] = own[:, i * LANES : (i + 1) * LANES]
+            out_ref[z, pieces * rows :, :] = side
+
+    outs = [((peers, pieces * rows + SIDE, LANES), bf16)]
     scratch = [
         pltpu.VMEM((rows, part), bf16),
         pltpu.VMEM((top, rows), i32),
@@ -81,15 +85,29 @@
     return call(body, outs, [SMEM])(pair)
 
 
-def route_rows(gathered, pair, ahead, wanted, top, n_x, n_pair, n_c, n_dp):
-    total = gathered.shape[0]
-    part = gathered.shape[1] - SIDE
+def route_rows(gathered, pair, ahead, wanted, rows, top, n_x, n_pair, n_c, n_dp):
+    blocks = gathered.shape[0]
+    total = blocks * rows
+    pieces = (gathered.shape[1] - SIDE) // rows
+    part = pieces * LANES
     experts = n_x * 2 * n_c
     held = n_pair * SLOTS
     pad = max(16, experts)
 
-    def body(pair_ref, gathered_ref, ahead_ref, wanted_ref, out_ref, high_ref, low_ref, pick_ref):
-        side = gathered_ref[:, part:].astype(f32).T
+    def body(pair_ref, gathered_ref, ahead_ref, wanted_ref, out_ref, high_ref, low_ref, pick_ref, own_ref):
+        for i in range(pieces):
+            own_ref[:, i * LANES : (i + 1) * LANES] = gathered_ref[:, i * rows : (i + 1) * rows, :].reshape(total, LANES)
+        lane = lax.broadcasted_iota(i32, (SIDE, LANES), 1) // rows
+        fields = []
+        for f in range(3):
+            field = jnp.zeros((SIDE, LANES), f32)
+            for b in range(blocks):
+                side = gathered_ref[b, pieces * rows :, :].astype(f32)
+                if b != f:
+                    side = pltpu.roll(side, (b - f) * rows % LANES, 1)
+                field = jnp.where(lane == b, side, field)
+            fields.append(field[:, :total])
+        ids, highs, lows = fields
         line = lax.broadcasted_iota(i32, (pad, 1), 0)
         core, chip, side_plane = line // (2 * n_x), line // 2 % n_x, line % 2
         name = ((chip * n_pair + pair_ref[0]) * 2 + side_plane) * n_c + core
@@ -98,10 +116,10 @@
         high = jnp.zeros((pad, total), f32)
         low = jnp.zeros((pad, total), f32)
         for k in range(top):
-            same = side[k : k + 1, :] == name
+            same = ids[k : k + 1, :] == name
             named = named + jnp.where(same, 1.0, 0.0)
-            high = high + jnp.where(same, side[top + k : top + k + 1, :], 0.0)
-            low = low + jnp.where(same, side[2 * top + k : 2 * top + k + 1, :], 0.0)
+            high = high + jnp.where(same, highs[k : k + 1, :], 0.0)
+            low = low + jnp.where(same, lows[k : k + 1, :], 0.0)
         rank = jnp.dot(named.astype(bf16), ahead_ref[...], preferred_element_type=f32)
         rank = jnp.where(named > 0.5, rank, -1.0)
         wanted = wanted_ref[...]
@@ -111,13 +129,13 @@
             pick_ref[at, :] = jnp.where(hit, 1.0, 0.0).astype(bf16)
             high_ref[at, :] = jnp.where(hit, high[j : j + 1, :], 0.0).astype(bf16)
             low_ref[at, :] = jnp.where(hit, low[j : j + 1, :], 0.0).astype(bf16)
-        sent = jnp.dot(pick_ref[...], gathered_ref[:, :part], preferred_element_type=f32).astype(bf16)
+        sent = jnp.dot(pick_ref[...], own_ref[...], preferred_element_type=f32).astype(bf16)
         for d in range(n_dp):
             out_ref[d] = sent
 
     slots = experts * held
     outs = (((n_dp, slots, part), bf16),) + (((slots, total), bf16),) * 2
-    scratch = [pltpu.VMEM((slots, total), bf16)]
+    scratch = [pltpu.VMEM((slots, total), bf16), pltpu.VMEM((total, part), bf16)]
     return call(body, outs, [SMEM] + [VMEM] * 3, scratch)(pair, gathered, ahead, wanted)
 
 
@@ -157,7 +175,7 @@
     )
 
 
-def mix_rows(received, high, low, share):
+def mix_rows(received, high, low, share, n_dp):
     _, part = received.shape
     total = high.shape[1]
 
@@ -167,7 +185,8 @@
         mixed = lax.dot_general(high_ref[...], rows, dims, preferred_element_type=f32)
         mixed = mixed + lax.dot_general(low_ref[...], rows, dims, preferred_element_type=f32)
         for i in range(total // share):
-            out_ref[i] = mixed[i * share : (i + 1) * share, :].astype(bf16)
+            block, owner = i // n_dp, i % n_dp
+            out_ref[owner * (total // share // n_dp) + block] = mixed[i * share : (i + 1) * share, :].astype(bf16)
 
     return call(body, [((total // share, share, part), bf16)], [VMEM] * 3)(received, high, low)
 
@@ -177,9 +196,10 @@
 
     def body(shares_ref, out_ref):
         for d in range(n_dp):
-            total = shares_ref[d].astype(f32)
+            first = d * (peers // n_dp)
+            total = shares_ref[first].astype(f32)
             for z in range(1, peers // n_dp):
-                total = total + shares_ref[z * n_dp + d].astype(f32)
+                total = total + shares_ref[first + z].astype(f32)
             out_ref[:, d * part : (d + 1) * part] = total.astype(bf16)
 
     return call(body, [((share, n_dp * part), bf16)], [VMEM])(shares)
@@ -203,7 +223,7 @@
     w_gate, w_up = expert_gate[0], expert_up[0]
 
     packed = pack_rows(tokens, expert_ids, route_logits, member_ref, n_dp, n_pair)
-    gathered = exchange(packed, "zh").reshape(n_pair * rows, -1)
+    gathered = exchange(packed, "zh")
 
     downs = []
     for s in range(n_dp):
@@ -215,15 +235,17 @@
         downs.append(piece)
 
     ahead, wanted = route_masks(pair_ref, n_pair * rows, rows, held)
-    outgoing, high, low = route_rows(gathered, pair_ref, ahead, wanted, top, n_x, n_pair, n_c, n_dp)
+    outgoing, high, low = route_rows(
+        gathered, pair_ref, ahead, wanted, rows, top, n_x, n_pair, n_c, n_dp
+    )
     arrived = exchange(outgoing.reshape(n_dp * experts, held, part), ("y", "c", "x", "zl"))
     hidden = hidden_rows(arrived.reshape(n_dp, slots, part), w_gate, w_up)
     hidden, downs = lax.optimization_barrier((hidden, downs))
     hidden = exchange(hidden, "y")
     results = output_rows(hidden, downs, member_ref)
     back = exchange(results.reshape(experts, held, part), ("c", "x", "zl"))
-    mixed = mix_rows(back.reshape(slots, part), high, low, rows // n_dp)
-    shares = exchange(mixed, ("zh", "y"))
+    mixed = mix_rows(back.reshape(slots, part), high, low, rows // n_dp, n_dp)
+    shares = exchange(mixed, ("y", "zh"))
     return sum_rows(shares, n_dp)
 
 

time: 177 us -> 176 us (level)
  no operation moved by 1% of the time
where the time goes in v10:
time: 176 us; the launch traced here: 174 us
  waiting for transfers between devices  63.3 us (36%)
  blocking collectives  59.7 us (34%)
  starting transfers between devices  34.7 us (20%)
  Pallas kernels  10.1 us (6%)
  local copies, waits for them, and re-layouts  6.09 us (3%)
    all_to_all x3, blocking collectives, exchange(): return lax.all_to_all(value, axes, split_axis=0, concat_axis=0, tiled=True)  59.7 us
    all_to_all x2, waiting for transfers between devices, exchange(): return lax.all_to_all(value, axes, split_axis=0, concat_axis=0, tiled=True)  50.6 us
    all_to_all x2, starting transfers between devices, exchange(): return lax.all_to_all(value, axes, split_axis=0, concat_axis=0, tiled=True)  23.2 us
    ppermute x3, waiting for transfers between devices, on_device(): piece = lax.ppermute(piece, 'y', [(i, (i + s) % n_dp) for i in range(n_dp)])  12.7 us
    ppermute x3, starting transfers between devices, on_device(): piece = lax.ppermute(piece, 'y', [(i, (i + s) % n_dp) for i in range(n_dp)])  11.4 us
    pallas_call x1, Pallas kernels, hidden_rows(): call(body, [((n_dp, slots, units), bf16)], [VMEM] * 3)  4.38 us
  transfers between devices with their start and end apart: 5, of which 4 were waited for; matrix products, arithmetic and copies ran while one was open for 2% of the time, Pallas kernels for 3%

profile of v10, /device:TPU:6, one launch (start us, length us, event | category | flops | bytes accessed | tf_op | source)
XLA Modules:
  0.0 174.0 jit_solution(5773814521780412392)
XLA Ops:
  0.0 1.6 shard_map.64
  1.6 15.1 %all-to-all-start = ((bf16[8,120,128]{2,1,0:T(8,128)(2,1)}), bf16[8,120,128]{2,1,0:T(8,128)(2,1)S(1)}, u32[]{:S(2)}, u32[]{:S(2)}) async-start(bf16[8,120,128]{2,1,0:T(8,128)(2,1)} %shard_map.64), calls=%async_computation | async-start | bytes 491520 | tf_op jit(solution)/shard_map/all_to_all | solution.py:209
  16.7 20.7 %all-to-all-done.gathered_ref = bf16[8,120,128]{2,1,0:T(8,128)(2,1)S(1)} async-done(((bf16[8,120,128]{2,1,0:T(8,128)(2,1)}), bf16[8,120,128]{2,1,0:T(8,128)(2,1)S(1)}, u32[]{:S(2)}, u32[]{:S(2)}) %all-to-all-start) | async-done | bytes 245792 | tf_op jit(solution)/shard_map/all_to_all | solution.py:209
  37.4 0.7 shard_map.66
  38.1 0.0 copy-start
  38.1 1.8 %copy-done = bf16[4,512,896]{2,1,0:T(8,128)(2,1)} copy-done((bf16[4,512,896]{2,1,0:T(8,128)(2,1)}, bf16[4,512,896]{2,1,0:T(8,128)(2,1)S(1)}, u32[]{:S(2)}) %copy-start) | copy-done | bytes 3670040
  39.9 8.1 %all-to-all-start.1 = ((bf16[64,32,896]{2,1,0:T(8,128)(2,1)}), bf16[64,32,896]{2,1,0:T(8,128)(2,1)}, u32[]{:S(2)}, u32[]{:S(2)}) async-start(bf16[64,32,896]{2,1,0:T(8,128)(2,1)} %bitcast.18), calls=%async_computation.1 | async-start | bytes 7340032 | tf_op jit(solution)/shard_map/all_to_all | solution.py:209
  48.1 0.0 copy-start.1
  48.1 2.8 %dynamic-slice_bitcast_fusion = (bf16[256,896]{1,0:T(8,128)(2,1)}, bf16[256,896]{1,0:T(8,128)(2,1)}, bf16[256,896]{1,0:T(8,128)(2,1)S(1)}, bf16[256,896]{1,0:T(8,128)(2,1)}) fusion(bf16[1,256,3584]{2,1,0:T(8,128)(2,1)} %param.11, s32[]{:T(128)S(6)} %select_n.32, s32[]{:T(128)S(6)} %select_n.28, s32[]{:T(128)S(6)} %select_n.26, s32[]{:T(128)S(6)} %select_n.30), kind=kLoop, calls=%fused_computation | loop fusion | bytes 3670032 | tf_op jit(solution)/shard_map/dynamic_slice | solution.py:232
  50.9 3.4 %collective-permute-start = (bf16[256,896]{1,0:T(8,128)(2,1)}, bf16[256,896]{1,0:T(8,128)(2,1)S(1)}, u32[]{:S(2)}, u32[]{:S(2)}) collective-permute-start(bf16[256,896]{1,0:T(8,128)(2,1)} %get-tuple-element.26), channel_id=1, source_target_pairs={{0,1},{1,2},{2,3},{3,0},{4,5},{5,6},{6,7},{7,4},{8,9},{9,10},{10,1... | collective-permute-start | bytes 1376264 | tf_op jit(solution)/shard_map/ppermute | solution.py:234
  54.3 4.8 %collective-permute-start.1 = (bf16[256,896]{1,0:T(8,128)(2,1)}, bf16[256,896]{1,0:T(8,128)(2,1)S(1)}, u32[]{:S(2)}, u32[]{:S(2)}) collective-permute-start(bf16[256,896]{1,0:T(8,128)(2,1)} %get-tuple-element.28), channel_id=1, source_target_pairs={{0,2},{1,3},{2,0},{3,1},{4,6},{5,7},{6,4},{7,5},{8,10},{9,11},{10,... | collective-permute-start | bytes 1376264 | tf_op jit(solution)/shard_map/ppermute | solution.py:234
  59.1 3.3 %collective-permute-start.2 = (bf16[256,896]{1,0:T(8,128)(2,1)}, bf16[256,896]{1,0:T(8,128)(2,1)}, u32[]{:S(2)}, u32[]{:S(2)}) collective-permute-start(bf16[256,896]{1,0:T(8,128)(2,1)} %get-tuple-element.25), channel_id=1, source_target_pairs={{0,3},{1,0},{2,1},{3,2},{4,7},{5,4},{6,5},{7,6},{8,11},{9,8},{10,9... | collective-permute-start | bytes 1376264 | tf_op jit(solution)/shard_map/ppermute | solution.py:234
  62.4 29.9 %all-to-all-done.1 = bf16[64,32,896]{2,1,0:T(8,128)(2,1)} async-done(((bf16[64,32,896]{2,1,0:T(8,128)(2,1)}), bf16[64,32,896]{2,1,0:T(8,128)(2,1)}, u32[]{:S(2)}, u32[]{:S(2)}) %all-to-all-start.1) | async-done | bytes 3670048 | tf_op jit(solution)/shard_map/all_to_all | solution.py:209
  92.3 0.0 copy-done.1
  92.3 0.0 copy-start.2
  92.3 1.5 copy-done.2
  93.8 4.4 %shard_map.67 = bf16[4,512,256]{2,1,0:T(8,128)(2,1)S(1)} custom-call(bf16[4,512,896]{2,1,0:T(8,128)(2,1)} %bitcast.5.rows_ref, bf16[3584,256]{1,0:T(8,128)(2,1)S(1)} %bitcast.21, bf16[3584,256]{1,0:T(8,128)(2,1)S(1)} %bitcast.22), custom_call_target="tpu_custom_call" | custom-call | tf_op jit(solution)/shard_map/pallas_call | solution.py:158
  98.2 3.0 %collective-permute-done.refs_1_ = bf16[256,896]{1,0:T(8,128)(2,1)S(1)} collective-permute-done((bf16[256,896]{1,0:T(8,128)(2,1)}, bf16[256,896]{1,0:T(8,128)(2,1)S(1)}, u32[]{:S(2)}, u32[]{:S(2)}) %collective-permute-start) | collective-permute-done | bytes 458784 | tf_op jit(solution)/shard_map/ppermute | solution.py:234
  101.2 9.7 %collective-permute-done.1.refs_2_ = bf16[256,896]{1,0:T(8,128)(2,1)S(1)} collective-permute-done((bf16[256,896]{1,0:T(8,128)(2,1)}, bf16[256,896]{1,0:T(8,128)(2,1)S(1)}, u32[]{:S(2)}, u32[]{:S(2)}) %collective-permute-start.1) | collective-permute-done | bytes 458784 | tf_op jit(solution)/shard_map/ppermute | solution.py:234
  110.9 0.0 collective-permute-done.2.refs_3_
  110.9 18.1 %all_to_all.25.hidden_ref = bf16[4,512,256]{2,1,0:T(8,128)(2,1)S(1)} all-to-all(bf16[4,512,256]{2,1,0:T(8,128)(2,1)S(1)} %shard_map.67), channel_id=1, replica_groups=mesh['x'=4,'zh'=8,'zl'=2,'c'=2,'y'=4] {'y'}, dimensions={0} | all-to-all | bytes 2097152 | tf_op jit(solution)/shard_map/all_to_all | solution.py:209
  129.0 2.3 %shard_map.68 = bf16[512,896]{1,0:T(8,128)(2,1)S(1)} custom-call(s32[1]{0:T(128)} %bitcast.member_ref, bf16[4,512,256]{2,1,0:T(8,128)(2,1)S(1)} %all_to_all.25.hidden_ref, bf16[256,896]{1,0:T(8,128)(2,1)S(1)} %get-tuple-element.19.refs_0_, bf16[256,896]{1,0:T(8,128)(2,1)S(1)} %collective-permute-done.refs_1_, ...), custom_call_target="tpu_custom_call" | custom-call | tf_op jit(solution)/shard_map/pallas_call | solution.py:173
  131.3 18.2 %all_to_all.26 = bf16[16,32,896]{2,1,0:T(8,128)(2,1)S(1)} all-to-all(bf16[16,32,896]{2,1,0:T(8,128)(2,1)S(1)} %bitcast.20), channel_id=1, replica_groups=mesh['x'=4,'zh'=8,'zl'=2,'c'=2,'y'=4] {'c','x','zl'}, dimensions={0} | all-to-all | bytes 1835008 | tf_op jit(solution)/shard_map/all_to_all | solution.py:209
  149.5 0.5 shard_map.69
  150.0 23.3 %all_to_all.27.shares_ref = bf16[32,4,896]{2,1,0:T(4,128)(2,1)S(1)} all-to-all(bf16[32,4,896]{2,1,0:T(4,128)(2,1)S(1)} %shard_map.69), channel_id=1, replica_groups=mesh['x'=4,'zh'=8,'zl'=2,'c'=2,'y'=4] {'y','zh'}, dimensions={0} | all-to-all | bytes 458752 | tf_op jit(solution)/shard_map/all_to_all | solution.py:209
  173.3 0.7 shard_map.70
  (1 shorter events, 0.0 us)
Async XLA Ops:
  1.6 35.8 %all-to-all-start = ((bf16[8,120,128]{2,1,0:T(8,128)(2,1)}), bf16[8,120,128]{2,1,0:T(8,128)(2,1)S(1)}, u32[]{:S(2)}, u32[]{:S(2)}) async-start(bf16[8,120,128]{2,1,0:T(8,128)(2,1)} %shard_map.64), calls=%async_computation | async-start | bytes 491520 | tf_op jit(solution)/shard_map/all_to_all | solution.py:209
  38.1 1.8 %copy-start = (bf16[4,512,896]{2,1,0:T(8,128)(2,1)}, bf16[4,512,896]{2,1,0:T(8,128)(2,1)S(1)}, u32[]{:S(2)}) copy-start(bf16[4,512,896]{2,1,0:T(8,128)(2,1)S(1)} %get-tuple-element.17) | copy-start | bytes 11010052
  39.9 52.3 %all-to-all-start.1 = ((bf16[64,32,896]{2,1,0:T(8,128)(2,1)}), bf16[64,32,896]{2,1,0:T(8,128)(2,1)}, u32[]{:S(2)}, u32[]{:S(2)}) async-start(bf16[64,32,896]{2,1,0:T(8,128)(2,1)} %bitcast.18), calls=%async_computation.1 | async-start | bytes 7340032 | tf_op jit(solution)/shard_map/all_to_all | solution.py:209
  48.1 44.2 %copy-start.1 = (bf16[1,3584,256]{2,1,0:T(8,128)(2,1)S(1)}, bf16[1,3584,256]{2,1,0:T(8,128)(2,1)}, u32[]{:S(2)}) copy-start(bf16[1,3584,256]{2,1,0:T(8,128)(2,1)} %param.9) | copy-start | bytes 5505028
  50.9 50.3 %collective-permute-start = (bf16[256,896]{1,0:T(8,128)(2,1)}, bf16[256,896]{1,0:T(8,128)(2,1)S(1)}, u32[]{:S(2)}, u32[]{:S(2)}) collective-permute-start(bf16[256,896]{1,0:T(8,128)(2,1)} %get-tuple-element.26), channel_id=1, source_target_pairs={{0,1},{1,2},{2,3},{3,0},{4,5},{5,6},{6,7},{7,4},{8,9},{9,10},{10,1... | collective-permute-start | bytes 1376264 | tf_op jit(solution)/shard_map/ppermute | solution.py:234
  54.3 56.6 %collective-permute-start.1 = (bf16[256,896]{1,0:T(8,128)(2,1)}, bf16[256,896]{1,0:T(8,128)(2,1)S(1)}, u32[]{:S(2)}, u32[]{:S(2)}) collective-permute-start(bf16[256,896]{1,0:T(8,128)(2,1)} %get-tuple-element.28), channel_id=1, source_target_pairs={{0,2},{1,3},{2,0},{3,1},{4,6},{5,7},{6,4},{7,5},{8,10},{9,11},{10,... | collective-permute-start | bytes 1376264 | tf_op jit(solution)/shard_map/ppermute | solution.py:234
  59.1 51.8 %collective-permute-start.2 = (bf16[256,896]{1,0:T(8,128)(2,1)}, bf16[256,896]{1,0:T(8,128)(2,1)}, u32[]{:S(2)}, u32[]{:S(2)}) collective-permute-start(bf16[256,896]{1,0:T(8,128)(2,1)} %get-tuple-element.25), channel_id=1, source_target_pairs={{0,3},{1,0},{2,1},{3,2},{4,7},{5,4},{6,5},{7,6},{8,11},{9,8},{10,9... | collective-permute-start | bytes 1376264 | tf_op jit(solution)/shard_map/ppermute | solution.py:234
  92.3 1.5 copy-start.2

commit v11 on v10

--- a/solution.py
+++ b/solution.py
@@ -158,21 +158,19 @@
     return call(body, [((n_dp, slots, units), bf16)], [VMEM] * 3)(received, w_gate, w_up)
 
 
-def output_rows(hidden, downs, member):
+def output_rows(hidden, down, downs, member):
     n_dp, slots, _ = hidden.shape
     part = downs[0].shape[1]
 
-    def body(member_ref, hidden_ref, *refs):
-        out_ref = refs[-1]
-        total = jnp.zeros((slots, part), f32)
-        for s in range(n_dp):
+    def body(member_ref, hidden_ref, down_ref, *refs):
+        start = pl.multiple_of(member_ref[0] * part, 128)
+        total = jnp.dot(hidden_ref[member_ref[0]], down_ref[:, pl.ds(start, part)], preferred_element_type=f32)
+        for s in range(1, n_dp):
             source = lax.rem(member_ref[0] + (n_dp - s), n_dp)
-            total = total + jnp.dot(hidden_ref[source], refs[s][...], preferred_element_type=f32)
-        out_ref[...] = total.astype(bf16)
-
-    return call(body, [((slots, part), bf16)], [SMEM, VMEM] + [VMEM] * n_dp)(
-        member, hidden, *downs
-    )
+            total = total + jnp.dot(hidden_ref[source], refs[s - 1][...], preferred_element_type=f32)
+        refs[-1][...] = total.astype(bf16)
+
+    return call(body, [((slots, part), bf16)], [SMEM] + [VMEM] * (n_dp + 1))(member, hidden, down, *downs)
 
 
 def mix_rows(received, high, low, share, n_dp):
@@ -226,12 +224,11 @@
     gathered = exchange(packed, "zh")
 
     downs = []
-    for s in range(n_dp):
+    for s in range(1, n_dp):
         owner = member + s
         owner = jnp.where(owner >= n_dp, owner - n_dp, owner)
         piece = lax.dynamic_slice_in_dim(expert_down[0], owner * part, part, axis=1)
-        if s:
-            piece = lax.ppermute(piece, "y", [(i, (i + s) % n_dp) for i in range(n_dp)])
+        piece = lax.ppermute(piece, "y", [(i, (i + s) % n_dp) for i in range(n_dp)])
         downs.append(piece)
 
     ahead, wanted = route_masks(pair_ref, n_pair * rows, rows, held)
@@ -242,7 +239,7 @@
     hidden = hidden_rows(arrived.reshape(n_dp, slots, part), w_gate, w_up)
     hidden, downs = lax.optimization_barrier((hidden, downs))
     hidden = exchange(hidden, "y")
-    results = output_rows(hidden, downs, member_ref)
+    results = output_rows(hidden, expert_down[0], downs, member_ref)
     back = exchange(results.reshape(experts, held, part), ("c", "x", "zl"))
     mixed = mix_rows(back.reshape(slots, part), high, low, rows // n_dp, n_dp)
     shares = exchange(mixed, ("y", "zh"))

time: 176 us -> 175 us (level)
    unnamed x6 -> x8, local copies, waits for them, and re-layouts: 3.34 us -> 4.83 us
  transfers between devices with their start and end apart: 5 -> 5, of which waited for: 4 -> 4; matrix products, arithmetic and copies ran while one was open for 2% -> 1% of each run, Pallas kernels for 3% -> 3%
where the time goes in v11:
time: 175 us; the launch traced here: 173 us
  waiting for transfers between devices  63.4 us (36%)
  blocking collectives  59.7 us (34%)
  starting transfers between devices  34.8 us (20%)
  Pallas kernels  9.06 us (5%)
  local copies, waits for them, and re-layouts  6.03 us (3%)
    all_to_all x3, blocking collectives, exchange(): return lax.all_to_all(value, axes, split_axis=0, concat_axis=0, tiled=True)  59.7 us
    all_to_all x2, waiting for transfers between devices, exchange(): return lax.all_to_all(value, axes, split_axis=0, concat_axis=0, tiled=True)  52.2 us
    all_to_all x2, starting transfers between devices, exchange(): return lax.all_to_all(value, axes, split_axis=0, concat_axis=0, tiled=True)  23.4 us
    ppermute x3, starting transfers between devices, on_device(): piece = lax.ppermute(piece, 'y', [(i, (i + s) % n_dp) for i in range(n_dp)])  11.4 us
    ppermute x3, waiting for transfers between devices, on_device(): piece = lax.ppermute(piece, 'y', [(i, (i + s) % n_dp) for i in range(n_dp)])  11.2 us
    unnamed x8, local copies, waits for them, and re-layouts  4.83 us
    pallas_call x1, Pallas kernels, hidden_rows(): call(body, [((n_dp, slots, units), bf16)], [VMEM] * 3)  4.38 us
  transfers between devices with their start and end apart: 5, of which 4 were waited for; matrix products, arithmetic and copies ran while one was open for 1% of the time, Pallas kernels for 3%

profile of v11, /device:TPU:6, one launch (start us, length us, event | category | flops | bytes accessed | tf_op | source)
XLA Modules:
  0.0 173.1 jit_solution(12608879691315590151)
XLA Ops:
  0.0 1.6 shard_map.64
  1.6 15.1 %all-to-all-start = ((bf16[8,120,128]{2,1,0:T(8,128)(2,1)}), bf16[8,120,128]{2,1,0:T(8,128)(2,1)S(1)}, u32[]{:S(2)}, u32[]{:S(2)}) async-start(bf16[8,120,128]{2,1,0:T(8,128)(2,1)} %shard_map.64), calls=%async_computation | async-start | bytes 491520 | tf_op jit(solution)/shard_map/all_to_all | solution.py:207
  16.7 20.7 %all-to-all-done.gathered_ref = bf16[8,120,128]{2,1,0:T(8,128)(2,1)S(1)} async-done(((bf16[8,120,128]{2,1,0:T(8,128)(2,1)}), bf16[8,120,128]{2,1,0:T(8,128)(2,1)S(1)}, u32[]{:S(2)}, u32[]{:S(2)}) %all-to-all-start) | async-done | bytes 245792 | tf_op jit(solution)/shard_map/all_to_all | solution.py:207
  37.4 0.7 shard_map.66
  38.1 0.0 copy-start.1
  38.1 1.8 %copy-done.1 = bf16[4,512,896]{2,1,0:T(8,128)(2,1)} copy-done((bf16[4,512,896]{2,1,0:T(8,128)(2,1)}, bf16[4,512,896]{2,1,0:T(8,128)(2,1)S(1)}, u32[]{:S(2)}) %copy-start.1) | copy-done | bytes 3670040
  39.9 0.0 copy-start
  39.9 8.3 %all-to-all-start.1 = ((bf16[64,32,896]{2,1,0:T(8,128)(2,1)}), bf16[64,32,896]{2,1,0:T(8,128)(2,1)}, u32[]{:S(2)}, u32[]{:S(2)}) async-start(bf16[64,32,896]{2,1,0:T(8,128)(2,1)} %bitcast.18), calls=%async_computation.1 | async-start | bytes 7340032 | tf_op jit(solution)/shard_map/all_to_all | solution.py:207
  48.2 0.0 copy-done
  48.2 1.2 dynamic-slice_bitcast_fusion
  49.4 3.4 %collective-permute-start = (bf16[256,896]{1,0:T(8,128)(2,1)}, bf16[256,896]{1,0:T(8,128)(2,1)S(1)}, u32[]{:S(2)}, u32[]{:S(2)}) collective-permute-start(bf16[256,896]{1,0:T(8,128)(2,1)} %get-tuple-element.25), channel_id=1, source_target_pairs={{0,1},{1,2},{2,3},{3,0},{4,5},{5,6},{6,7},{7,4},{8,9},{9,10},{10,1... | collective-permute-start | bytes 1376264 | tf_op jit(solution)/shard_map/ppermute | solution.py:231
  52.8 4.8 %collective-permute-start.1 = (bf16[256,896]{1,0:T(8,128)(2,1)}, bf16[256,896]{1,0:T(8,128)(2,1)S(1)}, u32[]{:S(2)}, u32[]{:S(2)}) collective-permute-start(bf16[256,896]{1,0:T(8,128)(2,1)} %get-tuple-element.24), channel_id=1, source_target_pairs={{0,2},{1,3},{2,0},{3,1},{4,6},{5,7},{6,4},{7,5},{8,10},{9,11},{10,... | collective-permute-start | bytes 1376264 | tf_op jit(solution)/shard_map/ppermute | solution.py:231
  57.6 3.3 %collective-permute-start.2 = (bf16[256,896]{1,0:T(8,128)(2,1)}, bf16[256,896]{1,0:T(8,128)(2,1)S(1)}, u32[]{:S(2)}, u32[]{:S(2)}) collective-permute-start(bf16[256,896]{1,0:T(8,128)(2,1)} %get-tuple-element.23), channel_id=1, source_target_pairs={{0,3},{1,0},{2,1},{3,2},{4,7},{5,4},{6,5},{7,6},{8,11},{9,8},{10,9... | collective-permute-start | bytes 1376264 | tf_op jit(solution)/shard_map/ppermute | solution.py:231
  60.9 31.5 %all-to-all-done.1 = bf16[64,32,896]{2,1,0:T(8,128)(2,1)} async-done(((bf16[64,32,896]{2,1,0:T(8,128)(2,1)}), bf16[64,32,896]{2,1,0:T(8,128)(2,1)}, u32[]{:S(2)}, u32[]{:S(2)}) %all-to-all-start.1) | async-done | bytes 3670048 | tf_op jit(solution)/shard_map/all_to_all | solution.py:207
  92.4 0.0 copy-start.2
  92.4 1.5 copy-done.2
  93.9 0.0 copy-start.3
  93.9 1.5 copy-done.3
  95.4 4.4 %shard_map.67 = bf16[4,512,256]{2,1,0:T(8,128)(2,1)S(1)} custom-call(bf16[4,512,896]{2,1,0:T(8,128)(2,1)} %bitcast.5.rows_ref, bf16[3584,256]{1,0:T(8,128)(2,1)S(1)} %bitcast.21, bf16[3584,256]{1,0:T(8,128)(2,1)S(1)} %bitcast.22), custom_call_target="tpu_custom_call" | custom-call | tf_op jit(solution)/shard_map/pallas_call | solution.py:158
  99.8 1.5 collective-permute-done.refs_0_
  101.3 9.7 %collective-permute-done.1.refs_1_ = bf16[256,896]{1,0:T(8,128)(2,1)S(1)} collective-permute-done((bf16[256,896]{1,0:T(8,128)(2,1)}, bf16[256,896]{1,0:T(8,128)(2,1)S(1)}, u32[]{:S(2)}, u32[]{:S(2)}) %collective-permute-start.1) | collective-permute-done | bytes 458784 | tf_op jit(solution)/shard_map/ppermute | solution.py:231
  111.0 0.0 collective-permute-done.2.refs_2_
  111.0 18.0 %all_to_all.25.hidden_ref = bf16[4,512,256]{2,1,0:T(8,128)(2,1)S(1)} all-to-all(bf16[4,512,256]{2,1,0:T(8,128)(2,1)S(1)} %shard_map.67), channel_id=1, replica_groups=mesh['x'=4,'zh'=8,'zl'=2,'c'=2,'y'=4] {'y'}, dimensions={0} | all-to-all | bytes 2097152 | tf_op jit(solution)/shard_map/all_to_all | solution.py:207
  129.0 1.2 shard_map.68
  130.3 18.3 %all_to_all.26 = bf16[16,32,896]{2,1,0:T(8,128)(2,1)S(1)} all-to-all(bf16[16,32,896]{2,1,0:T(8,128)(2,1)S(1)} %bitcast.20), channel_id=1, replica_groups=mesh['x'=4,'zh'=8,'zl'=2,'c'=2,'y'=4] {'c','x','zl'}, dimensions={0} | all-to-all | bytes 1835008 | tf_op jit(solution)/shard_map/all_to_all | solution.py:207
  148.6 0.5 shard_map.69
  149.1 23.3 %all_to_all.27.shares_ref = bf16[32,4,896]{2,1,0:T(4,128)(2,1)S(1)} all-to-all(bf16[32,4,896]{2,1,0:T(4,128)(2,1)S(1)} %shard_map.69), channel_id=1, replica_groups=mesh['x'=4,'zh'=8,'zl'=2,'c'=2,'y'=4] {'y','zh'}, dimensions={0} | all-to-all | bytes 458752 | tf_op jit(solution)/shard_map/all_to_all | solution.py:207
  172.4 0.7 shard_map.70
  (1 shorter events, 0.0 us)
Async XLA Ops:
  1.6 35.8 %all-to-all-start = ((bf16[8,120,128]{2,1,0:T(8,128)(2,1)}), bf16[8,120,128]{2,1,0:T(8,128)(2,1)S(1)}, u32[]{:S(2)}, u32[]{:S(2)}) async-start(bf16[8,120,128]{2,1,0:T(8,128)(2,1)} %shard_map.64), calls=%async_computation | async-start | bytes 491520 | tf_op jit(solution)/shard_map/all_to_all | solution.py:207
  38.1 1.8 %copy-start.1 = (bf16[4,512,896]{2,1,0:T(8,128)(2,1)}, bf16[4,512,896]{2,1,0:T(8,128)(2,1)S(1)}, u32[]{:S(2)}) copy-start(bf16[4,512,896]{2,1,0:T(8,128)(2,1)S(1)} %get-tuple-element.16) | copy-start | bytes 11010052
  39.9 8.3 %copy-start = (bf16[1,256,3584]{2,1,0:T(8,128)(2,1)S(1)}, bf16[1,256,3584]{2,1,0:T(8,128)(2,1)}, u32[]{:S(2)}) copy-start(bf16[1,256,3584]{2,1,0:T(8,128)(2,1)} %param.11) | copy-start | bytes 5505028
  39.9 52.5 %all-to-all-start.1 = ((bf16[64,32,896]{2,1,0:T(8,128)(2,1)}), bf16[64,32,896]{2,1,0:T(8,128)(2,1)}, u32[]{:S(2)}, u32[]{:S(2)}) async-start(bf16[64,32,896]{2,1,0:T(8,128)(2,1)} %bitcast.18), calls=%async_computation.1 | async-start | bytes 7340032 | tf_op jit(solution)/shard_map/all_to_all | solution.py:207
  49.4 51.9 %collective-permute-start = (bf16[256,896]{1,0:T(8,128)(2,1)}, bf16[256,896]{1,0:T(8,128)(2,1)S(1)}, u32[]{:S(2)}, u32[]{:S(2)}) collective-permute-start(bf16[256,896]{1,0:T(8,128)(2,1)} %get-tuple-element.25), channel_id=1, source_target_pairs={{0,1},{1,2},{2,3},{3,0},{4,5},{5,6},{6,7},{7,4},{8,9},{9,10},{10,1... | collective-permute-start | bytes 1376264 | tf_op jit(solution)/shard_map/ppermute | solution.py:231
  52.8 58.2 %collective-permute-start.1 = (bf16[256,896]{1,0:T(8,128)(2,1)}, bf16[256,896]{1,0:T(8,128)(2,1)S(1)}, u32[]{:S(2)}, u32[]{:S(2)}) collective-permute-start(bf16[256,896]{1,0:T(8,128)(2,1)} %get-tuple-element.24), channel_id=1, source_target_pairs={{0,2},{1,3},{2,0},{3,1},{4,6},{5,7},{6,4},{7,5},{8,10},{9,11},{10,... | collective-permute-start | bytes 1376264 | tf_op jit(solution)/shard_map/ppermute | solution.py:231
  57.6 53.3 %collective-permute-start.2 = (bf16[256,896]{1,0:T(8,128)(2,1)}, bf16[256,896]{1,0:T(8,128)(2,1)S(1)}, u32[]{:S(2)}, u32[]{:S(2)}) collective-permute-start(bf16[256,896]{1,0:T(8,128)(2,1)} %get-tuple-element.23), channel_id=1, source_target_pairs={{0,3},{1,0},{2,1},{3,2},{4,7},{5,4},{6,5},{7,6},{8,11},{9,8},{10,9... | collective-permute-start | bytes 1376264 | tf_op jit(solution)/shard_map/ppermute | solution.py:231
  92.4 1.5 copy-start.2
  93.9 1.5 copy-start.3

commit v12 on v11

--- a/solution.py
+++ b/solution.py
@@ -30,20 +30,27 @@
     )
 
 
-def pack_rows(tokens, expert_ids, route_logits, member, n_dp, peers):
+def pack_rows(tokens, expert_ids, route_logits, down, member, n_dp, peers):
     rows, width = tokens.shape
     top = expert_ids.shape[1]
     part = width // n_dp
     pieces = part // LANES
 
-    def body(member_ref, tokens_hbm, ids_hbm, logits_hbm, out_ref, own_ref, ids_ref, logits_ref, sems):
+    def body(member_ref, tokens_hbm, ids_hbm, logits_hbm, down_hbm, out_ref, *refs):
+        pieces_out, (own_ref, ids_ref, logits_ref, sems) = refs[: n_dp - 1], refs[n_dp - 1 :]
         start = pl.multiple_of(member_ref[0] * part, 128)
         copies = [
             pltpu.make_async_copy(tokens_hbm.at[:, pl.ds(start, part)], own_ref, sems.at[0]),
             pltpu.make_async_copy(ids_hbm, ids_ref, sems.at[1]),
             pltpu.make_async_copy(logits_hbm, logits_ref, sems.at[2]),
         ]
-        for copy in copies:
+        cuts = []
+        for s in range(1, n_dp):
+            begin = pl.multiple_of(lax.rem(member_ref[0] + s, n_dp) * part, 128)
+            cuts.append(
+                pltpu.make_async_copy(down_hbm.at[:, pl.ds(begin, part)], pieces_out[s - 1], sems.at[2 + s])
+            )
+        for copy in copies + cuts:
             copy.start()
         for copy in copies:
             copy.wait()
@@ -61,15 +68,19 @@
             for i in range(pieces):
                 out_ref[z, i * rows : (i + 1) * rows, :] = own[:, i * LANES : (i + 1) * LANES]
             out_ref[z, pieces * rows :, :] = side
-
-    outs = [((peers, pieces * rows + SIDE, LANES), bf16)]
+        for copy in cuts:
+            copy.wait()
+
+    outs = (((peers, pieces * rows + SIDE, LANES), bf16),) + (((down.shape[0], part), bf16),) * (n_dp - 1)
     scratch = [
         pltpu.VMEM((rows, part), bf16),
         pltpu.VMEM((top, rows), i32),
         pltpu.VMEM((top, rows), f32),
-        pltpu.SemaphoreType.DMA((3,)),
+        pltpu.SemaphoreType.DMA((2 + n_dp,)),
     ]
-    return call(body, outs, [SMEM, HBM, HBM, HBM], scratch, None)(member, tokens, expert_ids.T, route_logits.T)
+    return call(body, outs, [SMEM, HBM, HBM, HBM, HBM], scratch, None)(
+        member, tokens, expert_ids.T, route_logits.T, down
+    )
 
 
 def route_masks(pair, total, rows, held):
@@ -220,15 +231,14 @@
     pair_ref = lax.axis_index("zh").astype(i32).reshape(1)
     w_gate, w_up = expert_gate[0], expert_up[0]
 
-    packed = pack_rows(tokens, expert_ids, route_logits, member_ref, n_dp, n_pair)
+    packed, *cuts = pack_rows(
+        tokens, expert_ids, route_logits, expert_down[0], member_ref, n_dp, n_pair
+    )
     gathered = exchange(packed, "zh")
 
     downs = []
     for s in range(1, n_dp):
-        owner = member + s
-        owner = jnp.where(owner >= n_dp, owner - n_dp, owner)
-        piece = lax.dynamic_slice_in_dim(expert_down[0], owner * part, part, axis=1)
-        piece = lax.ppermute(piece, "y", [(i, (i + s) % n_dp) for i in range(n_dp)])
+        piece = lax.ppermute(cuts[s - 1], "y", [(i, (i + s) % n_dp) for i in range(n_dp)])
         downs.append(piece)
 
     ahead, wanted = route_masks(pair_ref, n_pair * rows, rows, held)

time: 175 us -> 176 us (level)
  waiting for transfers between devices: 63.4 us -> 66.1 us
  local copies, waits for them, and re-layouts: 6.03 us -> 3.34 us
  transfers between devices with their start and end apart: 5 -> 5, of which waited for: 4 -> 4; matrix products, arithmetic and copies ran while one was open for 1% -> 0% of each run, Pallas kernels for 3% -> 3%
where the time goes in v12:
time: 176 us; the launch traced here: 174 us
  waiting for transfers between devices  66.1 us (38%)
  blocking collectives  59.7 us (34%)
  starting transfers between devices  34.8 us (20%)
  Pallas kernels  10.2 us (6%)
  local copies, waits for them, and re-layouts  3.34 us (2%)
    all_to_all x3, blocking collectives, exchange(): return lax.all_to_all(value, axes, split_axis=0, concat_axis=0, tiled=True)  59.7 us
    all_to_all x2, waiting for transfers between devices, exchange(): return lax.all_to_all(value, axes, split_axis=0, concat_axis=0, tiled=True)  53.4 us
    all_to_all x2, starting transfers between devices, exchange(): return lax.all_to_all(value, axes, split_axis=0, concat_axis=0, tiled=True)  23.4 us
    ppermute x3, waiting for transfers between devices, on_device(): lax.ppermute(cuts[s - 1], 'y', [(i, (i + s) % n_dp) for i in range(n_dp)])  12.7 us
    ppermute x3, starting transfers between devices, on_device(): lax.ppermute(cuts[s - 1], 'y', [(i, (i + s) % n_dp) for i in range(n_dp)])  11.5 us
    pallas_call x1, Pallas kernels, hidden_rows(): call(body, [((n_dp, slots, units), bf16)], [VMEM] * 3)  4.38 us
  transfers between devices with their start and end apart: 5, of which 4 were waited for; matrix products, arithmetic and copies ran while one was open for 0% of the time, Pallas kernels for 3%

profile of v12, /device:TPU:6, one launch (start us, length us, event | category | flops | bytes accessed | tf_op | source)
XLA Modules:
  0.0 174.2 jit_solution(8532862998308761762)
XLA Ops:
  0.0 2.7 %shard_map.64 = (bf16[8,120,128]{2,1,0:T(8,128)(2,1)}, bf16[256,896]{1,0:T(8,128)(2,1)}, bf16[256,896]{1,0:T(8,128)(2,1)}, bf16[256,896]{1,0:T(8,128)(2,1)}) custom-call(s32[1]{0:T(128)} %bitcast.member_ref, bf16[16,3584]{1,0:T(8,128)(2,1)} %tokens_hbm.1, s32[8,16]{1,0:T(8,128)} %bitcast.18, f32[8,16]{1,0:T(8,128)} %bitcast.19, bf16[256,3584]{1,0:T(8,128)(2,1)} %bitcast.11), custom_call_target="tpu_custom_call" | custom-call | tf_op jit(solution)/shard_map/pallas_call | solution.py:81
  2.7 15.1 %all-to-all-start = ((bf16[8,120,128]{2,1,0:T(8,128)(2,1)}), bf16[8,120,128]{2,1,0:T(8,128)(2,1)S(1)}, u32[]{:S(2)}, u32[]{:S(2)}) async-start(bf16[8,120,128]{2,1,0:T(8,128)(2,1)} %get-tuple-element.18), calls=%async_computation | async-start | bytes 491520 | tf_op jit(solution)/shard_map/all_to_all | solution.py:218
  17.8 20.7 %all-to-all-done.gathered_ref = bf16[8,120,128]{2,1,0:T(8,128)(2,1)S(1)} async-done(((bf16[8,120,128]{2,1,0:T(8,128)(2,1)}), bf16[8,120,128]{2,1,0:T(8,128)(2,1)S(1)}, u32[]{:S(2)}, u32[]{:S(2)}) %all-to-all-start) | async-done | bytes 245792 | tf_op jit(solution)/shard_map/all_to_all | solution.py:218
  38.5 0.7 shard_map.66
  39.2 0.0 copy-start.1
  39.2 1.8 %copy-done.1 = bf16[4,512,896]{2,1,0:T(8,128)(2,1)} copy-done((bf16[4,512,896]{2,1,0:T(8,128)(2,1)}, bf16[4,512,896]{2,1,0:T(8,128)(2,1)S(1)}, u32[]{:S(2)}) %copy-start.1) | copy-done | bytes 3670040
  41.0 0.0 copy-start.2
  41.0 8.3 %all-to-all-start.1 = ((bf16[64,32,896]{2,1,0:T(8,128)(2,1)}), bf16[64,32,896]{2,1,0:T(8,128)(2,1)}, u32[]{:S(2)}, u32[]{:S(2)}) async-start(bf16[64,32,896]{2,1,0:T(8,128)(2,1)} %bitcast.13), calls=%async_computation.1 | async-start | bytes 7340032 | tf_op jit(solution)/shard_map/all_to_all | solution.py:218
  49.3 3.4 %collective-permute-start = (bf16[256,896]{1,0:T(8,128)(2,1)}, bf16[256,896]{1,0:T(8,128)(2,1)S(1)}, u32[]{:S(2)}, u32[]{:S(2)}) collective-permute-start(bf16[256,896]{1,0:T(8,128)(2,1)} %get-tuple-element.22), channel_id=1, source_target_pairs={{0,1},{1,2},{2,3},{3,0},{4,5},{5,6},{6,7},{7,4},{8,9},{9,10},{10,1... | collective-permute-start | bytes 1376264 | tf_op jit(solution)/shard_map/ppermute | solution.py:241
  52.7 4.8 %collective-permute-start.1 = (bf16[256,896]{1,0:T(8,128)(2,1)}, bf16[256,896]{1,0:T(8,128)(2,1)S(1)}, u32[]{:S(2)}, u32[]{:S(2)}) collective-permute-start(bf16[256,896]{1,0:T(8,128)(2,1)} %get-tuple-element.23), channel_id=1, source_target_pairs={{0,2},{1,3},{2,0},{3,1},{4,6},{5,7},{6,4},{7,5},{8,10},{9,11},{10,... | collective-permute-start | bytes 1376264 | tf_op jit(solution)/shard_map/ppermute | solution.py:241
  57.5 3.3 %collective-permute-start.2 = (bf16[256,896]{1,0:T(8,128)(2,1)}, bf16[256,896]{1,0:T(8,128)(2,1)S(1)}, u32[]{:S(2)}, u32[]{:S(2)}) collective-permute-start(bf16[256,896]{1,0:T(8,128)(2,1)} %get-tuple-element.24), channel_id=1, source_target_pairs={{0,3},{1,0},{2,1},{3,2},{4,7},{5,4},{6,5},{7,6},{8,11},{9,8},{10,9... | collective-permute-start | bytes 1376264 | tf_op jit(solution)/shard_map/ppermute | solution.py:241
  60.8 32.7 %all-to-all-done.1 = bf16[64,32,896]{2,1,0:T(8,128)(2,1)} async-done(((bf16[64,32,896]{2,1,0:T(8,128)(2,1)}), bf16[64,32,896]{2,1,0:T(8,128)(2,1)}, u32[]{:S(2)}, u32[]{:S(2)}) %all-to-all-start.1) | async-done | bytes 3670048 | tf_op jit(solution)/shard_map/all_to_all | solution.py:218
  93.5 0.0 copy-done.2
  93.5 0.0 copy-start.3
  93.5 1.5 copy-done.3
  95.0 4.4 %shard_map.67 = bf16[4,512,256]{2,1,0:T(8,128)(2,1)S(1)} custom-call(bf16[4,512,896]{2,1,0:T(8,128)(2,1)} %bitcast.6.rows_ref, bf16[3584,256]{1,0:T(8,128)(2,1)S(1)} %bitcast.16, bf16[3584,256]{1,0:T(8,128)(2,1)S(1)} %bitcast.17), custom_call_target="tpu_custom_call" | custom-call | tf_op jit(solution)/shard_map/pallas_call | solution.py:169
  99.4 0.0 copy-start
  99.4 3.0 %collective-permute-done.refs_0_ = bf16[256,896]{1,0:T(8,128)(2,1)S(1)} collective-permute-done((bf16[256,896]{1,0:T(8,128)(2,1)}, bf16[256,896]{1,0:T(8,128)(2,1)S(1)}, u32[]{:S(2)}, u32[]{:S(2)}) %collective-permute-start) | collective-permute-done | bytes 458784 | tf_op jit(solution)/shard_map/ppermute | solution.py:241
  102.4 9.7 %collective-permute-done.1.refs_1_ = bf16[256,896]{1,0:T(8,128)(2,1)S(1)} collective-permute-done((bf16[256,896]{1,0:T(8,128)(2,1)}, bf16[256,896]{1,0:T(8,128)(2,1)S(1)}, u32[]{:S(2)}, u32[]{:S(2)}) %collective-permute-start.1) | collective-permute-done | bytes 458784 | tf_op jit(solution)/shard_map/ppermute | solution.py:241
  112.1 0.0 collective-permute-done.2.refs_2_
  112.1 18.0 %all_to_all.25.hidden_ref = bf16[4,512,256]{2,1,0:T(8,128)(2,1)S(1)} all-to-all(bf16[4,512,256]{2,1,0:T(8,128)(2,1)S(1)} %shard_map.67), channel_id=1, replica_groups=mesh['x'=4,'zh'=8,'zl'=2,'c'=2,'y'=4] {'y'}, dimensions={0} | all-to-all | bytes 2097152 | tf_op jit(solution)/shard_map/all_to_all | solution.py:218
  130.1 0.0 copy-done
  130.1 1.2 shard_map.68
  131.4 18.3 %all_to_all.26 = bf16[16,32,896]{2,1,0:T(8,128)(2,1)S(1)} all-to-all(bf16[16,32,896]{2,1,0:T(8,128)(2,1)S(1)} %bitcast.15), channel_id=1, replica_groups=mesh['x'=4,'zh'=8,'zl'=2,'c'=2,'y'=4] {'c','x','zl'}, dimensions={0} | all-to-all | bytes 1835008 | tf_op jit(solution)/shard_map/all_to_all | solution.py:218
  149.7 0.5 shard_map.69
  150.2 23.3 %all_to_all.27.shares_ref = bf16[32,4,896]{2,1,0:T(4,128)(2,1)S(1)} all-to-all(bf16[32,4,896]{2,1,0:T(4,128)(2,1)S(1)} %shard_map.69), channel_id=1, replica_groups=mesh['x'=4,'zh'=8,'zl'=2,'c'=2,'y'=4] {'y','zh'}, dimensions={0} | all-to-all | bytes 458752 | tf_op jit(solution)/shard_map/all_to_all | solution.py:218
  173.5 0.7 shard_map.70
  (1 shorter events, 0.0 us)
Async XLA Ops:
  2.7 35.8 %all-to-all-start = ((bf16[8,120,128]{2,1,0:T(8,128)(2,1)}), bf16[8,120,128]{2,1,0:T(8,128)(2,1)S(1)}, u32[]{:S(2)}, u32[]{:S(2)}) async-start(bf16[8,120,128]{2,1,0:T(8,128)(2,1)} %get-tuple-element.18), calls=%async_computation | async-start | bytes 491520 | tf_op jit(solution)/shard_map/all_to_all | solution.py:218
  39.2 1.8 %copy-start.1 = (bf16[4,512,896]{2,1,0:T(8,128)(2,1)}, bf16[4,512,896]{2,1,0:T(8,128)(2,1)S(1)}, u32[]{:S(2)}) copy-start(bf16[4,512,896]{2,1,0:T(8,128)(2,1)S(1)} %get-tuple-element.21) | copy-start | bytes 11010052
  41.0 52.5 %copy-start.2 = (bf16[1,3584,256]{2,1,0:T(8,128)(2,1)S(1)}, bf16[1,3584,256]{2,1,0:T(8,128)(2,1)}, u32[]{:S(2)}) copy-start(bf16[1,3584,256]{2,1,0:T(8,128)(2,1)} %param.9) | copy-start | bytes 5505028
  41.0 52.5 %all-to-all-start.1 = ((bf16[64,32,896]{2,1,0:T(8,128)(2,1)}), bf16[64,32,896]{2,1,0:T(8,128)(2,1)}, u32[]{:S(2)}, u32[]{:S(2)}) async-start(bf16[64,32,896]{2,1,0:T(8,128)(2,1)} %bitcast.13), calls=%async_computation.1 | async-start | bytes 7340032 | tf_op jit(solution)/shard_map/all_to_all | solution.py:218
  49.3 53.1 %collective-permute-start = (bf16[256,896]{1,0:T(8,128)(2,1)}, bf16[256,896]{1,0:T(8,128)(2,1)S(1)}, u32[]{:S(2)}, u32[]{:S(2)}) collective-permute-start(bf16[256,896]{1,0:T(8,128)(2,1)} %get-tuple-element.22), channel_id=1, source_target_pairs={{0,1},{1,2},{2,3},{3,0},{4,5},{5,6},{6,7},{7,4},{8,9},{9,10},{10,1... | collective-permute-start | bytes 1376264 | tf_op jit(solution)/shard_map/ppermute | solution.py:241
  52.7 59.4 %collective-permute-start.1 = (bf16[256,896]{1,0:T(8,128)(2,1)}, bf16[256,896]{1,0:T(8,128)(2,1)S(1)}, u32[]{:S(2)}, u32[]{:S(2)}) collective-permute-start(bf16[256,896]{1,0:T(8,128)(2,1)} %get-tuple-element.23), channel_id=1, source_target_pairs={{0,2},{1,3},{2,0},{3,1},{4,6},{5,7},{6,4},{7,5},{8,10},{9,11},{10,... | collective-permute-start | bytes 1376264 | tf_op jit(solution)/shard_map/ppermute | solution.py:241
  57.5 54.6 %collective-permute-start.2 = (bf16[256,896]{1,0:T(8,128)(2,1)}, bf16[256,896]{1,0:T(8,128)(2,1)S(1)}, u32[]{:S(2)}, u32[]{:S(2)}) collective-permute-start(bf16[256,896]{1,0:T(8,128)(2,1)} %get-tuple-element.24), channel_id=1, source_target_pairs={{0,3},{1,0},{2,1},{3,2},{4,7},{5,4},{6,5},{7,6},{8,11},{9,8},{10,9... | collective-permute-start | bytes 1376264 | tf_op jit(solution)/shard_map/ppermute | solution.py:241
  93.5 1.5 copy-start.3
  99.4 30.7 %copy-start = (bf16[1,256,3584]{2,1,0:T(8,128)(2,1)S(1)}, bf16[1,256,3584]{2,1,0:T(8,128)(2,1)}, u32[]{:S(2)}) copy-start(bf16[1,256,3584]{2,1,0:T(8,128)(2,1)} %param.11) | copy-start | bytes 5505028

commit v13 on v10

--- a/solution.py
+++ b/solution.py
@@ -144,16 +144,19 @@
     units = w_gate.shape[1]
 
     def body(rows_ref, gate_ref, up_ref, out_ref):
-        v = jnp.zeros((slots, units), f32)
-        u = jnp.zeros((slots, units), f32)
-        for d in range(n_dp):
-            rows = rows_ref[d]
-            at = slice(d * part, (d + 1) * part)
-            v = v + jnp.dot(rows, gate_ref[at, :], preferred_element_type=f32)
-            u = u + jnp.dot(rows, up_ref[at, :], preferred_element_type=f32)
-        made = (v / (1.0 + jnp.exp(-v)) * u).astype(bf16)
-        for d in range(n_dp):
-            out_ref[d] = made
+        half = slots // 2
+        for h in range(2):
+            here = slice(h * half, (h + 1) * half)
+            v = jnp.zeros((half, units), f32)
+            u = jnp.zeros((half, units), f32)
+            for d in range(n_dp):
+                rows = rows_ref[d, here, :]
+                at = slice(d * part, (d + 1) * part)
+                v = v + jnp.dot(rows, gate_ref[at, :], preferred_element_type=f32)
+                u = u + jnp.dot(rows, up_ref[at, :], preferred_element_type=f32)
+            made = (v / (1.0 + jnp.exp(-v)) * u).astype(bf16)
+            for d in range(n_dp):
+                out_ref[d, here, :] = made
 
     return call(body, [((n_dp, slots, units), bf16)], [VMEM] * 3)(received, w_gate, w_up)
 

time: 176 us -> 176 us (level)
  no operation moved by 1% of the time
where the time goes in v13:
time: 176 us; the launch traced here: 174 us
  waiting for transfers between devices  63.3 us (36%)
  blocking collectives  59.7 us (34%)
  starting transfers between devices  34.7 us (20%)
  Pallas kernels  10.1 us (6%)
  local copies, waits for them, and re-layouts  6.09 us (3%)
    all_to_all x3, blocking collectives, exchange(): return lax.all_to_all(value, axes, split_axis=0, concat_axis=0, tiled=True)  59.7 us
    all_to_all x2, waiting for transfers between devices, exchange(): return lax.all_to_all(value, axes, split_axis=0, concat_axis=0, tiled=True)  50.6 us
    all_to_all x2, starting transfers between devices, exchange(): return lax.all_to_all(value, axes, split_axis=0, concat_axis=0, tiled=True)  23.2 us
    ppermute x3, waiting for transfers between devices, on_device(): piece = lax.ppermute(piece, 'y', [(i, (i + s) % n_dp) for i in range(n_dp)])  12.7 us
    ppermute x3, starting transfers between devices, on_device(): piece = lax.ppermute(piece, 'y', [(i, (i + s) % n_dp) for i in range(n_dp)])  11.4 us
    pallas_call x1, Pallas kernels, hidden_rows(): call(body, [((n_dp, slots, units), bf16)], [VMEM] * 3)  4.38 us
  transfers between devices with their start and end apart: 5, of which 4 were waited for; matrix products, arithmetic and copies ran while one was open for 2% of the time, Pallas kernels for 3%

profile of v13, /device:TPU:6, one launch (start us, length us, event | category | flops | bytes accessed | tf_op | source)
XLA Modules:
  0.0 174.0 jit_solution(6820314601890692374)
XLA Ops:
  0.0 1.6 shard_map.64
  1.6 15.1 %all-to-all-start = ((bf16[8,120,128]{2,1,0:T(8,128)(2,1)}), bf16[8,120,128]{2,1,0:T(8,128)(2,1)S(1)}, u32[]{:S(2)}, u32[]{:S(2)}) async-start(bf16[8,120,128]{2,1,0:T(8,128)(2,1)} %shard_map.64), calls=%async_computation | async-start | bytes 491520 | tf_op jit(solution)/shard_map/all_to_all | solution.py:212
  16.7 20.7 %all-to-all-done.gathered_ref = bf16[8,120,128]{2,1,0:T(8,128)(2,1)S(1)} async-done(((bf16[8,120,128]{2,1,0:T(8,128)(2,1)}), bf16[8,120,128]{2,1,0:T(8,128)(2,1)S(1)}, u32[]{:S(2)}, u32[]{:S(2)}) %all-to-all-start) | async-done | bytes 245792 | tf_op jit(solution)/shard_map/all_to_all | solution.py:212
  37.4 0.7 shard_map.66
  38.1 0.0 copy-start
  38.1 1.8 %copy-done = bf16[4,512,896]{2,1,0:T(8,128)(2,1)} copy-done((bf16[4,512,896]{2,1,0:T(8,128)(2,1)}, bf16[4,512,896]{2,1,0:T(8,128)(2,1)S(1)}, u32[]{:S(2)}) %copy-start) | copy-done | bytes 3670040
  39.9 8.1 %all-to-all-start.1 = ((bf16[64,32,896]{2,1,0:T(8,128)(2,1)}), bf16[64,32,896]{2,1,0:T(8,128)(2,1)}, u32[]{:S(2)}, u32[]{:S(2)}) async-start(bf16[64,32,896]{2,1,0:T(8,128)(2,1)} %bitcast.18), calls=%async_computation.1 | async-start | bytes 7340032 | tf_op jit(solution)/shard_map/all_to_all | solution.py:212
  48.1 0.0 copy-start.1
  48.1 2.8 %dynamic-slice_bitcast_fusion = (bf16[256,896]{1,0:T(8,128)(2,1)}, bf16[256,896]{1,0:T(8,128)(2,1)}, bf16[256,896]{1,0:T(8,128)(2,1)S(1)}, bf16[256,896]{1,0:T(8,128)(2,1)}) fusion(bf16[1,256,3584]{2,1,0:T(8,128)(2,1)} %param.11, s32[]{:T(128)S(6)} %select_n.32, s32[]{:T(128)S(6)} %select_n.28, s32[]{:T(128)S(6)} %select_n.26, s32[]{:T(128)S(6)} %select_n.30), kind=kLoop, calls=%fused_computation | loop fusion | bytes 3670032 | tf_op jit(solution)/shard_map/dynamic_slice | solution.py:235
  50.9 3.4 %collective-permute-start = (bf16[256,896]{1,0:T(8,128)(2,1)}, bf16[256,896]{1,0:T(8,128)(2,1)S(1)}, u32[]{:S(2)}, u32[]{:S(2)}) collective-permute-start(bf16[256,896]{1,0:T(8,128)(2,1)} %get-tuple-element.26), channel_id=1, source_target_pairs={{0,1},{1,2},{2,3},{3,0},{4,5},{5,6},{6,7},{7,4},{8,9},{9,10},{10,1... | collective-permute-start | bytes 1376264 | tf_op jit(solution)/shard_map/ppermute | solution.py:237
  54.3 4.8 %collective-permute-start.1 = (bf16[256,896]{1,0:T(8,128)(2,1)}, bf16[256,896]{1,0:T(8,128)(2,1)S(1)}, u32[]{:S(2)}, u32[]{:S(2)}) collective-permute-start(bf16[256,896]{1,0:T(8,128)(2,1)} %get-tuple-element.28), channel_id=1, source_target_pairs={{0,2},{1,3},{2,0},{3,1},{4,6},{5,7},{6,4},{7,5},{8,10},{9,11},{10,... | collective-permute-start | bytes 1376264 | tf_op jit(solution)/shard_map/ppermute | solution.py:237
  59.1 3.3 %collective-permute-start.2 = (bf16[256,896]{1,0:T(8,128)(2,1)}, bf16[256,896]{1,0:T(8,128)(2,1)}, u32[]{:S(2)}, u32[]{:S(2)}) collective-permute-start(bf16[256,896]{1,0:T(8,128)(2,1)} %get-tuple-element.25), channel_id=1, source_target_pairs={{0,3},{1,0},{2,1},{3,2},{4,7},{5,4},{6,5},{7,6},{8,11},{9,8},{10,9... | collective-permute-start | bytes 1376264 | tf_op jit(solution)/shard_map/ppermute | solution.py:237
  62.4 29.9 %all-to-all-done.1 = bf16[64,32,896]{2,1,0:T(8,128)(2,1)} async-done(((bf16[64,32,896]{2,1,0:T(8,128)(2,1)}), bf16[64,32,896]{2,1,0:T(8,128)(2,1)}, u32[]{:S(2)}, u32[]{:S(2)}) %all-to-all-start.1) | async-done | bytes 3670048 | tf_op jit(solution)/shard_map/all_to_all | solution.py:212
  92.3 0.0 copy-done.1
  92.3 0.0 copy-start.2
  92.3 1.5 copy-done.2
  93.8 4.4 %shard_map.67 = bf16[4,512,256]{2,1,0:T(8,128)(2,1)S(1)} custom-call(bf16[4,512,896]{2,1,0:T(8,128)(2,1)} %bitcast.5.rows_ref, bf16[3584,256]{1,0:T(8,128)(2,1)S(1)} %bitcast.21, bf16[3584,256]{1,0:T(8,128)(2,1)S(1)} %bitcast.22), custom_call_target="tpu_custom_call" | custom-call | tf_op jit(solution)/shard_map/pallas_call | solution.py:161
  98.2 3.0 %collective-permute-done.refs_1_ = bf16[256,896]{1,0:T(8,128)(2,1)S(1)} collective-permute-done((bf16[256,896]{1,0:T(8,128)(2,1)}, bf16[256,896]{1,0:T(8,128)(2,1)S(1)}, u32[]{:S(2)}, u32[]{:S(2)}) %collective-permute-start) | collective-permute-done | bytes 458784 | tf_op jit(solution)/shard_map/ppermute | solution.py:237
  101.2 9.7 %collective-permute-done.1.refs_2_ = bf16[256,896]{1,0:T(8,128)(2,1)S(1)} collective-permute-done((bf16[256,896]{1,0:T(8,128)(2,1)}, bf16[256,896]{1,0:T(8,128)(2,1)S(1)}, u32[]{:S(2)}, u32[]{:S(2)}) %collective-permute-start.1) | collective-permute-done | bytes 458784 | tf_op jit(solution)/shard_map/ppermute | solution.py:237
  110.9 0.0 collective-permute-done.2.refs_3_
  110.9 18.1 %all_to_all.25.hidden_ref = bf16[4,512,256]{2,1,0:T(8,128)(2,1)S(1)} all-to-all(bf16[4,512,256]{2,1,0:T(8,128)(2,1)S(1)} %shard_map.67), channel_id=1, replica_groups=mesh['x'=4,'zh'=8,'zl'=2,'c'=2,'y'=4] {'y'}, dimensions={0} | all-to-all | bytes 2097152 | tf_op jit(solution)/shard_map/all_to_all | solution.py:212
  129.0 2.3 %shard_map.68 = bf16[512,896]{1,0:T(8,128)(2,1)S(1)} custom-call(s32[1]{0:T(128)} %bitcast.member_ref, bf16[4,512,256]{2,1,0:T(8,128)(2,1)S(1)} %all_to_all.25.hidden_ref, bf16[256,896]{1,0:T(8,128)(2,1)S(1)} %get-tuple-element.19.refs_0_, bf16[256,896]{1,0:T(8,128)(2,1)S(1)} %collective-permute-done.refs_1_, ...), custom_call_target="tpu_custom_call" | custom-call | tf_op jit(solution)/shard_map/pallas_call | solution.py:176
  131.3 18.2 %all_to_all.26 = bf16[16,32,896]{2,1,0:T(8,128)(2,1)S(1)} all-to-all(bf16[16,32,896]{2,1,0:T(8,128)(2,1)S(1)} %bitcast.20), channel_id=1, replica_groups=mesh['x'=4,'zh'=8,'zl'=2,'c'=2,'y'=4] {'c','x','zl'}, dimensions={0} | all-to-all | bytes 1835008 | tf_op jit(solution)/shard_map/all_to_all | solution.py:212
  149.5 0.5 shard_map.69
  150.0 23.3 %all_to_all.27.shares_ref = bf16[32,4,896]{2,1,0:T(4,128)(2,1)S(1)} all-to-all(bf16[32,4,896]{2,1,0:T(4,128)(2,1)S(1)} %shard_map.69), channel_id=1, replica_groups=mesh['x'=4,'zh'=8,'zl'=2,'c'=2,'y'=4] {'y','zh'}, dimensions={0} | all-to-all | bytes 458752 | tf_op jit(solution)/shard_map/all_to_all | solution.py:212
  173.3 0.7 shard_map.70
  (1 shorter events, 0.0 us)
Async XLA Ops:
  1.6 35.8 %all-to-all-start = ((bf16[8,120,128]{2,1,0:T(8,128)(2,1)}), bf16[8,120,128]{2,1,0:T(8,128)(2,1)S(1)}, u32[]{:S(2)}, u32[]{:S(2)}) async-start(bf16[8,120,128]{2,1,0:T(8,128)(2,1)} %shard_map.64), calls=%async_computation | async-start | bytes 491520 | tf_op jit(solution)/shard_map/all_to_all | solution.py:212
  38.1 1.8 %copy-start = (bf16[4,512,896]{2,1,0:T(8,128)(2,1)}, bf16[4,512,896]{2,1,0:T(8,128)(2,1)S(1)}, u32[]{:S(2)}) copy-start(bf16[4,512,896]{2,1,0:T(8,128)(2,1)S(1)} %get-tuple-element.17) | copy-start | bytes 11010052
  39.9 52.3 %all-to-all-start.1 = ((bf16[64,32,896]{2,1,0:T(8,128)(2,1)}), bf16[64,32,896]{2,1,0:T(8,128)(2,1)}, u32[]{:S(2)}, u32[]{:S(2)}) async-start(bf16[64,32,896]{2,1,0:T(8,128)(2,1)} %bitcast.18), calls=%async_computation.1 | async-start | bytes 7340032 | tf_op jit(solution)/shard_map/all_to_all | solution.py:212
  48.1 44.2 %copy-start.1 = (bf16[1,3584,256]{2,1,0:T(8,128)(2,1)S(1)}, bf16[1,3584,256]{2,1,0:T(8,128)(2,1)}, u32[]{:S(2)}) copy-start(bf16[1,3584,256]{2,1,0:T(8,128)(2,1)} %param.9) | copy-start | bytes 5505028
  50.9 50.3 %collective-permute-start = (bf16[256,896]{1,0:T(8,128)(2,1)}, bf16[256,896]{1,0:T(8,128)(2,1)S(1)}, u32[]{:S(2)}, u32[]{:S(2)}) collective-permute-start(bf16[256,896]{1,0:T(8,128)(2,1)} %get-tuple-element.26), channel_id=1, source_target_pairs={{0,1},{1,2},{2,3},{3,0},{4,5},{5,6},{6,7},{7,4},{8,9},{9,10},{10,1... | collective-permute-start | bytes 1376264 | tf_op jit(solution)/shard_map/ppermute | solution.py:237
  54.3 56.6 %collective-permute-start.1 = (bf16[256,896]{1,0:T(8,128)(2,1)}, bf16[256,896]{1,0:T(8,128)(2,1)S(1)}, u32[]{:S(2)}, u32[]{:S(2)}) collective-permute-start(bf16[256,896]{1,0:T(8,128)(2,1)} %get-tuple-element.28), channel_id=1, source_target_pairs={{0,2},{1,3},{2,0},{3,1},{4,6},{5,7},{6,4},{7,5},{8,10},{9,11},{10,... | collective-permute-start | bytes 1376264 | tf_op jit(solution)/shard_map/ppermute | solution.py:237
  59.1 51.8 %collective-permute-start.2 = (bf16[256,896]{1,0:T(8,128)(2,1)}, bf16[256,896]{1,0:T(8,128)(2,1)}, u32[]{:S(2)}, u32[]{:S(2)}) collective-permute-start(bf16[256,896]{1,0:T(8,128)(2,1)} %get-tuple-element.25), channel_id=1, source_target_pairs={{0,3},{1,0},{2,1},{3,2},{4,7},{5,4},{6,5},{7,6},{8,11},{9,8},{10,9... | collective-permute-start | bytes 1376264 | tf_op jit(solution)/shard_map/ppermute | solution.py:237
  92.3 1.5 copy-start.2
